TPU v7x, 8 devices: a whole 2x2x1 slice. The times are simulated.
8 devices in a mesh: dp: 2 (over z, y), tp: 4 (over x, core).
Axes of the slice: x: 2, y: 2, z: 1, core: 2. Of those that a mesh axis runs over, the one named last changes fastest.
Arguments:
- hidden: bfloat16 [4096, 576], P('dp')
- w_final: float32 [576], replicated
- emb_table: bfloat16 [49152, 576], P('tp')
- teacher: bfloat16 [4096, 49152], P('dp', 'tp')
- tok_mask: float32 [4096], P('dp')
Outputs:
- output 1: float32 [], replicated
- output 2: bfloat16 [4096, 576], P('dp')
- output 3: float32 [576], replicated
- output 4: float32 [49152, 576], P('tp')
All inputs are finite; a program needn't handle non-finite values.
Results may differ from a plain program's by a relative error of at most 0.00105127.
Values sent between devices are 32-bit elements.
A program may use at most 1 GiB of HBM per device.

v0:
```python
import jax
import jax.numpy as jnp
from jax import lax
from jax.sharding import PartitionSpec as P

SOFT_CAP = 30.0
NORM_EPS = 1e-6


def final_norm(hid_rows, w_final):
    hid_f = hid_rows.astype(jnp.float32)
    inv_rms = lax.rsqrt(jnp.mean(hid_f * hid_f, axis=-1, keepdims=True) + NORM_EPS)
    normed = hid_f * inv_rms
    return inv_rms, normed, (normed * (1.0 + w_final)).astype(jnp.bfloat16)


def solution(mesh):
    def local_step(hid_rows, w_final, tab_rows, tea_rows, mask_rows):
        mask_sum = lax.psum(jnp.sum(mask_rows), 'dp')
        inv_rms, normed, x_rows = final_norm(hid_rows, w_final)
        logits = lax.dot_general(x_rows, tab_rows, (((1,), (1,)), ((), ())), preferred_element_type=jnp.float32)
        stu_cap = SOFT_CAP * jnp.tanh(logits / SOFT_CAP)
        tea_cap = SOFT_CAP * jnp.tanh(tea_rows.astype(jnp.float32) / SOFT_CAP)
        stu_exp = jnp.exp(stu_cap - SOFT_CAP)
        tea_exp = jnp.exp(tea_cap - SOFT_CAP)
        part_stats = jnp.stack([jnp.sum(stu_exp, axis=-1), jnp.sum(tea_exp, axis=-1), jnp.sum(tea_exp * (tea_cap - stu_cap), axis=-1)], axis=-1)
        tok_stats = lax.psum(part_stats, 'tp')
        stu_sum = tok_stats[:, 0:1]
        tea_sum = tok_stats[:, 1:2]
        kl_rows = tok_stats[:, 2] / tok_stats[:, 1] + jnp.log(tok_stats[:, 0]) - jnp.log(tok_stats[:, 1])
        loss_val = lax.psum(jnp.sum(mask_rows * kl_rows), 'dp') / mask_sum
        weight = (mask_rows / mask_sum)[:, None]
        cap_ratio = stu_cap / SOFT_CAP
        grad_z = ((stu_exp / stu_sum - tea_exp / tea_sum) * weight * (1.0 - cap_ratio * cap_ratio)).astype(jnp.bfloat16)
        grad_x = lax.psum(jnp.dot(grad_z, tab_rows, preferred_element_type=jnp.float32), 'tp')
        grad_table = lax.psum(lax.dot_general(grad_z, x_rows, (((0,), (0,)), ((), ())), preferred_element_type=jnp.float32), 'dp')
        grad_n = grad_x * (1.0 + w_final)
        grad_h = inv_rms * (grad_n - normed * jnp.mean(grad_n * normed, axis=-1, keepdims=True))
        grad_gain = lax.psum(jnp.sum(grad_x * normed, axis=0), 'dp')
        return loss_val, grad_h.astype(jnp.bfloat16), grad_gain, grad_table

    return jax.shard_map(local_step, mesh=mesh, in_specs=(P('dp', None), P(None), P('tp', None), P('dp', 'tp'), P('dp')), out_specs=(P(), P('dp', None), P(None), P('tp', None)), check_vma=False)
```

profile of v0, /device:TPU:0, one launch (start us, length us, event | category | flops | bytes accessed | tf_op | source)
XLA Modules:
  0.0 991.7 jit_solution(12877831492123751170)
XLA Ops:
  7.2 0.0 all-reduce.4.cloned.1.call-start
  7.2 0.7 broadcast_add_fusion
  7.9 2.2 fusion.12
  10.1 0.0 copy-start.1
  10.1 0.6 copy-done.1
  10.7 2.2 fusion.16.clone.4
  12.9 103.5 %fusion.1 = (f32[2048]{0:T(1024)S(1)}, f32[2048]{0:T(1024)S(1)}, f32[2048]{0:T(1024)S(1)}, f32[2048,12288]{1,0:T(8,128)}) fusion(bf16[2048,12288]{1,0:T(8,128)(2,1)} %param.8, bf16[12288,576]{0,1:T(8,128)(2,1)} %param.7, bf16[2048,576]{0,1:T(8,128)(2,1)S(1)} %fusion.16.clone.4), kind=kOutput, calls=%fused_computation.7 | convolution fusion | flops 29293012992 | bytes 167534592 | tf_op jit(solution)/shard_map/dot_general | solution.py:21
  116.4 13.2 %psum.42 = f32[2048,3]{0,1:T(4,128)S(1)} all-reduce(f32[2048,3]{0,1:T(4,128)S(1)} %pad_maximum_fusion), channel_id=1, replica_groups=mesh['dp'=2,'tp'=4] {'tp'}, use_global_device_ids=true, to_apply=%region_4.0 | all-reduce | flops 6144 | bytes 49152 | tf_op jit(solution)/shard_map/psum | solution.py:27
  129.7 0.6 fusion.17
  130.3 5.7 psum.44
  136.0 0.6 broadcast_divide_fusion
  136.7 78.4 %multiply_convert_fusion = bf16[2048,12288]{1,0:T(8,128)(2,1)} fusion(bf16[2048,12288]{1,0:T(8,128)(2,1)} %param.8, f32[2048,12288]{1,0:T(8,128)} %get-tuple-element.16, f32[2048]{0:T(1024)S(1)} %broadcast_divide_fusion, f32[2048]{0:T(1024)S(1)} %bitcast.15, f32[2048]{0:T(1024)S(1)} %bitcast.13), kind=kLoop, calls=%fused_computation | loop fusion | flops 377487360 | bytes 201351168 | tf_op jit(solution)/shard_map/convert_element_type | solution.py:34
  215.1 0.0 copy-start.4
  215.1 36.9 %fusion.19 = f32[2048,576]{0,1:T(8,128)} fusion(bf16[2048,12288]{1,0:T(8,128)(2,1)} %multiply_convert_fusion, bf16[12288,576]{0,1:T(8,128)(2,1)} %param.7), kind=kOutput, calls=%fused_computation.31 | convolution fusion | flops 28991029248 | bytes 69206016 | tf_op jit(solution)/shard_map/dot_general | solution.py:35
  252.0 0.0 all-reduce.4.cloned.1.call-update
  252.0 0.3 all-reduce.6.cloned.1.call-start
  252.3 38.0 %fusion.13 = f32[12288,576]{0,1:T(8,128)} fusion(bf16[2048,12288]{1,0:T(8,128)(2,1)} %multiply_convert_fusion, bf16[2048,576]{0,1:T(8,128)(2,1)S(1)} %copy-done, f32[576]{0:T(1024)S(1)} %copy-done.4, f32[2048]{0:T(1024)S(1)} %copy-done.2), kind=kOutput, calls=%fused_computation.21 | convolution fusion | flops 28995747840 | bytes 81012992 | tf_op jit(solution)/shard_map/dot_general | solution.py:36
  290.3 0.0 all-reduce.6.cloned.1.call-update
  290.3 50.3 %all-reduce.4.cloned.1.call-done = f32[2048,576]{0,1:T(8,128)} async-done(((f32[2048,576]{0,1:T(8,128)}), f32[2048,576]{0,1:T(8,128)}) %all-reduce.4.cloned.1.call-update) | async-done | bytes 4718608 | tf_op jit(solution)/shard_map/psum | solution.py:35
  340.6 3.5 fusion.11
  344.1 5.8 all-reduce
  351.2 4.9 fusion.10
  356.1 607.2 %all-reduce.6.cloned.1.call-done = f32[12288,576]{0,1:T(8,128)} async-done(((f32[12288,576]{0,1:T(8,128)}), f32[12288,576]{0,1:T(8,128)}) %all-reduce.6.cloned.1.call-update) | async-done | bytes 28311568 | tf_op jit(solution)/shard_map/psum | solution.py:36
  963.3 20.4 %copy.11 = f32[12288,576]{0,1:T(8,128)} copy(f32[12288,576]{0,1:T(8,128)} %all-reduce.6.cloned.1.call-done) | data formatting | bytes 56623104
  (13 shorter events, 0.1 us)
Async XLA Ops:
  7.2 333.4 %all-reduce.4.cloned.1.call-start = ((), (), s32[]{:S(2)}) async-start(), calls=%async_computation | async-start | bytes 9437184 | tf_op jit(solution)/shard_map/psum | solution.py:35
  7.9 2.2 copy-start.3
  10.1 0.6 copy-start.1
  12.9 116.7 %copy-start.5 = (f32[2048]{0:T(1024)S(1)}, f32[2048]{0:T(1024)}, u32[]{:S(2)}) copy-start(f32[2048]{0:T(1024)} %param.9) | copy-start | bytes 24580
  215.1 37.2 %copy-start = (bf16[2048,576]{0,1:T(8,128)(2,1)S(1)}, bf16[2048,576]{0,1:T(8,128)(2,1)}, u32[]{:S(2)}) copy-start(bf16[2048,576]{0,1:T(8,128)(2,1)} %param.5) | copy-start | bytes 7077892
  215.1 37.2 %copy-start.2 = (f32[2048]{0:T(1024)S(1)}, f32[2048]{0:T(1024)}, u32[]{:S(2)}) copy-start(f32[2048]{0:T(1024)} %copy-done.1) | copy-start | bytes 24580
  215.1 37.2 %copy-start.4 = (f32[576]{0:T(1024)S(1)}, f32[576]{0:T(1024)}, u32[]{:S(2)}) copy-start(f32[576]{0:T(1024)} %copy-done.3) | copy-start | bytes 6916
  252.0 711.3 %all-reduce.6.cloned.1.call-start = ((), (), s32[]{:S(2)}) async-start(), calls=%async_computation.1 | async-start | bytes 56623104 | tf_op jit(solution)/shard_map/psum | solution.py:36
Sparse Core Ops, SparseCore 0:
  252.1 88.4 all-reduce.3
  343.6 619.6 all-reduce.5
where the time goes:
time: 992 us
  waiting for transfers between devices  657 us (66%)
  matrix products  178 us (18%)
  other arithmetic  93.2 us (9%)
  blocking collectives  24.6 us (2%)
  local copies, waits for them, and re-layouts  21 us (2%)
  between operations  16.6 us (2%)
    psum x1, waiting for transfers between devices, local_step(): lax.psum(lax.dot_general(grad_z, x_rows, (((0,), (0,)), ((), ())), prefer...  607 us
    dot_general x1, matrix products, local_step(): lax.dot_general(x_rows, tab_rows, (((1,), (1,)), ((), ())), preferred_ele...  103 us
    convert_element_type x1, other arithmetic, local_step(): ((stu_exp / stu_sum - tea_exp / tea_sum) * weight * (1.0 - cap_ratio * ca...  78.4 us
    psum x1, waiting for transfers between devices, local_step(): lax.psum(jnp.dot(grad_z, tab_rows, preferred_element_type=jnp.float32), '...  50.3 us
    dot_general x1, matrix products, local_step(): lax.dot_general(grad_z, x_rows, (((0,), (0,)), ((), ())), preferred_eleme...  38 us
    dot_general x1, matrix products, local_step(): jnp.dot(grad_z, tab_rows, preferred_element_type=jnp.float32)  36.9 us
    unnamed x13, local copies, waits for them, and re-layouts  21 us
  transfers between devices with their start and end apart: 2, of which 2 were waited for; matrix products, arithmetic and copies ran while one was open for 5% of the time, Pallas kernels for 0%

commit v1 on v0

v1 whole, which is shorter than its diff:
```python
import functools
import math

import jax
import jax.numpy as jnp
from jax import lax
from jax.experimental import pallas as pl
from jax.experimental.pallas import tpu as pltpu
from jax.sharding import PartitionSpec as P

SOFT_CAP = 30.0
NORM_EPS = 1e-6
INV_CAP = 1.0 / SOFT_CAP
CAP_LOG2E = SOFT_CAP * math.log2(math.e)
MESH = pl.DeviceIdType.MESH
F32 = jnp.float32
BF16 = jnp.bfloat16
GROUP = 16
VMEM = pltpu.VMEM
NT_DIMS = (((1,), (1,)), ((), ()))


def full_spec(shape, single=True):
    zeros = (0,) * len(shape)
    if single:
        return pl.BlockSpec(shape, lambda j: zeros, pipeline_mode=pl.Buffered(1))
    return pl.BlockSpec(shape, lambda j: zeros)


STAT_TILE = 512
STAT_ROWS = 256


def stats_kernel(hid_ref, gain_ref, mask_ref, tab_ref, tea_ref, x_ref, xt_ref, stat_ref,
                 stu_acc, tea_acc, z_even, z_odd, count_vmem, count_smem, groups, live, sem):
    step = pl.program_id(0)
    dim, tokens = hid_ref.shape
    n_groups = tokens // GROUP
    per_block = STAT_ROWS // GROUP

    @pl.when(step == 0)
    def _():
        rows = lax.broadcasted_iota(jnp.int32, (128, 128), 0) // GROUP
        cols = lax.broadcasted_iota(jnp.int32, (128, 128), 1)
        pick = jnp.where(rows == cols, 1.0, 0.0).astype(BF16)
        counts = jnp.dot(mask_ref[...].astype(BF16), pick, preferred_element_type=F32)
        count_vmem[...] = counts.astype(jnp.int32)
        copy = pltpu.make_async_copy(count_vmem, count_smem, sem)
        copy.start()
        gain = jnp.broadcast_to(1.0 + gain_ref[...], (128, gain_ref.shape[1])).T[:dim, :]
        for blk in range(tokens // 128):
            hid = hid_ref[:, blk * 128:(blk + 1) * 128].astype(F32)
            inv_rms = lax.rsqrt(jnp.sum(hid * hid, axis=0, keepdims=True) * (1.0 / dim) + NORM_EPS)
            x_t = hid * inv_rms * gain
            xt_ref[:, blk * 128:(blk + 1) * 128] = x_t.astype(BF16)
            x_ref[blk * 128:(blk + 1) * 128, :] = x_t.T.astype(BF16)
        stu_acc[...] = jnp.zeros_like(stu_acc)
        tea_acc[...] = jnp.zeros_like(tea_acc)
        copy.wait()

        def add_group(g, n):
            groups[n] = g
            keep = count_smem[g // 8, g % 8] > 0
            return n + jnp.where(keep, 1, 0)

        n_live = lax.fori_loop(0, n_groups, add_group, 0)

        def pad(i, c):
            groups[n_live + i] = n_groups
            return c

        lax.fori_loop(0, 2 * per_block, pad, 0)
        live[0] = n_live

    n_pairs = (live[0] + 2 * per_block - 1) // (2 * per_block)

    def source(i):
        return pl.ds(pl.multiple_of(jnp.minimum(groups[i], n_groups - 1) * GROUP, GROUP), GROUP)

    def logits(first, z_ref):
        rows = jnp.concatenate([x_ref[source(first + i), :] for i in range(per_block)], axis=0)
        z_ref[...] = jnp.dot(rows, tab_ref[...], preferred_element_type=F32)

    def lane_sum(val):
        total = val[:, :128]
        for lane in range(128, STAT_TILE, 128):
            total = total + val[:, lane:lane + 128]
        return total

    def accumulate(first, z_ref):
        for i in range(per_block):
            dest = pl.ds(pl.multiple_of(groups[first + i] * GROUP, GROUP), GROUP)
            tea = jnp.tanh(tea_ref[source(first + i), :].astype(F32) * INV_CAP)
            tea_acc[dest, :] += lane_sum(jnp.exp2(tea * CAP_LOG2E))
            stu = jnp.tanh(z_ref[i * GROUP:(i + 1) * GROUP, :] * INV_CAP)
            stu_acc[dest, :] += lane_sum(jnp.exp2(stu * CAP_LOG2E))

    logits(0, z_even)

    def pair(p, c):
        first = p * 2 * per_block
        logits(first + per_block, z_odd)
        accumulate(first, z_even)
        logits(jnp.minimum(first + 2 * per_block, n_groups), z_even)
        accumulate(first + per_block, z_odd)
        return c

    lax.fori_loop(0, n_pairs, pair, 0)

    @pl.when(step == pl.num_programs(0) - 1)
    def _():
        for blk in range(tokens // 128):
            for k, acc in enumerate((stu_acc, tea_acc)):
                part = acc[blk * 128:(blk + 1) * 128, :].T
                stat_ref[k * 16 + blk:k * 16 + blk + 1, :] = jnp.sum(part, axis=0, keepdims=True)


def stats(hid_t, gain, mask, tab_t, tea):
    dim, tokens = hid_t.shape
    vocab = tab_t.shape[1]
    n_groups = tokens // GROUP
    extra = 2 * (STAT_ROWS // GROUP)
    return pl.pallas_call(
        stats_kernel,
        grid=(vocab // STAT_TILE,),
        in_specs=[
            full_spec(hid_t.shape), full_spec(gain.shape), full_spec(mask.shape),
            pl.BlockSpec((dim, STAT_TILE), lambda j: (0, j)),
            pl.BlockSpec((tokens, STAT_TILE), lambda j: (0, j)),
        ],
        out_specs=[full_spec((tokens, dim)), full_spec((dim, tokens)), full_spec((32, 128))],
        out_shape=[
            jax.ShapeDtypeStruct((tokens, dim), BF16),
            jax.ShapeDtypeStruct((dim, tokens), BF16),
            jax.ShapeDtypeStruct((32, 128), F32),
        ],
        scratch_shapes=[
            VMEM((tokens + GROUP, 128), F32), VMEM((tokens + GROUP, 128), F32),
            VMEM((STAT_ROWS, STAT_TILE), F32), VMEM((STAT_ROWS, STAT_TILE), F32),
            VMEM((16, 128), jnp.int32), pltpu.SMEM((16, 128), jnp.int32),
            pltpu.SMEM((n_groups + 2 * extra,), jnp.int32), pltpu.SMEM((1,), jnp.int32),
            pltpu.SemaphoreType.DMA,
        ],
        compiler_params=pltpu.CompilerParams(dimension_semantics=("arbitrary",), vmem_limit_bytes=40 * 2**20),
        cost_estimate=pl.CostEstimate(flops=50_000_000_000, bytes_accessed=70_000_000, transcendentals=0),
        name="stats",
    )(hid_t, gain, mask, tab_t, tea)


def gather_kernel(n_tp, stat_ref, mask_ref, stu_col, tea_col, base_ref, slots, mask_slot, send_sem, recv_sem):
    tp = lax.axis_index("tp")
    dp = lax.axis_index("dp")
    barrier = pltpu.get_barrier_semaphore()
    peers = [(dp, lax.rem(tp + k, n_tp)) for k in range(1, n_tp)] + [(1 - dp, tp)]
    for peer in peers:
        pl.semaphore_signal(barrier, inc=1, device_id=peer, device_id_type=MESH)
    pl.semaphore_wait(barrier, len(peers))
    copies = []
    for k, peer in enumerate(peers):
        last = k == n_tp - 1
        copies.append(pltpu.make_async_remote_copy(
            src_ref=mask_ref if last else stat_ref,
            dst_ref=mask_slot if last else slots.at[k],
            send_sem=send_sem.at[k], recv_sem=recv_sem.at[k], device_id=peer, device_id_type=MESH))
        copies[-1].start()
    for copy in copies:
        copy.wait()
    parts = [stat_ref[...]] + [slots[k] for k in range(n_tp - 1)]
    total = jnp.zeros_like(parts[0])
    for owner in range(n_tp):
        gap = lax.rem(tp - owner + n_tp, n_tp)
        part = parts[0]
        for k in range(1, n_tp):
            part = jnp.where(gap == k, parts[k], part)
        total = total + part
    total = jnp.where(total > 0.0, total, 1.0)
    mask = mask_ref[...]
    mask_sum = jnp.sum(mask) + jnp.sum(mask_slot[...])
    weight = mask / mask_sum
    stu_sum, tea_sum = total[:16, :], total[16:, :]
    base = jnp.sum(weight * (jnp.log(stu_sum) - jnp.log(tea_sum)))
    base_ref[...] = jnp.full((8, 128), base, F32)
    stu_row, tea_row = weight / stu_sum, weight / tea_sum
    for blk in range(16):
        rows = slice(blk * 128, (blk + 1) * 128)
        stu_col[rows, :] = jnp.broadcast_to(stu_row[blk:blk + 1, :], (128, 128)).T
        tea_col[rows, :] = jnp.broadcast_to(tea_row[blk:blk + 1, :], (128, 128)).T


def gather_stats(stat, mask, n_tp):
    tokens = mask.size
    whole = pl.BlockSpec(memory_space=VMEM)
    return pl.pallas_call(
        functools.partial(gather_kernel, n_tp),
        in_specs=[whole, whole],
        out_specs=[whole, whole, whole],
        out_shape=[
            jax.ShapeDtypeStruct((tokens, 128), F32),
            jax.ShapeDtypeStruct((tokens, 128), F32),
            jax.ShapeDtypeStruct((8, 128), F32),
        ],
        scratch_shapes=[
            VMEM((n_tp - 1,) + stat.shape, F32), VMEM(mask.shape, F32),
            pltpu.SemaphoreType.DMA((n_tp,)), pltpu.SemaphoreType.DMA((n_tp,)),
        ],
        compiler_params=pltpu.CompilerParams(collective_id=0, has_side_effects=True, vmem_limit_bytes=8 * 2**20),
        cost_estimate=pl.CostEstimate(flops=5_000_000, bytes_accessed=2_000_000, transcendentals=0),
        name="gather_stats",
    )(stat, mask)


GRAD_TILE = 256
GRAD_ROWS = 256


def chunk_kernel(first, x_ref, xt_ref, stu_col, tea_col, tab_ref, tea_ref, *refs):
    if first:
        de_ref, dx_out, kl_out, dx_acc, kl_acc, g_ref, sem = refs
    else:
        dx_in, kl_in, de_ref, dx_out, kl_out, dx_acc, kl_acc, g_ref, sem = refs
    step = pl.program_id(0)
    tokens = x_ref.shape[0]

    @pl.when(step == 0)
    def _():
        if first:
            dx_acc[...] = jnp.zeros_like(dx_acc)
            kl_acc[...] = jnp.zeros_like(kl_acc)
        else:
            loads = [pltpu.make_async_copy(dx_in, dx_acc, sem.at[0]), pltpu.make_async_copy(kl_in, kl_acc, sem.at[1])]
            for load in loads:
                load.start()
            for load in loads:
                load.wait()

    def block(b, c):
        rows = pl.ds(pl.multiple_of(b * GRAD_ROWS, GRAD_ROWS), GRAD_ROWS)
        z = jnp.dot(x_ref[rows, :], tab_ref[...], preferred_element_type=F32)
        stu_scale = stu_col[rows, :]
        tea_scale = tea_col[rows, :]
        kl = kl_acc[rows, :]
        parts = []
        for lane in range(0, GRAD_TILE, 128):
            stu = jnp.tanh(z[:, lane:lane + 128] * INV_CAP)
            tea = jnp.tanh(tea_ref[rows, lane:lane + 128].astype(F32) * INV_CAP)
            stu_p = jnp.exp2(stu * CAP_LOG2E) * stu_scale
            tea_p = jnp.exp2(tea * CAP_LOG2E) * tea_scale
            kl = kl + tea_p * (tea - stu)
            parts.append(((stu_p - tea_p) * (1.0 - stu * stu)).astype(BF16))
        kl_acc[rows, :] = kl
        g = jnp.concatenate(parts, axis=1)
        g_ref[rows, :] = g
        dx_acc[rows, :] += lax.dot_general(g, tab_ref[...], NT_DIMS, preferred_element_type=F32)
        return c

    lax.fori_loop(0, tokens // GRAD_ROWS, block, 0)
    de_ref[...] = jnp.dot(xt_ref[...], g_ref[...], preferred_element_type=F32)

    @pl.when(step == pl.num_programs(0) - 1)
    def _():
        saves = [pltpu.make_async_copy(dx_acc, dx_out, sem.at[0]), pltpu.make_async_copy(kl_acc, kl_out, sem.at[1])]
        for save in saves:
            save.start()
        for save in saves:
            save.wait()


def chunk_grad(start, size, x, x_t, stu_col, tea_col, tab_t, tea, carry):
    tokens, dim = x.shape
    off = start // GRAD_TILE
    hbm = pl.BlockSpec(memory_space=pl.ANY)
    first = carry is None
    work = tokens * size
    return pl.pallas_call(
        functools.partial(chunk_kernel, first),
        grid=(size // GRAD_TILE,),
        in_specs=[
            full_spec((tokens, dim)), full_spec((dim, tokens)), full_spec((tokens, 128)), full_spec((tokens, 128)),
            pl.BlockSpec((dim, GRAD_TILE), lambda j: (0, j + off)),
            pl.BlockSpec((tokens, GRAD_TILE), lambda j: (0, j + off)),
        ] + ([] if first else [hbm, hbm]),
        out_specs=[pl.BlockSpec((dim, GRAD_TILE), lambda j: (0, j)), hbm, hbm],
        out_shape=[
            jax.ShapeDtypeStruct((dim, size), F32),
            jax.ShapeDtypeStruct((tokens, dim), F32),
            jax.ShapeDtypeStruct((tokens, 128), F32),
        ],
        scratch_shapes=[
            VMEM((tokens, dim), F32), VMEM((tokens, 128), F32), VMEM((tokens, GRAD_TILE), BF16),
            pltpu.SemaphoreType.DMA((2,)),
        ],
        input_output_aliases={} if first else {6: 1, 7: 2},
        compiler_params=pltpu.CompilerParams(dimension_semantics=("arbitrary",), vmem_limit_bytes=40 * 2**20),
        cost_estimate=pl.CostEstimate(flops=work * 3 * 2 * dim, bytes_accessed=work * 2, transcendentals=0),
        name="chunk_grad",
    )(x, x_t, stu_col, tea_col, tab_t, tea, *(() if first else carry))


def dx_kernel(n_tp, dx_ref, kl_ref, base_ref, hid_ref, gain_ref, gh_ref, part_ref,
              dxt, slots, own, parts_buf, part_out, local_sem, send_sem, recv_sem):
    tp = lax.axis_index("tp")
    dp = lax.axis_index("dp")
    dim, tokens = hid_ref.shape
    width = tokens // n_tp
    load = pltpu.make_async_copy(dx_ref, dxt, local_sem.at[0])
    load.start()
    barrier = pltpu.get_barrier_semaphore()
    peers = [lax.rem(tp + k, n_tp) for k in range(1, n_tp)]
    for peer in peers:
        pl.semaphore_signal(barrier, inc=1, device_id=(dp, peer), device_id_type=MESH)
    pl.semaphore_wait(barrier, n_tp - 1)
    load.wait()

    def window(index):
        return pl.ds(pl.multiple_of(index * width, width), width)

    reduce = []
    for k, peer in enumerate(peers):
        reduce.append(pltpu.make_async_remote_copy(
            src_ref=dxt.at[window(peer), :], dst_ref=slots.at[k],
            send_sem=send_sem.at[0, k], recv_sem=recv_sem.at[0, k], device_id=(dp, peer), device_id_type=MESH))
        reduce[-1].start()
    for copy in reduce:
        copy.wait()
    mine = window(tp)
    total = jnp.zeros((width, dim), F32)
    for owner in range(n_tp):
        gap = lax.rem(tp - owner + n_tp, n_tp)
        part = dxt[mine, :]
        for k in range(1, n_tp):
            part = jnp.where(gap == k, slots[k - 1], part)
        total = total + part
    grad_x = total.T
    gain = jnp.broadcast_to(1.0 + gain_ref[...], (128, gain_ref.shape[1])).T[:dim, :1]
    hid = hid_ref[:, mine].astype(F32)
    inv_rms = lax.rsqrt(jnp.sum(hid * hid, axis=0, keepdims=True) * (1.0 / dim) + NORM_EPS)
    normed = hid * inv_rms
    grad_n = grad_x * gain
    corr = jnp.sum(grad_n * normed, axis=0, keepdims=True) * (1.0 / dim)
    own[...] = inv_rms * (grad_n - normed * corr)

    prod = grad_x * normed
    col = prod[:, :128]
    for lane in range(128, width, 128):
        col = col + prod[:, lane:lane + 128]
    row = jnp.sum(col.T, axis=0, keepdims=True)
    part_out[0:1, :dim] = row
    part_out[0:1, dim:] = jnp.zeros((1, part_out.shape[1] - dim), F32)
    loss = SOFT_CAP * jnp.sum(kl_ref[...]) + jnp.sum(base_ref[0:1, 0:1]) * (1.0 / n_tp)
    part_out[1:2, :] = jnp.full((1, part_out.shape[1]), loss, F32)
    part_out[2:8, :] = jnp.zeros((6, part_out.shape[1]), F32)

    spread = []
    for k, peer in enumerate(peers):
        spread.append(pltpu.make_async_remote_copy(
            src_ref=own, dst_ref=gh_ref.at[:, mine],
            send_sem=send_sem.at[1, k], recv_sem=recv_sem.at[1, k], device_id=(dp, peer), device_id_type=MESH))
        spread.append(pltpu.make_async_remote_copy(
            src_ref=part_out, dst_ref=parts_buf.at[tp],
            send_sem=send_sem.at[2, k], recv_sem=recv_sem.at[2, k], device_id=(dp, peer), device_id_type=MESH))
    for copy in spread:
        copy.start()
    gh_ref[:, mine] = own[...]
    parts_buf[tp] = part_out[...]
    for copy in spread:
        copy.wait()
    share = parts_buf[0]
    for k in range(1, n_tp):
        share = share + parts_buf[k]
    part_ref[...] = share


def reduce_dx(dx, kl, base, hid_t, gain, n_tp):
    tokens, dim = dx.shape
    width = tokens // n_tp
    whole = pl.BlockSpec(memory_space=VMEM)
    return pl.pallas_call(
        functools.partial(dx_kernel, n_tp),
        in_specs=[pl.BlockSpec(memory_space=pl.ANY), whole, whole, whole, whole],
        out_specs=[whole, whole],
        out_shape=[
            jax.ShapeDtypeStruct((dim, tokens), F32),
            jax.ShapeDtypeStruct((8, gain.shape[1]), F32),
        ],
        scratch_shapes=[
            VMEM((tokens, dim), F32), VMEM((n_tp - 1, width, dim), F32), VMEM((dim, width), F32),
            VMEM((n_tp, 8, gain.shape[1]), F32), VMEM((8, gain.shape[1]), F32),
            pltpu.SemaphoreType.DMA((1,)), pltpu.SemaphoreType.DMA((3, n_tp - 1)), pltpu.SemaphoreType.DMA((3, n_tp - 1)),
        ],
        compiler_params=pltpu.CompilerParams(collective_id=1, has_side_effects=True, vmem_limit_bytes=48 * 2**20),
        cost_estimate=pl.CostEstimate(flops=50_000_000_000, bytes_accessed=20_000_000, transcendentals=0),
        name="reduce_dx",
    )(dx, kl, base, hid_t, gain)


def add_kernel(*refs):
    a_ref, b_ref, out_ref = refs[-3], refs[-2], refs[-1]
    out_ref[...] = a_ref[...] + b_ref[...]


def add_chunk(start, size, vocab, own, other, out, after):
    dim = own.shape[0]
    tile = math.gcd(math.gcd(start, size), 512)
    off = start // tile
    hbm = pl.BlockSpec(memory_space=pl.ANY)
    block = pl.BlockSpec((dim, tile), lambda j: (0, j))
    lead = (after,) if out is None else (out,)
    return pl.pallas_call(
        add_kernel,
        grid=(size // tile,),
        in_specs=[hbm, block, block],
        out_specs=pl.BlockSpec((dim, tile), lambda j: (0, j + off)),
        out_shape=jax.ShapeDtypeStruct((dim, vocab), F32),
        input_output_aliases={} if out is None else {0: 0},
        compiler_params=pltpu.CompilerParams(dimension_semantics=("arbitrary",), vmem_limit_bytes=16 * 2**20),
        cost_estimate=pl.CostEstimate(flops=dim * size, bytes_accessed=12 * dim * size, transcendentals=0),
        name="add_chunk",
    )(*lead, own, other)


CHUNKS = (256, 512, 1024, 2048, 3072, 3072, 1536, 512, 256)


def solution(mesh):
    n_tp = mesh.shape["tp"]
    swap = [(0, 1), (1, 0)]

    def step(hid_rows, w_final, tab_rows, tea_rows, mask_rows):
        tokens, dim = hid_rows.shape
        vocab = tab_rows.shape[0]
        hid_t = hid_rows.T
        tab_t = tab_rows.T
        mask = mask_rows.reshape(tokens // 128, 128)
        gain = jnp.pad(w_final, (0, 640 - dim)).reshape(1, 640)
        x, x_t, stat = stats(hid_t, gain, mask, tab_t, tea_rows)
        stu_col, tea_col, base = gather_stats(stat, mask, n_tp)
        carry = None
        own, other = [], []
        start = 0
        for size in CHUNKS:
            part, dx, kl = chunk_grad(start, size, x, x_t, stu_col, tea_col, tab_t, tea_rows, carry)
            carry = (dx, kl)
            other.append(lax.ppermute(part, "dp", swap))
            own.append(part)
            start += size
        gh_t, share = reduce_dx(*carry, base, hid_t, gain, n_tp)
        share = share + lax.ppermute(share, "dp", swap)
        out = None
        start = 0
        for size, a, b in zip(CHUNKS, own, other):
            out = add_chunk(start, size, vocab, a, b, out, gh_t)
            start += size
        return share[1, 0], gh_t.T.astype(BF16), share[0, :dim], out.T

    return jax.shard_map(
        step, mesh=mesh,
        in_specs=(P("dp", None), P(None), P("tp", None), P("dp", "tp"), P("dp")),
        out_specs=(P(), P("dp", None), P(None), P("tp", None)), check_vma=False)
```

time: 992 us -> 790 us (0.80)
  Pallas kernels: 0 us -> 559 us
  waiting for transfers between devices: 657 us -> 194 us
  matrix products: 178 us -> 0 us
  other arithmetic: 93.2 us -> 4.11 us
  blocking collectives: 24.6 us -> 0 us
  between operations: 16.6 us -> 0.88 us
    psum x2 -> x0, waiting for transfers between devices: 657 us -> none  [the longest x1 607 us: local_step(): lax.psum(lax.dot_general(grad_z, x_rows, (((0,), (0,)), ((), ())), prefer...]
    pallas_call x0 -> x21, Pallas kernels: none -> 559 us  [the longest x9 332 us: chunk_grad(): pl.pallas_call(functools.partial(chunk_kernel, first), grid=(size // GRAD...]
    ppermute x0 -> x10, waiting for transfers between devices: none -> 194 us  [the longest x9 138 us: step(): other.append(lax.ppermute(part, 'dp', swap))]
    dot_general x3 -> x0, matrix products: 178 us -> none  [the longest x1 103 us: local_step(): lax.dot_general(x_rows, tab_rows, (((1,), (1,)), ((), ())), preferred_ele...]
    convert_element_type x2 -> x1, other arithmetic: 83.3 us -> 4.1 us  [step(): return (share[1, 0], gh_t.T.astype(BF16), share[0, :dim], out.T)]
    psum x3 -> x0, blocking collectives: 24.6 us -> none  [the longest x1 13.2 us: local_step(): tok_stats = lax.psum(part_stats, 'tp')]
    unnamed x13 -> x46, local copies, waits for them, and re-layouts: 21 us -> 19.2 us
  transfers between devices with their start and end apart: 2 -> 10, of which waited for: 2 -> 3; matrix products, arithmetic and copies ran while one was open for 5% -> 1% of each run, Pallas kernels for 0% -> 58%
where the time goes in v1:
time: 790 us; the launch traced here: 789 us
  Pallas kernels  559 us (71%)
  waiting for transfers between devices  194 us (25%)
  local copies, waits for them, and re-layouts  21 us (3%)
  starting transfers between devices  9.9 us (1%)
    pallas_call x9, Pallas kernels, chunk_grad(): pl.pallas_call(functools.partial(chunk_kernel, first), grid=(size // GRAD...  332 us
    ppermute x9, waiting for transfers between devices, step(): other.append(lax.ppermute(part, 'dp', swap))  138 us
    pallas_call x1, Pallas kernels, reduce_dx(): pl.pallas_call(functools.partial(dx_kernel, n_tp), in_specs=[pl.BlockSpec...  114 us
    pallas_call x1, Pallas kernels, stats(): pl.pallas_call(stats_kernel, grid=(vocab // STAT_TILE,), in_specs=[full_s...  66.1 us
    ppermute x1, waiting for transfers between devices, step(): share = share + lax.ppermute(share, 'dp', swap)  55.2 us
    pallas_call x9, Pallas kernels, add_chunk(): pl.pallas_call(add_kernel, grid=(size // tile,), in_specs=[hbm, block, bl...  39.8 us
    unnamed x46, local copies, waits for them, and re-layouts  19.2 us
  transfers between devices with their start and end apart: 10, of which 3 were waited for; matrix products, arithmetic and copies ran while one was open for 1% of the time, Pallas kernels for 58%

profile of v1, /device:TPU:0, one launch (start us, length us, event | category | flops | bytes accessed | tf_op | source)
XLA Modules:
  0.0 788.8 jit_solution(174360893101491812)
XLA Ops:
  3.7 66.1 %stats.1 = (bf16[2048,576]{1,0:T(8,128)(2,1)S(1)}, bf16[576,2048]{1,0:T(8,128)(2,1)S(1)}, f32[32,128]{1,0:T(8,128)S(1)}) custom-call(bf16[576,2048]{1,0:T(8,128)(2,1)S(1)} %bitcast.13, f32[1,640]{1,0:T(1,128)S(1)} %reshape.14.gain_ref, f32[16,128]{1,0:T(8,128)S(1)} %bitcast.11, bf16[576,12288]{1,0:T(8,128)(2,1)} %bitcast.16, bf16[2048,12288]{1,0:T(8,128)(2,1)} %tea_ref.19), custom_call_target="tpu_custom_call" | custom-call | flops 49999998976 | bytes 70000000 | tf_op jit(solution)/shard_map/stats/pallas_call | solution.py:123
  69.8 8.2 %gather_stats.1 = (f32[2048,128]{1,0:T(8,128)S(1)}, f32[2048,128]{1,0:T(8,128)S(1)}, f32[8,128]{1,0:T(8,128)S(1)}) custom-call(f32[32,128]{1,0:T(8,128)S(1)} %get-tuple-element.41.stat_ref, f32[16,128]{1,0:T(8,128)S(1)} %bitcast.12), custom_call_target="tpu_custom_call" | custom-call | flops 5000000 | bytes 2000000 | tf_op jit(solution)/shard_map/gather_stats/pallas_call | solution.py:193
  78.0 8.3 %chunk_grad.9 = (f32[576,256]{1,0:T(8,128)S(1)}, f32[2048,576]{1,0:T(8,128)S(1)}, f32[2048,128]{1,0:T(8,128)S(1)}) custom-call(bf16[2048,576]{1,0:T(8,128)(2,1)S(1)} %get-tuple-element.39.x_ref, bf16[576,2048]{1,0:T(8,128)(2,1)S(1)} %get-tuple-element.40.xt_ref, f32[2048,128]{1,0:T(8,128)S(1)} %get-tuple-element.42.stu_col, ...), custom_call_target="tpu_custom_call" | custom-call | flops 1811939328 | bytes 1048576 | tf_op jit(solution)/shard_map/chunk_grad/pallas_call | solution.py:274
  86.4 15.6 %chunk_grad.10 = (f32[576,512]{1,0:T(8,128)}, f32[2048,576]{1,0:T(8,128)S(1)}, f32[2048,128]{1,0:T(8,128)S(1)}) custom-call(bf16[2048,576]{1,0:T(8,128)(2,1)S(1)} %get-tuple-element.39.x_ref, bf16[576,2048]{1,0:T(8,128)(2,1)S(1)} %get-tuple-element.40.xt_ref, ...), custom_call_target="tpu_custom_call", output_to_operand_aliasing={{1}: (6, {}), {2}: (7, {})} | custom-call | flops 3623878656 | bytes 2097152 | tf_op jit(solution)/shard_map/chunk_grad/pallas_call | solution.py:274
  102.0 2.3 copy-done
  105.2 30.4 %chunk_grad.11 = (f32[576,1024]{1,0:T(8,128)S(1)}, f32[2048,576]{1,0:T(8,128)}, f32[2048,128]{1,0:T(8,128)S(1)}) custom-call(bf16[2048,576]{1,0:T(8,128)(2,1)S(1)} %get-tuple-element.39.x_ref, bf16[576,2048]{1,0:T(8,128)(2,1)S(1)} %get-tuple-element.40.xt_ref, ...), custom_call_target="tpu_custom_call", output_to_operand_aliasing={{1}: (6, {}), {2}: (7, {})} | custom-call | flops 7247757312 | bytes 4194304 | tf_op jit(solution)/shard_map/chunk_grad/pallas_call | solution.py:274
  135.7 56.8 %chunk_grad.12 = (f32[576,2048]{1,0:T(8,128)}, f32[2048,576]{1,0:T(8,128)}, f32[2048,128]{1,0:T(8,128)S(1)}) custom-call(bf16[2048,576]{1,0:T(8,128)(2,1)S(1)} %get-tuple-element.39.x_ref, bf16[576,2048]{1,0:T(8,128)(2,1)S(1)} %get-tuple-element.40.xt_ref, f32[2048,128]{1,0:T(8,128)S(1)} %get-tuple-element.42.stu_col, ...), custom_call_target="tpu_custom_call", output_to_operand_aliasing={{1}: (6, {}), {2}: (7, {})} | custom-call | flops 14495514624 | bytes 8388608 | tf_op jit(solution)/shard_map/chunk_grad/pallas_call | solution.py:274
  193.7 2.5 copy-done.1
  196.2 77.3 %chunk_grad.13 = (f32[576,3072]{1,0:T(8,128)}, f32[2048,576]{1,0:T(8,128)S(1)}, f32[2048,128]{1,0:T(8,128)S(1)}) custom-call(bf16[2048,576]{1,0:T(8,128)(2,1)S(1)} %get-tuple-element.39.x_ref, bf16[576,2048]{1,0:T(8,128)(2,1)S(1)} %get-tuple-element.40.xt_ref, ...), custom_call_target="tpu_custom_call", output_to_operand_aliasing={{1}: (6, {}), {2}: (7, {})} | custom-call | flops 21743271936 | bytes 12582912 | tf_op jit(solution)/shard_map/chunk_grad/pallas_call | solution.py:274
  274.3 77.3 %chunk_grad.14 = (f32[576,3072]{1,0:T(8,128)}, f32[2048,576]{1,0:T(8,128)S(1)}, f32[2048,128]{1,0:T(8,128)S(1)}) custom-call(bf16[2048,576]{1,0:T(8,128)(2,1)S(1)} %get-tuple-element.39.x_ref, bf16[576,2048]{1,0:T(8,128)(2,1)S(1)} %get-tuple-element.40.xt_ref, ...), custom_call_target="tpu_custom_call", output_to_operand_aliasing={{1}: (6, {}), {2}: (7, {})} | custom-call | flops 21743271936 | bytes 12582912 | tf_op jit(solution)/shard_map/chunk_grad/pallas_call | solution.py:274
  355.2 42.9 %chunk_grad.15 = (f32[576,1536]{1,0:T(8,128)S(1)}, f32[2048,576]{1,0:T(8,128)}, f32[2048,128]{1,0:T(8,128)S(1)}) custom-call(bf16[2048,576]{1,0:T(8,128)(2,1)S(1)} %get-tuple-element.39.x_ref, bf16[576,2048]{1,0:T(8,128)(2,1)S(1)} %get-tuple-element.40.xt_ref, ...), custom_call_target="tpu_custom_call", output_to_operand_aliasing={{1}: (6, {}), {2}: (7, {})} | custom-call | flops 10871635968 | bytes 6291456 | tf_op jit(solution)/shard_map/chunk_grad/pallas_call | solution.py:274
  398.1 2.5 copy-done.3
  400.6 14.6 %chunk_grad.16 = (f32[576,512]{1,0:T(8,128)S(1)}, f32[2048,576]{1,0:T(8,128)S(1)}, f32[2048,128]{1,0:T(8,128)S(1)}) custom-call(bf16[2048,576]{1,0:T(8,128)(2,1)S(1)} %get-tuple-element.39.x_ref, bf16[576,2048]{1,0:T(8,128)(2,1)S(1)} %get-tuple-element.40.xt_ref, ...), custom_call_target="tpu_custom_call", output_to_operand_aliasing={{1}: (6, {}), {2}: (7, {})} | custom-call | flops 3623878656 | bytes 2097152 | tf_op jit(solution)/shard_map/chunk_grad/pallas_call | solution.py:274
  415.3 8.3 %chunk_grad.17 = (f32[576,256]{1,0:T(8,128)S(1)}, f32[2048,576]{1,0:T(8,128)S(1)}, f32[2048,128]{1,0:T(8,128)S(1)}) custom-call(bf16[2048,576]{1,0:T(8,128)(2,1)S(1)} %get-tuple-element.39.x_ref, bf16[576,2048]{1,0:T(8,128)(2,1)S(1)} %get-tuple-element.40.xt_ref, ...), custom_call_target="tpu_custom_call", output_to_operand_aliasing={{1}: (6, {}), {2}: (7, {})} | custom-call | flops 1811939328 | bytes 1048576 | tf_op jit(solution)/shard_map/chunk_grad/pallas_call | solution.py:274
  430.7 113.6 %reduce_dx.1 = (f32[576,2048]{1,0:T(8,128)}, f32[8,640]{1,0:T(8,128)S(1)}) custom-call(f32[2048,576]{1,0:T(8,128)} %copy-done.4, f32[2048,128]{1,0:T(8,128)S(1)} %copy-done.6, f32[8,128]{1,0:T(8,128)S(1)} %get-tuple-element.62.base_ref, bf16[576,2048]{1,0:T(8,128)(2,1)S(1)} %bitcast.14, f32[1,640]{1,0:T(1,128)S(1)} %copy-done.16), custom_call_target="tpu_custom_call" | custom-call | flops 49999998976 | bytes 20000000 | tf_op jit(solution)/shard_map/reduce_dx/pallas_call | solution.py:377
  544.9 55.2 %collective-permute-done = f32[8,640]{1,0:T(8,128)S(1)} collective-permute-done((f32[8,640]{1,0:T(8,128)S(1)}, f32[8,640]{1,0:T(8,128)S(1)}, u32[]{:S(2)}, u32[]{:S(2)}) %collective-permute-start) | collective-permute-done | bytes 20512 | tf_op jit(solution)/shard_map/ppermute | solution.py:447
  601.2 13.2 %collective-permute-done.1.refs_2_ = f32[576,256]{1,0:T(8,128)S(1)} collective-permute-done((f32[576,256]{1,0:T(8,128)S(1)}, f32[576,256]{1,0:T(8,128)S(1)}, u32[]{:S(2)}, u32[]{:S(2)}) %collective-permute-start.1) | collective-permute-done | bytes 589856 | tf_op jit(solution)/shard_map/ppermute | solution.py:443
  616.4 125.2 %collective-permute-done.3.refs_2_ = f32[576,1024]{1,0:T(8,128)S(1)} collective-permute-done((f32[576,1024]{1,0:T(8,128)S(1)}, f32[576,1024]{1,0:T(8,128)S(1)}, u32[]{:S(2)}, u32[]{:S(2)}) %collective-permute-start.3) | collective-permute-done | bytes 2359328 | tf_op jit(solution)/shard_map/ppermute | solution.py:443
  743.7 4.1 convert_bitcast_fusion
  749.8 2.5 add_chunk.10.refs_0_
  754.5 9.2 %add_chunk.12.refs_0_ = f32[576,12288]{1,0:T(8,128)} custom-call(f32[576,12288]{1,0:T(8,128)} %add_chunk.11.refs_0_, f32[576,2048]{1,0:T(8,128)} %get-tuple-element.68.refs_1_, f32[576,2048]{1,0:T(8,128)} %collective-permute-done.4.refs_2_), custom_call_target="tpu_custom_call", output_to_operand_aliasing={{}: (0, {})} | custom-call | flops 1179648 | bytes 14155776 | tf_op jit(solution)/shard_map/add_chunk/pallas_call | solution.py:408
  763.7 9.9 %add_chunk.13.refs_0_ = f32[576,12288]{1,0:T(8,128)} custom-call(f32[576,12288]{1,0:T(8,128)} %add_chunk.12.refs_0_, f32[576,3072]{1,0:T(8,128)S(1)} %bitcast.8, f32[576,3072]{1,0:T(8,128)} %collective-permute-done.5.refs_2_), custom_call_target="tpu_custom_call", output_to_operand_aliasing={{}: (0, {})} | custom-call | flops 1769472 | bytes 21233664 | tf_op jit(solution)/shard_map/add_chunk/pallas_call | solution.py:408
  773.7 9.8 %add_chunk.14.refs_0_ = f32[576,12288]{1,0:T(8,128)} custom-call(f32[576,12288]{1,0:T(8,128)} %add_chunk.13.refs_0_, f32[576,3072]{1,0:T(8,128)S(1)} %bitcast.10, f32[576,3072]{1,0:T(8,128)} %collective-permute-done.6.refs_2_), custom_call_target="tpu_custom_call", output_to_operand_aliasing={{}: (0, {})} | custom-call | flops 1769472 | bytes 21233664 | tf_op jit(solution)/shard_map/add_chunk/pallas_call | solution.py:408
  783.5 3.2 add_chunk.15.refs_0_
  (71 shorter events, 28.8 us)
Async XLA Ops:
  1.3 68.5 %copy-start.15 = (f32[1,640]{1,0:T(1,128)}, f32[1,640]{1,0:T(1,128)S(1)}, u32[]{:S(2)}) copy-start(f32[1,640]{1,0:T(1,128)S(1)} %reshape.14.gain_ref) | copy-start | bytes 7684
  86.4 15.6 %copy-start.12 = (f32[576,256]{1,0:T(8,128)}, f32[576,256]{1,0:T(8,128)S(1)}, u32[]{:S(2)}) copy-start(f32[576,256]{1,0:T(8,128)S(1)} %get-tuple-element.65.refs_1_) | copy-start | bytes 1769476
  104.4 511.1 %collective-permute-start.2 = (f32[576,512]{1,0:T(8,128)}, f32[576,512]{1,0:T(8,128)}, u32[]{:S(2)}, u32[]{:S(2)}) collective-permute-start(f32[576,512]{1,0:T(8,128)} %get-tuple-element.66.refs_1_), channel_id=1, source_target_pairs={{0,4},{4,0},{1,5},{5,1},{2,6},{6,2},{3,7},{7,3}} | collective-permute-start | bytes 3538952 | tf_op jit(solution)/shard_map/ppermute | solution.py:443
  135.7 56.8 %copy-start.8 = (f32[576,1024]{1,0:T(8,128)}, f32[576,1024]{1,0:T(8,128)S(1)}, u32[]{:S(2)}) copy-start(f32[576,1024]{1,0:T(8,128)S(1)} %get-tuple-element.67.refs_1_) | copy-start | bytes 7077892
  192.5 550.3 %collective-permute-start.4 = (f32[576,2048]{1,0:T(8,128)}, f32[576,2048]{1,0:T(8,128)}, u32[]{:S(2)}, u32[]{:S(2)}) collective-permute-start(f32[576,2048]{1,0:T(8,128)} %get-tuple-element.68.refs_1_), channel_id=1, source_target_pairs={{0,4},{4,0},{1,5},{5,1},{2,6},{6,2},{3,7},{7,3}} | collective-permute-start | bytes 14155784 | tf_op jit(solution)/shard_map/ppermute | solution.py:443
  193.7 2.5 copy-start.1
  273.5 490.2 %collective-permute-start.5 = (f32[576,3072]{1,0:T(8,128)}, f32[576,3072]{1,0:T(8,128)}, u32[]{:S(2)}, u32[]{:S(2)}) collective-permute-start(f32[576,3072]{1,0:T(8,128)} %get-tuple-element.69.refs_1_), channel_id=1, source_target_pairs={{0,4},{4,0},{1,5},{5,1},{2,6},{6,2},{3,7},{7,3}} | collective-permute-start | bytes 21233672 | tf_op jit(solution)/shard_map/ppermute | solution.py:443
  354.0 419.7 %collective-permute-start.6 = (f32[576,3072]{1,0:T(8,128)}, f32[576,3072]{1,0:T(8,128)}, u32[]{:S(2)}, u32[]{:S(2)}) collective-permute-start(f32[576,3072]{1,0:T(8,128)} %get-tuple-element.70.refs_1_), channel_id=1, source_target_pairs={{0,4},{4,0},{1,5},{5,1},{2,6},{6,2},{3,7},{7,3}} | collective-permute-start | bytes 21233672 | tf_op jit(solution)/shard_map/ppermute | solution.py:443
  398.1 2.5 copy-start.3
  415.2 12.5 %copy-start.16 = (f32[1,640]{1,0:T(1,128)S(1)}, f32[1,640]{1,0:T(1,128)}, u32[]{:S(2)}) copy-start(f32[1,640]{1,0:T(1,128)} %copy-done.15) | copy-start | bytes 7684
  430.7 169.4 %copy-start.13 = (f32[576,256]{1,0:T(8,128)S(1)}, f32[576,256]{1,0:T(8,128)}, u32[]{:S(2)}) copy-start(f32[576,256]{1,0:T(8,128)} %copy-done.12) | copy-start | bytes 1769476
  430.7 184.9 %copy-start.9 = (f32[576,1024]{1,0:T(8,128)S(1)}, f32[576,1024]{1,0:T(8,128)}, u32[]{:S(2)}) copy-start(f32[576,1024]{1,0:T(8,128)} %copy-done.8) | copy-start | bytes 7077892
  430.7 312.1 %copy-start.11 = (f32[576,256]{1,0:T(8,128)S(1)}, f32[576,256]{1,0:T(8,128)}, u32[]{:S(2)}) copy-start(f32[576,256]{1,0:T(8,128)} %copy-done.10) | copy-start | bytes 1769476
  544.3 204.1 %copy-start.7 = (f32[576,2048]{1,0:T(8,128)S(1)}, f32[576,2048]{1,0:T(8,128)}, u32[]{:S(2)}) copy-start(f32[576,2048]{1,0:T(8,128)} %get-tuple-element.64.refs_0_) | copy-start | bytes 14155780
  544.3 55.8 %collective-permute-start = (f32[8,640]{1,0:T(8,128)S(1)}, f32[8,640]{1,0:T(8,128)S(1)}, u32[]{:S(2)}, u32[]{:S(2)}) collective-permute-start(f32[8,640]{1,0:T(8,128)S(1)} %get-tuple-element.63), channel_id=1, source_target_pairs={{0,4},{4,0},{1,5},{5,1},{2,6},{6,2},{3,7},{7,3}} | collective-permute-start | bytes 61448 | tf_op jit(solution)/shard_map/ppermute | solution.py:447
  600.1 14.3 %collective-permute-start.1 = (f32[576,256]{1,0:T(8,128)S(1)}, f32[576,256]{1,0:T(8,128)S(1)}, u32[]{:S(2)}, u32[]{:S(2)}) collective-permute-start(f32[576,256]{1,0:T(8,128)S(1)} %copy-done.13), channel_id=1, source_target_pairs={{0,4},{4,0},{1,5},{5,1},{2,6},{6,2},{3,7},{7,3}} | collective-permute-start | bytes 1769480 | tf_op jit(solution)/shard_map/ppermute | solution.py:443
  614.4 169.1 %collective-permute-start.7 = (f32[576,1536]{1,0:T(8,128)S(1)}, f32[576,1536]{1,0:T(8,128)S(1)}, u32[]{:S(2)}, u32[]{:S(2)}) collective-permute-start(f32[576,1536]{1,0:T(8,128)S(1)} %get-tuple-element.71.refs_1_), channel_id=1, source_target_pairs={{0,4},{4,0},{1,5},{5,1},{2,6},{6,2},{3,7},{7,3}} | collective-permute-start | bytes 10616840 | tf_op jit(solution)/shard_map/ppermute | solution.py:443
  615.5 126.1 %collective-permute-start.3 = (f32[576,1024]{1,0:T(8,128)S(1)}, f32[576,1024]{1,0:T(8,128)S(1)}, u32[]{:S(2)}, u32[]{:S(2)}) collective-permute-start(f32[576,1024]{1,0:T(8,128)S(1)} %copy-done.9), channel_id=1, source_target_pairs={{0,4},{4,0},{1,5},{5,1},{2,6},{6,2},{3,7},{7,3}} | collective-permute-start | bytes 7077896 | tf_op jit(solution)/shard_map/ppermute | solution.py:443
  741.6 45.0 %collective-permute-start.8 = (f32[576,512]{1,0:T(8,128)S(1)}, f32[576,512]{1,0:T(8,128)S(1)}, u32[]{:S(2)}, u32[]{:S(2)}) collective-permute-start(f32[576,512]{1,0:T(8,128)S(1)} %get-tuple-element.72.refs_1_), channel_id=1, source_target_pairs={{0,4},{4,0},{1,5},{5,1},{2,6},{6,2},{3,7},{7,3}} | collective-permute-start | bytes 3538952 | tf_op jit(solution)/shard_map/ppermute | solution.py:443
  742.8 45.1 %collective-permute-start.9 = (f32[576,256]{1,0:T(8,128)S(1)}, f32[576,256]{1,0:T(8,128)S(1)}, u32[]{:S(2)}, u32[]{:S(2)}) collective-permute-start(f32[576,256]{1,0:T(8,128)S(1)} %copy-done.11), channel_id=1, source_target_pairs={{0,4},{4,0},{1,5},{5,1},{2,6},{6,2},{3,7},{7,3}} | collective-permute-start | bytes 1769480 | tf_op jit(solution)/shard_map/ppermute | solution.py:443
  752.2 11.5 %slice-start = ((s8[7077888]{0:T(1024)(128)(4,1)}), s8[4194304]{0:T(1024)(128)(4,1)S(1)}, s32[]{:S(2)}) async-start(s8[7077888]{0:T(1024)(128)(4,1)} %bitcast.7), calls=%async_computation | async-start | bytes 8388608
  754.5 9.2 %slice-start.1 = ((s8[7077888]{0:T(1024)(128)(4,1)}), s8[2883584]{0:T(1024)(128)(4,1)S(1)}, s32[]{:S(2)}) async-start(s8[7077888]{0:T(1024)(128)(4,1)} %bitcast.7), calls=%async_computation.1 | async-start | bytes 5767168
  754.5 19.2 %slice-start.2 = ((s8[7077888]{0:T(1024)(128)(4,1)}), s8[4194304]{0:T(1024)(128)(4,1)S(1)}, s32[]{:S(2)}) async-start(s8[7077888]{0:T(1024)(128)(4,1)} %bitcast.9), calls=%async_computation.2 | async-start | bytes 8388608
  763.7 10.0 %slice-start.3 = ((s8[7077888]{0:T(1024)(128)(4,1)}), s8[2883584]{0:T(1024)(128)(4,1)S(1)}, s32[]{:S(2)}) async-start(s8[7077888]{0:T(1024)(128)(4,1)} %bitcast.9), calls=%async_computation.3 | async-start | bytes 5767168
  (9 other events, 14.2 us)

commit v2 on v1

--- a/solution.py
+++ b/solution.py
@@ -20,15 +20,10 @@
 NT_DIMS = (((1,), (1,)), ((), ()))
 
 
-def full_spec(shape, single=True):
-    zeros = (0,) * len(shape)
-    if single:
-        return pl.BlockSpec(shape, lambda j: zeros, pipeline_mode=pl.Buffered(1))
-    return pl.BlockSpec(shape, lambda j: zeros)
-
-
 STAT_TILE = 512
 STAT_ROWS = 256
+PER_BLOCK = STAT_ROWS // GROUP
+TAIL_STEP = 4
 
 
 def stats_kernel(hid_ref, gain_ref, mask_ref, tab_ref, tea_ref, x_ref, xt_ref, stat_ref,
@@ -36,10 +31,11 @@
     step = pl.program_id(0)
     dim, tokens = hid_ref.shape
     n_groups = tokens // GROUP
-    per_block = STAT_ROWS // GROUP
 
     @pl.when(step == 0)
     def _():
+        stu_acc[...] = jnp.zeros_like(stu_acc)
+        tea_acc[...] = jnp.zeros_like(tea_acc)
         rows = lax.broadcasted_iota(jnp.int32, (128, 128), 0) // GROUP
         cols = lax.broadcasted_iota(jnp.int32, (128, 128), 1)
         pick = jnp.where(rows == cols, 1.0, 0.0).astype(BF16)
@@ -54,8 +50,6 @@
             x_t = hid * inv_rms * gain
             xt_ref[:, blk * 128:(blk + 1) * 128] = x_t.astype(BF16)
             x_ref[blk * 128:(blk + 1) * 128, :] = x_t.T.astype(BF16)
-        stu_acc[...] = jnp.zeros_like(stu_acc)
-        tea_acc[...] = jnp.zeros_like(tea_acc)
         copy.wait()
 
         def add_group(g, n):
@@ -69,43 +63,71 @@
             groups[n_live + i] = n_groups
             return c
 
-        lax.fori_loop(0, 2 * per_block, pad, 0)
+        lax.fori_loop(0, PER_BLOCK, pad, 0)
         live[0] = n_live
 
-    n_pairs = (live[0] + 2 * per_block - 1) // (2 * per_block)
+    n_live = live[0]
+    n_full = n_live // PER_BLOCK
 
     def source(i):
         return pl.ds(pl.multiple_of(jnp.minimum(groups[i], n_groups - 1) * GROUP, GROUP), GROUP)
 
-    def logits(first, z_ref):
-        rows = jnp.concatenate([x_ref[source(first + i), :] for i in range(per_block)], axis=0)
+    def dest(i):
+        return pl.ds(pl.multiple_of(groups[i] * GROUP, GROUP), GROUP)
+
+    def logits(block, z_ref):
+        rows = jnp.concatenate([x_ref[source(block * PER_BLOCK + i), :] for i in range(PER_BLOCK)], axis=0)
         z_ref[...] = jnp.dot(rows, tab_ref[...], preferred_element_type=F32)
 
-    def lane_sum(val):
+    def exp_sum(val):
+        val = jnp.exp2(jnp.tanh(val * INV_CAP) * CAP_LOG2E)
         total = val[:, :128]
         for lane in range(128, STAT_TILE, 128):
             total = total + val[:, lane:lane + 128]
         return total
 
-    def accumulate(first, z_ref):
-        for i in range(per_block):
-            dest = pl.ds(pl.multiple_of(groups[first + i] * GROUP, GROUP), GROUP)
-            tea = jnp.tanh(tea_ref[source(first + i), :].astype(F32) * INV_CAP)
-            tea_acc[dest, :] += lane_sum(jnp.exp2(tea * CAP_LOG2E))
-            stu = jnp.tanh(z_ref[i * GROUP:(i + 1) * GROUP, :] * INV_CAP)
-            stu_acc[dest, :] += lane_sum(jnp.exp2(stu * CAP_LOG2E))
+    def teacher_group(i):
+        tea_acc[dest(i), :] += exp_sum(tea_ref[source(i), :].astype(F32))
+
+    def student_group(i, z):
+        stu_acc[dest(i), :] += exp_sum(z)
+
+    def accumulate(block, z_ref):
+        for i in range(PER_BLOCK):
+            teacher_group(block * PER_BLOCK + i)
+            student_group(block * PER_BLOCK + i, z_ref[i * GROUP:(i + 1) * GROUP, :])
 
     logits(0, z_even)
+    for i in range(PER_BLOCK):
+        teacher_group(n_full * PER_BLOCK + i)
 
     def pair(p, c):
-        first = p * 2 * per_block
-        logits(first + per_block, z_odd)
-        accumulate(first, z_even)
-        logits(jnp.minimum(first + 2 * per_block, n_groups), z_even)
-        accumulate(first + per_block, z_odd)
+        logits(2 * p + 1, z_odd)
+        accumulate(2 * p, z_even)
+        logits(2 * p + 2, z_even)
+        accumulate(2 * p + 1, z_odd)
         return c
 
-    lax.fori_loop(0, n_pairs, pair, 0)
+    lax.fori_loop(0, n_full // 2, pair, 0)
+
+    def tail(z_ref):
+        def some(q, c):
+            for i in range(TAIL_STEP):
+                row = pl.multiple_of((q * TAIL_STEP + i) * GROUP, GROUP)
+                student_group(n_full * PER_BLOCK + q * TAIL_STEP + i, z_ref[pl.ds(row, GROUP), :])
+            return c
+
+        lax.fori_loop(0, (n_live - n_full * PER_BLOCK + TAIL_STEP - 1) // TAIL_STEP, some, 0)
+
+    @pl.when(n_full % 2 == 1)
+    def _():
+        logits(n_full, z_odd)
+        accumulate(n_full - 1, z_even)
+        tail(z_odd)
+
+    @pl.when(n_full % 2 == 0)
+    def _():
+        tail(z_even)
 
     @pl.when(step == pl.num_programs(0) - 1)
     def _():
@@ -119,16 +141,16 @@
     dim, tokens = hid_t.shape
     vocab = tab_t.shape[1]
     n_groups = tokens // GROUP
-    extra = 2 * (STAT_ROWS // GROUP)
+    whole = pl.BlockSpec(memory_space=VMEM)
     return pl.pallas_call(
         stats_kernel,
         grid=(vocab // STAT_TILE,),
         in_specs=[
-            full_spec(hid_t.shape), full_spec(gain.shape), full_spec(mask.shape),
+            whole, whole, whole,
             pl.BlockSpec((dim, STAT_TILE), lambda j: (0, j)),
             pl.BlockSpec((tokens, STAT_TILE), lambda j: (0, j)),
         ],
-        out_specs=[full_spec((tokens, dim)), full_spec((dim, tokens)), full_spec((32, 128))],
+        out_specs=[whole, whole, whole],
         out_shape=[
             jax.ShapeDtypeStruct((tokens, dim), BF16),
             jax.ShapeDtypeStruct((dim, tokens), BF16),
@@ -138,10 +160,10 @@
             VMEM((tokens + GROUP, 128), F32), VMEM((tokens + GROUP, 128), F32),
             VMEM((STAT_ROWS, STAT_TILE), F32), VMEM((STAT_ROWS, STAT_TILE), F32),
             VMEM((16, 128), jnp.int32), pltpu.SMEM((16, 128), jnp.int32),
-            pltpu.SMEM((n_groups + 2 * extra,), jnp.int32), pltpu.SMEM((1,), jnp.int32),
+            pltpu.SMEM((n_groups + 2 * PER_BLOCK,), jnp.int32), pltpu.SMEM((1,), jnp.int32),
             pltpu.SemaphoreType.DMA,
         ],
-        compiler_params=pltpu.CompilerParams(dimension_semantics=("arbitrary",), vmem_limit_bytes=40 * 2**20),
+        compiler_params=pltpu.CompilerParams(dimension_semantics=("arbitrary",), vmem_limit_bytes=46 * 2**20),
         cost_estimate=pl.CostEstimate(flops=50_000_000_000, bytes_accessed=70_000_000, transcendentals=0),
         name="stats",
     )(hid_t, gain, mask, tab_t, tea)
@@ -211,105 +233,110 @@
 
 GRAD_TILE = 256
 GRAD_ROWS = 256
+SLICE = 16
 
 
 def chunk_kernel(first, x_ref, xt_ref, stu_col, tea_col, tab_ref, tea_ref, *refs):
     if first:
-        de_ref, dx_out, kl_out, dx_acc, kl_acc, g_ref, sem = refs
+        de_ref, dx_acc, kl_acc, g_ref, z_even, z_odd = refs
     else:
-        dx_in, kl_in, de_ref, dx_out, kl_out, dx_acc, kl_acc, g_ref, sem = refs
-    step = pl.program_id(0)
+        _, _, de_ref, dx_acc, kl_acc, g_ref, z_even, z_odd = refs
     tokens = x_ref.shape[0]
-
-    @pl.when(step == 0)
-    def _():
-        if first:
+    n_blocks = tokens // GRAD_ROWS
+
+    if first:
+        @pl.when(pl.program_id(0) == 0)
+        def _():
             dx_acc[...] = jnp.zeros_like(dx_acc)
             kl_acc[...] = jnp.zeros_like(kl_acc)
-        else:
-            loads = [pltpu.make_async_copy(dx_in, dx_acc, sem.at[0]), pltpu.make_async_copy(kl_in, kl_acc, sem.at[1])]
-            for load in loads:
-                load.start()
-            for load in loads:
-                load.wait()
-
-    def block(b, c):
-        rows = pl.ds(pl.multiple_of(b * GRAD_ROWS, GRAD_ROWS), GRAD_ROWS)
-        z = jnp.dot(x_ref[rows, :], tab_ref[...], preferred_element_type=F32)
-        stu_scale = stu_col[rows, :]
-        tea_scale = tea_col[rows, :]
-        kl = kl_acc[rows, :]
-        parts = []
-        for lane in range(0, GRAD_TILE, 128):
-            stu = jnp.tanh(z[:, lane:lane + 128] * INV_CAP)
-            tea = jnp.tanh(tea_ref[rows, lane:lane + 128].astype(F32) * INV_CAP)
-            stu_p = jnp.exp2(stu * CAP_LOG2E) * stu_scale
-            tea_p = jnp.exp2(tea * CAP_LOG2E) * tea_scale
-            kl = kl + tea_p * (tea - stu)
-            parts.append(((stu_p - tea_p) * (1.0 - stu * stu)).astype(BF16))
-        kl_acc[rows, :] = kl
-        g = jnp.concatenate(parts, axis=1)
-        g_ref[rows, :] = g
-        dx_acc[rows, :] += lax.dot_general(g, tab_ref[...], NT_DIMS, preferred_element_type=F32)
+
+    def window(b, size=GRAD_ROWS, skip=0):
+        return pl.ds(pl.multiple_of(b * GRAD_ROWS + skip, size), size)
+
+    def logits(b, z_ref):
+        z_ref[...] = jnp.dot(x_ref[window(b), :], tab_ref[...], preferred_element_type=F32)
+
+    def grads(b, z_ref):
+        for skip in range(0, GRAD_ROWS, SLICE):
+            rows = window(b, SLICE, skip)
+            stu_scale = stu_col[rows, :]
+            tea_scale = tea_col[rows, :]
+            kl = kl_acc[rows, :]
+            parts = []
+            for lane in range(0, GRAD_TILE, 128):
+                stu = jnp.tanh(z_ref[skip:skip + SLICE, lane:lane + 128] * INV_CAP)
+                tea = jnp.tanh(tea_ref[rows, lane:lane + 128].astype(F32) * INV_CAP)
+                stu_p = jnp.exp2(stu * CAP_LOG2E) * stu_scale
+                tea_p = jnp.exp2(tea * CAP_LOG2E) * tea_scale
+                kl = kl + tea_p * (tea - stu)
+                parts.append(((stu_p - tea_p) * (1.0 - stu * stu)).astype(BF16))
+            kl_acc[rows, :] = kl
+            g_ref[rows, :] = jnp.concatenate(parts, axis=1)
+
+    def add_dx(b):
+        dx_acc[window(b), :] += lax.dot_general(g_ref[window(b), :], tab_ref[...], NT_DIMS, preferred_element_type=F32)
+
+    logits(0, z_even)
+    logits(1, z_odd)
+    grads(0, z_even)
+
+    def pair(p, c):
+        add_dx(2 * p)
+        logits(2 * p + 2, z_even)
+        grads(2 * p + 1, z_odd)
+        add_dx(2 * p + 1)
+        logits(2 * p + 3, z_odd)
+        grads(2 * p + 2, z_even)
         return c
 
-    lax.fori_loop(0, tokens // GRAD_ROWS, block, 0)
+    lax.fori_loop(0, n_blocks // 2 - 1, pair, 0)
+    add_dx(n_blocks - 2)
+    grads(n_blocks - 1, z_odd)
     de_ref[...] = jnp.dot(xt_ref[...], g_ref[...], preferred_element_type=F32)
-
-    @pl.when(step == pl.num_programs(0) - 1)
-    def _():
-        saves = [pltpu.make_async_copy(dx_acc, dx_out, sem.at[0]), pltpu.make_async_copy(kl_acc, kl_out, sem.at[1])]
-        for save in saves:
-            save.start()
-        for save in saves:
-            save.wait()
+    add_dx(n_blocks - 1)
 
 
 def chunk_grad(start, size, x, x_t, stu_col, tea_col, tab_t, tea, carry):
     tokens, dim = x.shape
     off = start // GRAD_TILE
-    hbm = pl.BlockSpec(memory_space=pl.ANY)
+    whole = pl.BlockSpec(memory_space=VMEM)
     first = carry is None
     work = tokens * size
     return pl.pallas_call(
         functools.partial(chunk_kernel, first),
         grid=(size // GRAD_TILE,),
         in_specs=[
-            full_spec((tokens, dim)), full_spec((dim, tokens)), full_spec((tokens, 128)), full_spec((tokens, 128)),
+            whole, whole, whole, whole,
             pl.BlockSpec((dim, GRAD_TILE), lambda j: (0, j + off)),
             pl.BlockSpec((tokens, GRAD_TILE), lambda j: (0, j + off)),
-        ] + ([] if first else [hbm, hbm]),
-        out_specs=[pl.BlockSpec((dim, GRAD_TILE), lambda j: (0, j)), hbm, hbm],
+        ] + ([] if first else [whole, whole]),
+        out_specs=[pl.BlockSpec((dim, GRAD_TILE), lambda j: (0, j)), whole, whole],
         out_shape=[
             jax.ShapeDtypeStruct((dim, size), F32),
             jax.ShapeDtypeStruct((tokens, dim), F32),
             jax.ShapeDtypeStruct((tokens, 128), F32),
         ],
         scratch_shapes=[
-            VMEM((tokens, dim), F32), VMEM((tokens, 128), F32), VMEM((tokens, GRAD_TILE), BF16),
-            pltpu.SemaphoreType.DMA((2,)),
+            VMEM((tokens, GRAD_TILE), BF16), VMEM((GRAD_ROWS, GRAD_TILE), F32), VMEM((GRAD_ROWS, GRAD_TILE), F32),
         ],
         input_output_aliases={} if first else {6: 1, 7: 2},
-        compiler_params=pltpu.CompilerParams(dimension_semantics=("arbitrary",), vmem_limit_bytes=40 * 2**20),
+        compiler_params=pltpu.CompilerParams(dimension_semantics=("arbitrary",), vmem_limit_bytes=32 * 2**20),
         cost_estimate=pl.CostEstimate(flops=work * 3 * 2 * dim, bytes_accessed=work * 2, transcendentals=0),
         name="chunk_grad",
     )(x, x_t, stu_col, tea_col, tab_t, tea, *(() if first else carry))
 
 
 def dx_kernel(n_tp, dx_ref, kl_ref, base_ref, hid_ref, gain_ref, gh_ref, part_ref,
-              dxt, slots, own, parts_buf, part_out, local_sem, send_sem, recv_sem):
+              slots, own, parts_buf, part_out, send_sem, recv_sem):
     tp = lax.axis_index("tp")
     dp = lax.axis_index("dp")
     dim, tokens = hid_ref.shape
     width = tokens // n_tp
-    load = pltpu.make_async_copy(dx_ref, dxt, local_sem.at[0])
-    load.start()
     barrier = pltpu.get_barrier_semaphore()
     peers = [lax.rem(tp + k, n_tp) for k in range(1, n_tp)]
     for peer in peers:
         pl.semaphore_signal(barrier, inc=1, device_id=(dp, peer), device_id_type=MESH)
     pl.semaphore_wait(barrier, n_tp - 1)
-    load.wait()
 
     def window(index):
         return pl.ds(pl.multiple_of(index * width, width), width)
@@ -317,7 +344,7 @@
     reduce = []
     for k, peer in enumerate(peers):
         reduce.append(pltpu.make_async_remote_copy(
-            src_ref=dxt.at[window(peer), :], dst_ref=slots.at[k],
+            src_ref=dx_ref.at[window(peer), :], dst_ref=slots.at[k],
             send_sem=send_sem.at[0, k], recv_sem=recv_sem.at[0, k], device_id=(dp, peer), device_id_type=MESH))
         reduce[-1].start()
     for copy in reduce:
@@ -326,7 +353,7 @@
     total = jnp.zeros((width, dim), F32)
     for owner in range(n_tp):
         gap = lax.rem(tp - owner + n_tp, n_tp)
-        part = dxt[mine, :]
+        part = dx_ref[mine, :]
         for k in range(1, n_tp):
             part = jnp.where(gap == k, slots[k - 1], part)
         total = total + part
@@ -376,18 +403,18 @@
     whole = pl.BlockSpec(memory_space=VMEM)
     return pl.pallas_call(
         functools.partial(dx_kernel, n_tp),
-        in_specs=[pl.BlockSpec(memory_space=pl.ANY), whole, whole, whole, whole],
+        in_specs=[whole, whole, whole, whole, whole],
         out_specs=[whole, whole],
         out_shape=[
             jax.ShapeDtypeStruct((dim, tokens), F32),
-            jax.ShapeDtypeStruct((8, gain.shape[1]), F32),
+            jax.ShapeDtypeStruct((8, 640), F32),
         ],
         scratch_shapes=[
-            VMEM((tokens, dim), F32), VMEM((n_tp - 1, width, dim), F32), VMEM((dim, width), F32),
-            VMEM((n_tp, 8, gain.shape[1]), F32), VMEM((8, gain.shape[1]), F32),
-            pltpu.SemaphoreType.DMA((1,)), pltpu.SemaphoreType.DMA((3, n_tp - 1)), pltpu.SemaphoreType.DMA((3, n_tp - 1)),
-        ],
-        compiler_params=pltpu.CompilerParams(collective_id=1, has_side_effects=True, vmem_limit_bytes=48 * 2**20),
+            VMEM((n_tp - 1, width, dim), F32), VMEM((dim, width), F32),
+            VMEM((n_tp, 8, 640), F32), VMEM((8, 640), F32),
+            pltpu.SemaphoreType.DMA((3, n_tp - 1)), pltpu.SemaphoreType.DMA((3, n_tp - 1)),
+        ],
+        compiler_params=pltpu.CompilerParams(collective_id=1, has_side_effects=True, vmem_limit_bytes=24 * 2**20),
         cost_estimate=pl.CostEstimate(flops=50_000_000_000, bytes_accessed=20_000_000, transcendentals=0),
         name="reduce_dx",
     )(dx, kl, base, hid_t, gain)
@@ -418,7 +445,7 @@
     )(*lead, own, other)
 
 
-CHUNKS = (256, 512, 1024, 2048, 3072, 3072, 1536, 512, 256)
+CHUNKS = (256, 512, 1536, 3584, 3584, 2048, 512, 256)
 
 
 def solution(mesh):
@@ -431,7 +458,7 @@
         hid_t = hid_rows.T
         tab_t = tab_rows.T
         mask = mask_rows.reshape(tokens // 128, 128)
-        gain = jnp.pad(w_final, (0, 640 - dim)).reshape(1, 640)
+        gain = w_final.reshape(1, dim)
         x, x_t, stat = stats(hid_t, gain, mask, tab_t, tea_rows)
         stu_col, tea_col, base = gather_stats(stat, mask, n_tp)
         carry = None
@@ -444,7 +471,8 @@
             own.append(part)
             start += size
         gh_t, share = reduce_dx(*carry, base, hid_t, gain, n_tp)
-        share = share + lax.ppermute(share, "dp", swap)
+        share_other = lax.ppermute(share, "dp", swap)
+        share = share + share_other
         out = None
         start = 0
         for size, a, b in zip(CHUNKS, own, other):

time: 790 us -> 745 us (0.943)
  Pallas kernels: 559 us -> 424 us
  waiting for transfers between devices: 194 us -> 304 us
  local copies, waits for them, and re-layouts: 21 us -> 4.19 us
    ppermute x1, waiting for transfers between devices: 55.2 us -> 266 us  [step(): share_other = lax.ppermute(share, 'dp', swap)]
    pallas_call x9 -> x8, Pallas kernels: 332 us -> 190 us  [chunk_grad(): pl.pallas_call(functools.partial(chunk_kernel, first), grid=(size // GRAD...]
    ppermute x9 -> x8, waiting for transfers between devices: 138 us -> 37.9 us  [step(): other.append(lax.ppermute(part, 'dp', swap))]
    unnamed x46 -> x10, local copies, waits for them, and re-layouts: 19.2 us -> 2.38 us
    pallas_call x9 -> x8, Pallas kernels: 39.8 us -> 45.2 us  [add_chunk(): pl.pallas_call(add_kernel, grid=(size // tile,), in_specs=[hbm, block, bl...]
  transfers between devices with their start and end apart: 10 -> 9, of which waited for: 3 -> 3; matrix products, arithmetic and copies ran while one was open for 1% -> 0% of each run, Pallas kernels for 58% -> 42%
where the time goes in v2:
time: 745 us; the launch traced here: 744 us
  Pallas kernels  424 us (57%)
  waiting for transfers between devices  304 us (41%)
  starting transfers between devices  9.51 us (1%)
    ppermute x1, waiting for transfers between devices, step(): share_other = lax.ppermute(share, 'dp', swap)  266 us
    pallas_call x8, Pallas kernels, chunk_grad(): pl.pallas_call(functools.partial(chunk_kernel, first), grid=(size // GRAD...  190 us
    pallas_call x1, Pallas kernels, reduce_dx(): pl.pallas_call(functools.partial(dx_kernel, n_tp), in_specs=[whole, whole...  112 us
    pallas_call x1, Pallas kernels, stats(): pl.pallas_call(stats_kernel, grid=(vocab // STAT_TILE,), in_specs=[whole,...  70.2 us
    pallas_call x8, Pallas kernels, add_chunk(): pl.pallas_call(add_kernel, grid=(size // tile,), in_specs=[hbm, block, bl...  45.2 us
    ppermute x8, waiting for transfers between devices, step(): other.append(lax.ppermute(part, 'dp', swap))  37.9 us
  transfers between devices with their start and end apart: 9, of which 3 were waited for; matrix products, arithmetic and copies ran while one was open for 0% of the time, Pallas kernels for 42%

profile of v2, /device:TPU:0, one launch (start us, length us, event | category | flops | bytes accessed | tf_op | source)
XLA Modules:
  0.0 743.8 jit_solution(5859375965404967403)
XLA Ops:
  2.0 1.7 copy-done.3
  3.7 70.2 %stats.1 = (bf16[2048,576]{1,0:T(8,128)(2,1)S(1)}, bf16[576,2048]{1,0:T(8,128)(2,1)S(1)}, f32[32,128]{1,0:T(8,128)S(1)}) custom-call(bf16[576,2048]{1,0:T(8,128)(2,1)S(1)} %bitcast.9, f32[1,576]{1,0:T(1,128)S(1)} %reshape.14.gain_ref, f32[16,128]{1,0:T(8,128)S(1)} %bitcast.7, bf16[576,12288]{1,0:T(8,128)(2,1)} %bitcast.12, bf16[2048,12288]{1,0:T(8,128)(2,1)} %tea_ref.17), custom_call_target="tpu_custom_call" | custom-call | flops 49999998976 | bytes 70000000 | tf_op jit(solution)/shard_map/stats/pallas_call | solution.py:145
  73.9 6.1 gather_stats.1
  80.0 5.3 chunk_grad.8
  85.2 8.7 %chunk_grad.9 = (f32[576,512]{1,0:T(8,128)S(1)}, f32[2048,576]{1,0:T(8,128)S(1)}, f32[2048,128]{1,0:T(8,128)S(1)}) custom-call(bf16[2048,576]{1,0:T(8,128)(2,1)S(1)} %get-tuple-element.36.x_ref, bf16[576,2048]{1,0:T(8,128)(2,1)S(1)} %get-tuple-element.37.xt_ref, ...), custom_call_target="tpu_custom_call", output_to_operand_aliasing={{1}: (6, {}), {2}: (7, {})} | custom-call | flops 3623878656 | bytes 2097152 | tf_op jit(solution)/shard_map/chunk_grad/pallas_call | solution.py:305
  94.0 24.2 %chunk_grad.10 = (f32[576,1536]{1,0:T(8,128)}, f32[2048,576]{1,0:T(8,128)S(1)}, f32[2048,128]{1,0:T(8,128)S(1)}) custom-call(bf16[2048,576]{1,0:T(8,128)(2,1)S(1)} %get-tuple-element.36.x_ref, bf16[576,2048]{1,0:T(8,128)(2,1)S(1)} %get-tuple-element.37.xt_ref, ...), custom_call_target="tpu_custom_call", output_to_operand_aliasing={{1}: (6, {}), {2}: (7, {})} | custom-call | flops 10871635968 | bytes 6291456 | tf_op jit(solution)/shard_map/chunk_grad/pallas_call | solution.py:305
  118.1 1.9 collective-permute-start.3
  120.0 53.5 %chunk_grad.11 = (f32[576,3584]{1,0:T(8,128)}, f32[2048,576]{1,0:T(8,128)S(1)}, f32[2048,128]{1,0:T(8,128)S(1)}) custom-call(bf16[2048,576]{1,0:T(8,128)(2,1)S(1)} %get-tuple-element.36.x_ref, bf16[576,2048]{1,0:T(8,128)(2,1)S(1)} %get-tuple-element.37.xt_ref, ...), custom_call_target="tpu_custom_call", output_to_operand_aliasing={{1}: (6, {}), {2}: (7, {})} | custom-call | flops 25367150592 | bytes 14680064 | tf_op jit(solution)/shard_map/chunk_grad/pallas_call | solution.py:305
  173.7 53.5 %chunk_grad.12 = (f32[576,3584]{1,0:T(8,128)}, f32[2048,576]{1,0:T(8,128)S(1)}, f32[2048,128]{1,0:T(8,128)S(1)}) custom-call(bf16[2048,576]{1,0:T(8,128)(2,1)S(1)} %get-tuple-element.36.x_ref, bf16[576,2048]{1,0:T(8,128)(2,1)S(1)} %get-tuple-element.37.xt_ref, ...), custom_call_target="tpu_custom_call", output_to_operand_aliasing={{1}: (6, {}), {2}: (7, {})} | custom-call | flops 25367150592 | bytes 14680064 | tf_op jit(solution)/shard_map/chunk_grad/pallas_call | solution.py:305
  227.1 1.8 collective-permute-start.5
  229.0 31.5 %chunk_grad.13 = (f32[576,2048]{1,0:T(8,128)}, f32[2048,576]{1,0:T(8,128)S(1)}, f32[2048,128]{1,0:T(8,128)S(1)}) custom-call(bf16[2048,576]{1,0:T(8,128)(2,1)S(1)} %get-tuple-element.36.x_ref, bf16[576,2048]{1,0:T(8,128)(2,1)S(1)} %get-tuple-element.37.xt_ref, ...), custom_call_target="tpu_custom_call", output_to_operand_aliasing={{1}: (6, {}), {2}: (7, {})} | custom-call | flops 14495514624 | bytes 8388608 | tf_op jit(solution)/shard_map/chunk_grad/pallas_call | solution.py:305
  260.6 8.7 %chunk_grad.14 = (f32[576,512]{1,0:T(8,128)S(1)}, f32[2048,576]{1,0:T(8,128)S(1)}, f32[2048,128]{1,0:T(8,128)S(1)}) custom-call(bf16[2048,576]{1,0:T(8,128)(2,1)S(1)} %get-tuple-element.36.x_ref, bf16[576,2048]{1,0:T(8,128)(2,1)S(1)} %get-tuple-element.37.xt_ref, ...), custom_call_target="tpu_custom_call", output_to_operand_aliasing={{1}: (6, {}), {2}: (7, {})} | custom-call | flops 3623878656 | bytes 2097152 | tf_op jit(solution)/shard_map/chunk_grad/pallas_call | solution.py:305
  269.4 5.1 chunk_grad.15
  274.5 112.3 %reduce_dx.1 = (f32[576,2048]{1,0:T(8,128)S(1)}, f32[8,640]{1,0:T(8,128)S(1)}) custom-call(f32[2048,576]{1,0:T(8,128)S(1)} %get-tuple-element.55.dx_ref, f32[2048,128]{1,0:T(8,128)S(1)} %get-tuple-element.56.kl_ref, f32[8,128]{1,0:T(8,128)S(1)} %get-tuple-element.57.base_ref, bf16[576,2048]{1,0:T(8,128)(2,1)S(1)} %bitcast.10, f32[1,576]{1,0:T(1,128)S(1)} %copy-done.2), custom_call_target="tpu_custom_call" | custom-call | flops 49999998976 | bytes 20000000 | tf_op jit(solution)/shard_map/reduce_dx/pallas_call | solution.py:404
  386.8 265.7 %collective-permute-done = f32[8,640]{1,0:T(8,128)S(1)} collective-permute-done((f32[8,640]{1,0:T(8,128)S(1)}, f32[8,640]{1,0:T(8,128)S(1)}, u32[]{:S(2)}, u32[]{:S(2)}) %collective-permute-start) | collective-permute-done | bytes 20512 | tf_op jit(solution)/shard_map/ppermute | solution.py:474
  652.5 1.7 collective-permute-start.1
  654.2 13.0 %collective-permute-done.1.refs_2_ = f32[576,256]{1,0:T(8,128)S(1)} collective-permute-done((f32[576,256]{1,0:T(8,128)S(1)}, f32[576,256]{1,0:T(8,128)S(1)}, u32[]{:S(2)}, u32[]{:S(2)}) %collective-permute-start.1) | collective-permute-done | bytes 589856 | tf_op jit(solution)/shard_map/ppermute | solution.py:470
  667.2 1.6 collective-permute-start.2
  668.8 24.9 %collective-permute-done.2.refs_2_ = f32[576,512]{1,0:T(8,128)S(1)} collective-permute-done((f32[576,512]{1,0:T(8,128)S(1)}, f32[576,512]{1,0:T(8,128)S(1)}, u32[]{:S(2)}, u32[]{:S(2)}) %collective-permute-start.2) | collective-permute-done | bytes 1179680 | tf_op jit(solution)/shard_map/ppermute | solution.py:470
  695.7 1.8 convert_bitcast_fusion
  700.7 6.1 add_chunk.10.refs_0_
  706.9 13.4 %add_chunk.11.refs_0_ = f32[576,12288]{1,0:T(8,128)} custom-call(f32[576,12288]{1,0:T(8,128)} %add_chunk.10.refs_0_, f32[576,3584]{1,0:T(8,128)} %get-tuple-element.63.refs_1_, f32[576,3584]{1,0:T(8,128)} %collective-permute-done.4.refs_2_), custom_call_target="tpu_custom_call", output_to_operand_aliasing={{}: (0, {})} | custom-call | flops 2064384 | bytes 24772608 | tf_op jit(solution)/shard_map/add_chunk/pallas_call | solution.py:435
  720.3 13.4 %add_chunk.12.refs_0_ = f32[576,12288]{1,0:T(8,128)} custom-call(f32[576,12288]{1,0:T(8,128)} %add_chunk.11.refs_0_, f32[576,3584]{1,0:T(8,128)} %get-tuple-element.64.refs_1_, f32[576,3584]{1,0:T(8,128)} %collective-permute-done.5.refs_2_), custom_call_target="tpu_custom_call", output_to_operand_aliasing={{}: (0, {})} | custom-call | flops 2064384 | bytes 24772608 | tf_op jit(solution)/shard_map/add_chunk/pallas_call | solution.py:435
  733.7 8.0 %add_chunk.13.refs_0_ = f32[576,12288]{1,0:T(8,128)} custom-call(f32[576,12288]{1,0:T(8,128)} %add_chunk.12.refs_0_, f32[576,2048]{1,0:T(8,128)} %get-tuple-element.65.refs_1_, f32[576,2048]{1,0:T(8,128)} %collective-permute-done.6.refs_2_), custom_call_target="tpu_custom_call", output_to_operand_aliasing={{}: (0, {})} | custom-call | flops 1179648 | bytes 14155776 | tf_op jit(solution)/shard_map/add_chunk/pallas_call | solution.py:435
  (28 shorter events, 9.2 us)
Async XLA Ops:
  1.3 72.6 %copy-start.1 = (f32[1,576]{1,0:T(1,128)}, f32[1,576]{1,0:T(1,128)S(1)}, u32[]{:S(2)}) copy-start(f32[1,576]{1,0:T(1,128)S(1)} %reshape.14.gain_ref) | copy-start | bytes 6916
  1.3 0.7 copy-start
  2.0 1.7 copy-start.3
  118.1 577.1 %collective-permute-start.3 = (f32[576,1536]{1,0:T(8,128)}, f32[576,1536]{1,0:T(8,128)}, u32[]{:S(2)}, u32[]{:S(2)}) collective-permute-start(f32[576,1536]{1,0:T(8,128)} %get-tuple-element.62.refs_1_), channel_id=1, source_target_pairs={{0,4},{4,0},{1,5},{5,1},{2,6},{6,2},{3,7},{7,3}} | collective-permute-start | bytes 10616840 | tf_op jit(solution)/shard_map/ppermute | solution.py:470
  173.5 533.4 %collective-permute-start.4 = (f32[576,3584]{1,0:T(8,128)}, f32[576,3584]{1,0:T(8,128)}, u32[]{:S(2)}, u32[]{:S(2)}) collective-permute-start(f32[576,3584]{1,0:T(8,128)} %get-tuple-element.63.refs_1_), channel_id=1, source_target_pairs={{0,4},{4,0},{1,5},{5,1},{2,6},{6,2},{3,7},{7,3}} | collective-permute-start | bytes 24772616 | tf_op jit(solution)/shard_map/ppermute | solution.py:470
  227.1 493.2 %collective-permute-start.5 = (f32[576,3584]{1,0:T(8,128)}, f32[576,3584]{1,0:T(8,128)}, u32[]{:S(2)}, u32[]{:S(2)}) collective-permute-start(f32[576,3584]{1,0:T(8,128)} %get-tuple-element.64.refs_1_), channel_id=1, source_target_pairs={{0,4},{4,0},{1,5},{5,1},{2,6},{6,2},{3,7},{7,3}} | collective-permute-start | bytes 24772616 | tf_op jit(solution)/shard_map/ppermute | solution.py:470
  260.4 473.3 %collective-permute-start.6 = (f32[576,2048]{1,0:T(8,128)}, f32[576,2048]{1,0:T(8,128)}, u32[]{:S(2)}, u32[]{:S(2)}) collective-permute-start(f32[576,2048]{1,0:T(8,128)} %get-tuple-element.65.refs_1_), channel_id=1, source_target_pairs={{0,4},{4,0},{1,5},{5,1},{2,6},{6,2},{3,7},{7,3}} | collective-permute-start | bytes 14155784 | tf_op jit(solution)/shard_map/ppermute | solution.py:470
  269.3 5.1 copy-start.2
  269.4 5.1 copy-start.4
  386.8 265.7 %collective-permute-start = (f32[8,640]{1,0:T(8,128)S(1)}, f32[8,640]{1,0:T(8,128)S(1)}, u32[]{:S(2)}, u32[]{:S(2)}) collective-permute-start(f32[8,640]{1,0:T(8,128)S(1)} %get-tuple-element.58), channel_id=1, source_target_pairs={{0,4},{4,0},{1,5},{5,1},{2,6},{6,2},{3,7},{7,3}} | collective-permute-start | bytes 61448 | tf_op jit(solution)/shard_map/ppermute | solution.py:474
  652.5 14.7 %collective-permute-start.1 = (f32[576,256]{1,0:T(8,128)S(1)}, f32[576,256]{1,0:T(8,128)S(1)}, u32[]{:S(2)}, u32[]{:S(2)}) collective-permute-start(f32[576,256]{1,0:T(8,128)S(1)} %get-tuple-element.60.refs_1_), channel_id=1, source_target_pairs={{0,4},{4,0},{1,5},{5,1},{2,6},{6,2},{3,7},{7,3}} | collective-permute-start | bytes 1769480 | tf_op jit(solution)/shard_map/ppermute | solution.py:470
  667.2 26.5 %collective-permute-start.2 = (f32[576,512]{1,0:T(8,128)S(1)}, f32[576,512]{1,0:T(8,128)S(1)}, u32[]{:S(2)}, u32[]{:S(2)}) collective-permute-start(f32[576,512]{1,0:T(8,128)S(1)} %get-tuple-element.61.refs_1_), channel_id=1, source_target_pairs={{0,4},{4,0},{1,5},{5,1},{2,6},{6,2},{3,7},{7,3}} | collective-permute-start | bytes 3538952 | tf_op jit(solution)/shard_map/ppermute | solution.py:470
  693.7 48.0 %collective-permute-start.7 = (f32[576,512]{1,0:T(8,128)S(1)}, f32[576,512]{1,0:T(8,128)S(1)}, u32[]{:S(2)}, u32[]{:S(2)}) collective-permute-start(f32[576,512]{1,0:T(8,128)S(1)} %get-tuple-element.66.refs_1_), channel_id=1, source_target_pairs={{0,4},{4,0},{1,5},{5,1},{2,6},{6,2},{3,7},{7,3}} | collective-permute-start | bytes 3538952 | tf_op jit(solution)/shard_map/ppermute | solution.py:470
  695.2 47.7 %collective-permute-start.8 = (f32[576,256]{1,0:T(8,128)S(1)}, f32[576,256]{1,0:T(8,128)S(1)}, u32[]{:S(2)}, u32[]{:S(2)}) collective-permute-start(f32[576,256]{1,0:T(8,128)S(1)} %get-tuple-element.67.refs_1_), channel_id=1, source_target_pairs={{0,4},{4,0},{1,5},{5,1},{2,6},{6,2},{3,7},{7,3}} | collective-permute-start | bytes 1769480 | tf_op jit(solution)/shard_map/ppermute | solution.py:470

commit v3 on v2

--- a/solution.py
+++ b/solution.py
@@ -20,17 +20,39 @@
 NT_DIMS = (((1,), (1,)), ((), ()))
 
 
-STAT_TILE = 512
-STAT_ROWS = 256
+STAT_TILE = 1024
+STAT_ROWS = 128
 PER_BLOCK = STAT_ROWS // GROUP
-TAIL_STEP = 4
-
-
-def stats_kernel(hid_ref, gain_ref, mask_ref, tab_ref, tea_ref, x_ref, xt_ref, stat_ref,
+
+
+def stats_kernel(hid_ref, gain_ref, mask_ref, tab_ref, next_ref, tea_ref, x_ref, xt_ref, stat_ref,
                  stu_acc, tea_acc, z_even, z_odd, count_vmem, count_smem, groups, live, sem):
     step = pl.program_id(0)
     dim, tokens = hid_ref.shape
     n_groups = tokens // GROUP
+
+    def source(i):
+        return pl.ds(pl.multiple_of(jnp.minimum(groups[i], n_groups - 1) * GROUP, GROUP), GROUP)
+
+    def dest(i):
+        return pl.ds(pl.multiple_of(groups[i] * GROUP, GROUP), GROUP)
+
+    def logits(block, table, z_ref):
+        rows = jnp.concatenate([x_ref[source(block * PER_BLOCK + i), :] for i in range(PER_BLOCK)], axis=0)
+        z_ref[...] = jnp.dot(rows, table[...], preferred_element_type=F32)
+
+    def exp_sum(val):
+        val = jnp.exp2(jnp.tanh(val * INV_CAP) * CAP_LOG2E)
+        total = val[:, :128]
+        for lane in range(128, STAT_TILE, 128):
+            total = total + val[:, lane:lane + 128]
+        return total
+
+    def accumulate(block, z_ref):
+        for i in range(PER_BLOCK):
+            at = block * PER_BLOCK + i
+            tea_acc[dest(at), :] += exp_sum(tea_ref[source(at), :].astype(F32))
+            stu_acc[dest(at), :] += exp_sum(z_ref[i * GROUP:(i + 1) * GROUP, :])
 
     @pl.when(step == 0)
     def _():
@@ -63,71 +85,24 @@
             groups[n_live + i] = n_groups
             return c
 
-        lax.fori_loop(0, PER_BLOCK, pad, 0)
+        lax.fori_loop(0, 2 * PER_BLOCK, pad, 0)
         live[0] = n_live
-
-    n_live = live[0]
-    n_full = n_live // PER_BLOCK
-
-    def source(i):
-        return pl.ds(pl.multiple_of(jnp.minimum(groups[i], n_groups - 1) * GROUP, GROUP), GROUP)
-
-    def dest(i):
-        return pl.ds(pl.multiple_of(groups[i] * GROUP, GROUP), GROUP)
-
-    def logits(block, z_ref):
-        rows = jnp.concatenate([x_ref[source(block * PER_BLOCK + i), :] for i in range(PER_BLOCK)], axis=0)
-        z_ref[...] = jnp.dot(rows, tab_ref[...], preferred_element_type=F32)
-
-    def exp_sum(val):
-        val = jnp.exp2(jnp.tanh(val * INV_CAP) * CAP_LOG2E)
-        total = val[:, :128]
-        for lane in range(128, STAT_TILE, 128):
-            total = total + val[:, lane:lane + 128]
-        return total
-
-    def teacher_group(i):
-        tea_acc[dest(i), :] += exp_sum(tea_ref[source(i), :].astype(F32))
-
-    def student_group(i, z):
-        stu_acc[dest(i), :] += exp_sum(z)
-
-    def accumulate(block, z_ref):
-        for i in range(PER_BLOCK):
-            teacher_group(block * PER_BLOCK + i)
-            student_group(block * PER_BLOCK + i, z_ref[i * GROUP:(i + 1) * GROUP, :])
-
-    logits(0, z_even)
-    for i in range(PER_BLOCK):
-        teacher_group(n_full * PER_BLOCK + i)
+        logits(0, tab_ref, z_even)
+
+    more = jnp.maximum((live[0] + 2 * PER_BLOCK - 1) // (2 * PER_BLOCK) - 1, 0)
 
     def pair(p, c):
-        logits(2 * p + 1, z_odd)
+        logits(2 * p + 1, tab_ref, z_odd)
         accumulate(2 * p, z_even)
-        logits(2 * p + 2, z_even)
+        logits(2 * p + 2, tab_ref, z_even)
         accumulate(2 * p + 1, z_odd)
         return c
 
-    lax.fori_loop(0, n_full // 2, pair, 0)
-
-    def tail(z_ref):
-        def some(q, c):
-            for i in range(TAIL_STEP):
-                row = pl.multiple_of((q * TAIL_STEP + i) * GROUP, GROUP)
-                student_group(n_full * PER_BLOCK + q * TAIL_STEP + i, z_ref[pl.ds(row, GROUP), :])
-            return c
-
-        lax.fori_loop(0, (n_live - n_full * PER_BLOCK + TAIL_STEP - 1) // TAIL_STEP, some, 0)
-
-    @pl.when(n_full % 2 == 1)
-    def _():
-        logits(n_full, z_odd)
-        accumulate(n_full - 1, z_even)
-        tail(z_odd)
-
-    @pl.when(n_full % 2 == 0)
-    def _():
-        tail(z_even)
+    lax.fori_loop(0, more, pair, 0)
+    logits(2 * more + 1, tab_ref, z_odd)
+    accumulate(2 * more, z_even)
+    logits(0, next_ref, z_even)
+    accumulate(2 * more + 1, z_odd)
 
     @pl.when(step == pl.num_programs(0) - 1)
     def _():
@@ -148,6 +123,7 @@
         in_specs=[
             whole, whole, whole,
             pl.BlockSpec((dim, STAT_TILE), lambda j: (0, j)),
+            pl.BlockSpec((dim, STAT_TILE), lambda j: (0, jnp.minimum(j + 1, vocab // STAT_TILE - 1))),
             pl.BlockSpec((tokens, STAT_TILE), lambda j: (0, j)),
         ],
         out_specs=[whole, whole, whole],
@@ -160,13 +136,13 @@
             VMEM((tokens + GROUP, 128), F32), VMEM((tokens + GROUP, 128), F32),
             VMEM((STAT_ROWS, STAT_TILE), F32), VMEM((STAT_ROWS, STAT_TILE), F32),
             VMEM((16, 128), jnp.int32), pltpu.SMEM((16, 128), jnp.int32),
-            pltpu.SMEM((n_groups + 2 * PER_BLOCK,), jnp.int32), pltpu.SMEM((1,), jnp.int32),
+            pltpu.SMEM((n_groups + 4 * PER_BLOCK,), jnp.int32), pltpu.SMEM((1,), jnp.int32),
             pltpu.SemaphoreType.DMA,
         ],
         compiler_params=pltpu.CompilerParams(dimension_semantics=("arbitrary",), vmem_limit_bytes=46 * 2**20),
         cost_estimate=pl.CostEstimate(flops=50_000_000_000, bytes_accessed=70_000_000, transcendentals=0),
         name="stats",
-    )(hid_t, gain, mask, tab_t, tea)
+    )(hid_t, gain, mask, tab_t, tab_t, tea)
 
 
 def gather_kernel(n_tp, stat_ref, mask_ref, stu_col, tea_col, base_ref, slots, mask_slot, send_sem, recv_sem):

time: 745 us -> 738 us (level)
  Pallas kernels: 424 us -> 414 us
    pallas_call x1, Pallas kernels: 70.2 us -> 61.5 us  [stats(): pl.pallas_call(stats_kernel, grid=(vocab // STAT_TILE,), in_specs=[whole,...]
where the time goes in v3:
time: 738 us; the launch traced here: 736 us
  Pallas kernels  414 us (56%)
  waiting for transfers between devices  305 us (41%)
  starting transfers between devices  9.61 us (1%)
    ppermute x1, waiting for transfers between devices, step(): share_other = lax.ppermute(share, 'dp', swap)  266 us
    pallas_call x8, Pallas kernels, chunk_grad(): pl.pallas_call(functools.partial(chunk_kernel, first), grid=(size // GRAD...  190 us
    pallas_call x1, Pallas kernels, reduce_dx(): pl.pallas_call(functools.partial(dx_kernel, n_tp), in_specs=[whole, whole...  110 us
    pallas_call x1, Pallas kernels, stats(): pl.pallas_call(stats_kernel, grid=(vocab // STAT_TILE,), in_specs=[whole,...  61.5 us
    pallas_call x8, Pallas kernels, add_chunk(): pl.pallas_call(add_kernel, grid=(size // tile,), in_specs=[hbm, block, bl...  45.2 us
    ppermute x8, waiting for transfers between devices, step(): other.append(lax.ppermute(part, 'dp', swap))  39.9 us
  transfers between devices with their start and end apart: 9, of which 3 were waited for; matrix products, arithmetic and copies ran while one was open for 0% of the time, Pallas kernels for 42%

profile of v3, /device:TPU:0, one launch (start us, length us, event | category | flops | bytes accessed | tf_op | source)
XLA Modules:
  0.0 736.3 jit_solution(9965274984106805320)
XLA Ops:
  2.0 1.7 copy-done.3
  3.7 61.5 %stats.1 = (bf16[2048,576]{1,0:T(8,128)(2,1)S(1)}, bf16[576,2048]{1,0:T(8,128)(2,1)S(1)}, f32[32,128]{1,0:T(8,128)S(1)}) custom-call(bf16[576,2048]{1,0:T(8,128)(2,1)S(1)} %bitcast.9, f32[1,576]{1,0:T(1,128)S(1)} %reshape.14.gain_ref, f32[16,128]{1,0:T(8,128)S(1)} %bitcast.7, bf16[576,12288]{1,0:T(8,128)(2,1)} %bitcast.12, bf16[576,12288]{1,0:T(8,128)(2,1)} %bitcast.13, ...), custom_call_target="tpu_custom_call" | custom-call | flops 49999998976 | bytes 70000000 | tf_op jit(solution)/shard_map/stats/pallas_call | solution.py:120
  65.3 7.5 %gather_stats.1 = (f32[2048,128]{1,0:T(8,128)S(1)}, f32[2048,128]{1,0:T(8,128)S(1)}, f32[8,128]{1,0:T(8,128)S(1)}) custom-call(f32[32,128]{1,0:T(8,128)S(1)} %get-tuple-element.38.stat_ref, f32[16,128]{1,0:T(8,128)S(1)} %bitcast.8), custom_call_target="tpu_custom_call" | custom-call | flops 5000000 | bytes 2000000 | tf_op jit(solution)/shard_map/gather_stats/pallas_call | solution.py:191
  72.8 5.3 chunk_grad.8
  78.1 8.7 %chunk_grad.9 = (f32[576,512]{1,0:T(8,128)S(1)}, f32[2048,576]{1,0:T(8,128)S(1)}, f32[2048,128]{1,0:T(8,128)S(1)}) custom-call(bf16[2048,576]{1,0:T(8,128)(2,1)S(1)} %get-tuple-element.36.x_ref, bf16[576,2048]{1,0:T(8,128)(2,1)S(1)} %get-tuple-element.37.xt_ref, ...), custom_call_target="tpu_custom_call", output_to_operand_aliasing={{1}: (6, {}), {2}: (7, {})} | custom-call | flops 3623878656 | bytes 2097152 | tf_op jit(solution)/shard_map/chunk_grad/pallas_call | solution.py:281
  86.8 24.2 %chunk_grad.10 = (f32[576,1536]{1,0:T(8,128)}, f32[2048,576]{1,0:T(8,128)S(1)}, f32[2048,128]{1,0:T(8,128)S(1)}) custom-call(bf16[2048,576]{1,0:T(8,128)(2,1)S(1)} %get-tuple-element.36.x_ref, bf16[576,2048]{1,0:T(8,128)(2,1)S(1)} %get-tuple-element.37.xt_ref, ...), custom_call_target="tpu_custom_call", output_to_operand_aliasing={{1}: (6, {}), {2}: (7, {})} | custom-call | flops 10871635968 | bytes 6291456 | tf_op jit(solution)/shard_map/chunk_grad/pallas_call | solution.py:281
  111.5 53.5 %chunk_grad.11 = (f32[576,3584]{1,0:T(8,128)}, f32[2048,576]{1,0:T(8,128)S(1)}, f32[2048,128]{1,0:T(8,128)S(1)}) custom-call(bf16[2048,576]{1,0:T(8,128)(2,1)S(1)} %get-tuple-element.36.x_ref, bf16[576,2048]{1,0:T(8,128)(2,1)S(1)} %get-tuple-element.37.xt_ref, ...), custom_call_target="tpu_custom_call", output_to_operand_aliasing={{1}: (6, {}), {2}: (7, {})} | custom-call | flops 25367150592 | bytes 14680064 | tf_op jit(solution)/shard_map/chunk_grad/pallas_call | solution.py:281
  165.0 1.5 collective-permute-start.4
  166.5 53.5 %chunk_grad.12 = (f32[576,3584]{1,0:T(8,128)}, f32[2048,576]{1,0:T(8,128)S(1)}, f32[2048,128]{1,0:T(8,128)S(1)}) custom-call(bf16[2048,576]{1,0:T(8,128)(2,1)S(1)} %get-tuple-element.36.x_ref, bf16[576,2048]{1,0:T(8,128)(2,1)S(1)} %get-tuple-element.37.xt_ref, ...), custom_call_target="tpu_custom_call", output_to_operand_aliasing={{1}: (6, {}), {2}: (7, {})} | custom-call | flops 25367150592 | bytes 14680064 | tf_op jit(solution)/shard_map/chunk_grad/pallas_call | solution.py:281
  220.5 31.5 %chunk_grad.13 = (f32[576,2048]{1,0:T(8,128)}, f32[2048,576]{1,0:T(8,128)S(1)}, f32[2048,128]{1,0:T(8,128)S(1)}) custom-call(bf16[2048,576]{1,0:T(8,128)(2,1)S(1)} %get-tuple-element.36.x_ref, bf16[576,2048]{1,0:T(8,128)(2,1)S(1)} %get-tuple-element.37.xt_ref, ...), custom_call_target="tpu_custom_call", output_to_operand_aliasing={{1}: (6, {}), {2}: (7, {})} | custom-call | flops 14495514624 | bytes 8388608 | tf_op jit(solution)/shard_map/chunk_grad/pallas_call | solution.py:281
  251.9 1.5 collective-permute-start.6
  253.4 8.7 %chunk_grad.14 = (f32[576,512]{1,0:T(8,128)S(1)}, f32[2048,576]{1,0:T(8,128)S(1)}, f32[2048,128]{1,0:T(8,128)S(1)}) custom-call(bf16[2048,576]{1,0:T(8,128)(2,1)S(1)} %get-tuple-element.36.x_ref, bf16[576,2048]{1,0:T(8,128)(2,1)S(1)} %get-tuple-element.37.xt_ref, ...), custom_call_target="tpu_custom_call", output_to_operand_aliasing={{1}: (6, {}), {2}: (7, {})} | custom-call | flops 3623878656 | bytes 2097152 | tf_op jit(solution)/shard_map/chunk_grad/pallas_call | solution.py:281
  262.2 5.1 chunk_grad.15
  267.3 109.9 %reduce_dx.1 = (f32[576,2048]{1,0:T(8,128)S(1)}, f32[8,640]{1,0:T(8,128)S(1)}) custom-call(f32[2048,576]{1,0:T(8,128)S(1)} %get-tuple-element.55.dx_ref, f32[2048,128]{1,0:T(8,128)S(1)} %get-tuple-element.56.kl_ref, f32[8,128]{1,0:T(8,128)S(1)} %get-tuple-element.57.base_ref, bf16[576,2048]{1,0:T(8,128)(2,1)S(1)} %bitcast.10, f32[1,576]{1,0:T(1,128)S(1)} %copy-done.2), custom_call_target="tpu_custom_call" | custom-call | flops 49999998976 | bytes 20000000 | tf_op jit(solution)/shard_map/reduce_dx/pallas_call | solution.py:380
  377.2 2.4 collective-permute-start
  379.6 265.6 %collective-permute-done = f32[8,640]{1,0:T(8,128)S(1)} collective-permute-done((f32[8,640]{1,0:T(8,128)S(1)}, f32[8,640]{1,0:T(8,128)S(1)}, u32[]{:S(2)}, u32[]{:S(2)}) %collective-permute-start) | collective-permute-done | bytes 20512 | tf_op jit(solution)/shard_map/ppermute | solution.py:450
  645.7 14.0 %collective-permute-done.1.refs_2_ = f32[576,256]{1,0:T(8,128)S(1)} collective-permute-done((f32[576,256]{1,0:T(8,128)S(1)}, f32[576,256]{1,0:T(8,128)S(1)}, u32[]{:S(2)}, u32[]{:S(2)}) %collective-permute-start.1) | collective-permute-done | bytes 589856 | tf_op jit(solution)/shard_map/ppermute | solution.py:446
  660.3 25.8 %collective-permute-done.2.refs_2_ = f32[576,512]{1,0:T(8,128)S(1)} collective-permute-done((f32[576,512]{1,0:T(8,128)S(1)}, f32[576,512]{1,0:T(8,128)S(1)}, u32[]{:S(2)}, u32[]{:S(2)}) %collective-permute-start.2) | collective-permute-done | bytes 1179680 | tf_op jit(solution)/shard_map/ppermute | solution.py:446
  686.7 1.5 collective-permute-start.8
  688.2 1.8 convert_bitcast_fusion
  693.2 6.1 add_chunk.10.refs_0_
  699.3 13.4 %add_chunk.11.refs_0_ = f32[576,12288]{1,0:T(8,128)} custom-call(f32[576,12288]{1,0:T(8,128)} %add_chunk.10.refs_0_, f32[576,3584]{1,0:T(8,128)} %get-tuple-element.63.refs_1_, f32[576,3584]{1,0:T(8,128)} %collective-permute-done.4.refs_2_), custom_call_target="tpu_custom_call", output_to_operand_aliasing={{}: (0, {})} | custom-call | flops 2064384 | bytes 24772608 | tf_op jit(solution)/shard_map/add_chunk/pallas_call | solution.py:411
  712.8 13.4 %add_chunk.12.refs_0_ = f32[576,12288]{1,0:T(8,128)} custom-call(f32[576,12288]{1,0:T(8,128)} %add_chunk.11.refs_0_, f32[576,3584]{1,0:T(8,128)} %get-tuple-element.64.refs_1_, f32[576,3584]{1,0:T(8,128)} %collective-permute-done.5.refs_2_), custom_call_target="tpu_custom_call", output_to_operand_aliasing={{}: (0, {})} | custom-call | flops 2064384 | bytes 24772608 | tf_op jit(solution)/shard_map/add_chunk/pallas_call | solution.py:411
  726.2 8.0 %add_chunk.13.refs_0_ = f32[576,12288]{1,0:T(8,128)} custom-call(f32[576,12288]{1,0:T(8,128)} %add_chunk.12.refs_0_, f32[576,2048]{1,0:T(8,128)} %get-tuple-element.65.refs_1_, f32[576,2048]{1,0:T(8,128)} %collective-permute-done.6.refs_2_), custom_call_target="tpu_custom_call", output_to_operand_aliasing={{}: (0, {})} | custom-call | flops 1179648 | bytes 14155776 | tf_op jit(solution)/shard_map/add_chunk/pallas_call | solution.py:411
  (28 shorter events, 9.5 us)
Async XLA Ops:
  1.3 63.9 %copy-start.1 = (f32[1,576]{1,0:T(1,128)}, f32[1,576]{1,0:T(1,128)S(1)}, u32[]{:S(2)}) copy-start(f32[1,576]{1,0:T(1,128)S(1)} %reshape.14.gain_ref) | copy-start | bytes 6916
  1.3 0.7 copy-start
  2.0 1.7 copy-start.3
  111.0 575.7 %collective-permute-start.3 = (f32[576,1536]{1,0:T(8,128)}, f32[576,1536]{1,0:T(8,128)}, u32[]{:S(2)}, u32[]{:S(2)}) collective-permute-start(f32[576,1536]{1,0:T(8,128)} %get-tuple-element.62.refs_1_), channel_id=1, source_target_pairs={{0,4},{4,0},{1,5},{5,1},{2,6},{6,2},{3,7},{7,3}} | collective-permute-start | bytes 10616840 | tf_op jit(solution)/shard_map/ppermute | solution.py:446
  165.0 534.3 %collective-permute-start.4 = (f32[576,3584]{1,0:T(8,128)}, f32[576,3584]{1,0:T(8,128)}, u32[]{:S(2)}, u32[]{:S(2)}) collective-permute-start(f32[576,3584]{1,0:T(8,128)} %get-tuple-element.63.refs_1_), channel_id=1, source_target_pairs={{0,4},{4,0},{1,5},{5,1},{2,6},{6,2},{3,7},{7,3}} | collective-permute-start | bytes 24772616 | tf_op jit(solution)/shard_map/ppermute | solution.py:446
  219.9 492.8 %collective-permute-start.5 = (f32[576,3584]{1,0:T(8,128)}, f32[576,3584]{1,0:T(8,128)}, u32[]{:S(2)}, u32[]{:S(2)}) collective-permute-start(f32[576,3584]{1,0:T(8,128)} %get-tuple-element.64.refs_1_), channel_id=1, source_target_pairs={{0,4},{4,0},{1,5},{5,1},{2,6},{6,2},{3,7},{7,3}} | collective-permute-start | bytes 24772616 | tf_op jit(solution)/shard_map/ppermute | solution.py:446
  251.9 474.2 %collective-permute-start.6 = (f32[576,2048]{1,0:T(8,128)}, f32[576,2048]{1,0:T(8,128)}, u32[]{:S(2)}, u32[]{:S(2)}) collective-permute-start(f32[576,2048]{1,0:T(8,128)} %get-tuple-element.65.refs_1_), channel_id=1, source_target_pairs={{0,4},{4,0},{1,5},{5,1},{2,6},{6,2},{3,7},{7,3}} | collective-permute-start | bytes 14155784 | tf_op jit(solution)/shard_map/ppermute | solution.py:446
  262.1 5.1 copy-start.2
  262.1 5.1 copy-start.4
  377.2 268.0 %collective-permute-start = (f32[8,640]{1,0:T(8,128)S(1)}, f32[8,640]{1,0:T(8,128)S(1)}, u32[]{:S(2)}, u32[]{:S(2)}) collective-permute-start(f32[8,640]{1,0:T(8,128)S(1)} %get-tuple-element.58), channel_id=1, source_target_pairs={{0,4},{4,0},{1,5},{5,1},{2,6},{6,2},{3,7},{7,3}} | collective-permute-start | bytes 61448 | tf_op jit(solution)/shard_map/ppermute | solution.py:450
  645.2 14.6 %collective-permute-start.1 = (f32[576,256]{1,0:T(8,128)S(1)}, f32[576,256]{1,0:T(8,128)S(1)}, u32[]{:S(2)}, u32[]{:S(2)}) collective-permute-start(f32[576,256]{1,0:T(8,128)S(1)} %get-tuple-element.60.refs_1_), channel_id=1, source_target_pairs={{0,4},{4,0},{1,5},{5,1},{2,6},{6,2},{3,7},{7,3}} | collective-permute-start | bytes 1769480 | tf_op jit(solution)/shard_map/ppermute | solution.py:446
  659.8 26.4 %collective-permute-start.2 = (f32[576,512]{1,0:T(8,128)S(1)}, f32[576,512]{1,0:T(8,128)S(1)}, u32[]{:S(2)}, u32[]{:S(2)}) collective-permute-start(f32[576,512]{1,0:T(8,128)S(1)} %get-tuple-element.61.refs_1_), channel_id=1, source_target_pairs={{0,4},{4,0},{1,5},{5,1},{2,6},{6,2},{3,7},{7,3}} | collective-permute-start | bytes 3538952 | tf_op jit(solution)/shard_map/ppermute | solution.py:446
  686.1 48.0 %collective-permute-start.7 = (f32[576,512]{1,0:T(8,128)S(1)}, f32[576,512]{1,0:T(8,128)S(1)}, u32[]{:S(2)}, u32[]{:S(2)}) collective-permute-start(f32[576,512]{1,0:T(8,128)S(1)} %get-tuple-element.66.refs_1_), channel_id=1, source_target_pairs={{0,4},{4,0},{1,5},{5,1},{2,6},{6,2},{3,7},{7,3}} | collective-permute-start | bytes 3538952 | tf_op jit(solution)/shard_map/ppermute | solution.py:446
  686.7 48.7 %collective-permute-start.8 = (f32[576,256]{1,0:T(8,128)S(1)}, f32[576,256]{1,0:T(8,128)S(1)}, u32[]{:S(2)}, u32[]{:S(2)}) collective-permute-start(f32[576,256]{1,0:T(8,128)S(1)} %get-tuple-element.67.refs_1_), channel_id=1, source_target_pairs={{0,4},{4,0},{1,5},{5,1},{2,6},{6,2},{3,7},{7,3}} | collective-permute-start | bytes 1769480 | tf_op jit(solution)/shard_map/ppermute | solution.py:446

commit v4 on v3

--- a/solution.py
+++ b/solution.py
@@ -70,8 +70,9 @@
             hid = hid_ref[:, blk * 128:(blk + 1) * 128].astype(F32)
             inv_rms = lax.rsqrt(jnp.sum(hid * hid, axis=0, keepdims=True) * (1.0 / dim) + NORM_EPS)
             x_t = hid * inv_rms * gain
-            xt_ref[:, blk * 128:(blk + 1) * 128] = x_t.astype(BF16)
-            x_ref[blk * 128:(blk + 1) * 128, :] = x_t.T.astype(BF16)
+            x_t = x_t.astype(BF16)
+            xt_ref[:, blk * 128:(blk + 1) * 128] = x_t
+            x_ref[blk * 128:(blk + 1) * 128, :] = x_t.T
         copy.wait()
 
         def add_group(g, n):
@@ -145,9 +146,21 @@
     )(hid_t, gain, mask, tab_t, tab_t, tea)
 
 
-def gather_kernel(n_tp, stat_ref, mask_ref, stu_col, tea_col, base_ref, slots, mask_slot, send_sem, recv_sem):
+GRAD_TILE = 256
+GRAD_ROWS = 256
+SLICE = 16
+
+
+def head_kernel(n_tp, stat_ref, mask_ref, x_ref, xt_ref, tab_hbm, tea_hbm, stu_col, tea_col, base_ref, de_ref, kl_acc, g_ref,
+                slots, mask_slot, tab_ref, tea_ref, stu_q, tea_q, z_even, z_odd, load_sem, send_sem, recv_sem):
     tp = lax.axis_index("tp")
     dp = lax.axis_index("dp")
+    tokens = x_ref.shape[0]
+    n_blocks = tokens // GRAD_ROWS
+    load_tab = pltpu.make_async_copy(tab_hbm.at[:, 0:GRAD_TILE], tab_ref, load_sem.at[0])
+    load_tea = pltpu.make_async_copy(tea_hbm.at[:, 0:GRAD_TILE], tea_ref, load_sem.at[1])
+    load_tab.start()
+    load_tea.start()
     barrier = pltpu.get_barrier_semaphore()
     peers = [(dp, lax.rem(tp + k, n_tp)) for k in range(1, n_tp)] + [(1 - dp, tp)]
     for peer in peers:
@@ -161,6 +174,40 @@
             dst_ref=mask_slot if last else slots.at[k],
             send_sem=send_sem.at[k], recv_sem=recv_sem.at[k], device_id=peer, device_id_type=MESH))
         copies[-1].start()
+    load_tab.wait()
+    load_tea.wait()
+
+    def window(b, size=GRAD_ROWS, skip=0):
+        return pl.ds(pl.multiple_of(b * GRAD_ROWS + skip, size), size)
+
+    def logits(b, z_ref):
+        z_ref[...] = jnp.dot(x_ref[window(b), :], tab_ref[...], preferred_element_type=F32)
+
+    def factors(b, z_ref):
+        for skip in range(0, GRAD_ROWS, SLICE):
+            rows = window(b, SLICE, skip)
+            kl = 0.0
+            for lane in range(0, GRAD_TILE, 128):
+                stu = jnp.tanh(z_ref[skip:skip + SLICE, lane:lane + 128] * INV_CAP)
+                tea = jnp.tanh(tea_ref[rows, lane:lane + 128].astype(F32) * INV_CAP)
+                tea_e = jnp.exp2(tea * CAP_LOG2E)
+                slope = 1.0 - stu * stu
+                kl = kl + tea_e * (tea - stu)
+                stu_q[rows, lane:lane + 128] = jnp.exp2(stu * CAP_LOG2E) * slope
+                tea_q[rows, lane:lane + 128] = tea_e * slope
+            kl_acc[rows, :] = kl
+
+    logits(0, z_even)
+
+    def pair(p, c):
+        logits(2 * p + 1, z_odd)
+        factors(2 * p, z_even)
+        logits(lax.rem(2 * p + 2, n_blocks), z_even)
+        factors(2 * p + 1, z_odd)
+        return c
+
+    lax.fori_loop(0, n_blocks // 2, pair, 0)
+
     for copy in copies:
         copy.wait()
     parts = [stat_ref[...]] + [slots[k] for k in range(n_tp - 1)]
@@ -179,52 +226,65 @@
     base = jnp.sum(weight * (jnp.log(stu_sum) - jnp.log(tea_sum)))
     base_ref[...] = jnp.full((8, 128), base, F32)
     stu_row, tea_row = weight / stu_sum, weight / tea_sum
-    for blk in range(16):
+    for blk in range(tokens // 128):
         rows = slice(blk * 128, (blk + 1) * 128)
-        stu_col[rows, :] = jnp.broadcast_to(stu_row[blk:blk + 1, :], (128, 128)).T
-        tea_col[rows, :] = jnp.broadcast_to(tea_row[blk:blk + 1, :], (128, 128)).T
-
-
-def gather_stats(stat, mask, n_tp):
-    tokens = mask.size
+        stu_scale = jnp.broadcast_to(stu_row[blk:blk + 1, :], (128, 128)).T
+        tea_scale = jnp.broadcast_to(tea_row[blk:blk + 1, :], (128, 128)).T
+        stu_col[rows, :] = stu_scale
+        tea_col[rows, :] = tea_scale
+        kl_acc[rows, :] = kl_acc[rows, :] * tea_scale
+        for lane in range(0, GRAD_TILE, 128):
+            lanes = slice(lane, lane + 128)
+            g_ref[rows, lanes] = (stu_q[rows, lanes] * stu_scale - tea_q[rows, lanes] * tea_scale).astype(BF16)
+    de_ref[...] = jnp.dot(xt_ref[...], g_ref[...], preferred_element_type=F32)
+
+
+def head(stat, mask, x, x_t, tab_t, tea, n_tp):
+    tokens, dim = x.shape
     whole = pl.BlockSpec(memory_space=VMEM)
+    hbm = pl.BlockSpec(memory_space=pl.ANY)
     return pl.pallas_call(
-        functools.partial(gather_kernel, n_tp),
-        in_specs=[whole, whole],
-        out_specs=[whole, whole, whole],
+        functools.partial(head_kernel, n_tp),
+        in_specs=[whole, whole, whole, whole, hbm, hbm],
+        out_specs=[whole] * 6,
         out_shape=[
             jax.ShapeDtypeStruct((tokens, 128), F32),
             jax.ShapeDtypeStruct((tokens, 128), F32),
             jax.ShapeDtypeStruct((8, 128), F32),
+            jax.ShapeDtypeStruct((dim, GRAD_TILE), F32),
+            jax.ShapeDtypeStruct((tokens, 128), F32),
+            jax.ShapeDtypeStruct((tokens, GRAD_TILE), BF16),
         ],
         scratch_shapes=[
             VMEM((n_tp - 1,) + stat.shape, F32), VMEM(mask.shape, F32),
-            pltpu.SemaphoreType.DMA((n_tp,)), pltpu.SemaphoreType.DMA((n_tp,)),
-        ],
-        compiler_params=pltpu.CompilerParams(collective_id=0, has_side_effects=True, vmem_limit_bytes=8 * 2**20),
-        cost_estimate=pl.CostEstimate(flops=5_000_000, bytes_accessed=2_000_000, transcendentals=0),
-        name="gather_stats",
-    )(stat, mask)
-
-
-GRAD_TILE = 256
-GRAD_ROWS = 256
-SLICE = 16
-
-
-def chunk_kernel(first, x_ref, xt_ref, stu_col, tea_col, tab_ref, tea_ref, *refs):
+            VMEM((dim, GRAD_TILE), BF16), VMEM((tokens, GRAD_TILE), BF16),
+            VMEM((tokens, GRAD_TILE), F32), VMEM((tokens, GRAD_TILE), F32),
+            VMEM((GRAD_ROWS, GRAD_TILE), F32), VMEM((GRAD_ROWS, GRAD_TILE), F32),
+            pltpu.SemaphoreType.DMA((2,)), pltpu.SemaphoreType.DMA((n_tp,)), pltpu.SemaphoreType.DMA((n_tp,)),
+        ],
+        compiler_params=pltpu.CompilerParams(collective_id=0, has_side_effects=True, vmem_limit_bytes=40 * 2**20),
+        cost_estimate=pl.CostEstimate(flops=5_000_000_000, bytes_accessed=2_000_000, transcendentals=0),
+        name="head",
+    )(stat, mask, x, x_t, tab_t, tea)
+
+
+def chunk_kernel(first, x_ref, xt_ref, stu_col, tea_col, tab_ref, tea_ref, _, *refs):
     if first:
-        de_ref, dx_acc, kl_acc, g_ref, z_even, z_odd = refs
+        head_g, head_tab, de_ref, kl_acc, dx_acc, g_ref, z_even, z_odd = refs
     else:
-        _, _, de_ref, dx_acc, kl_acc, g_ref, z_even, z_odd = refs
+        _, de_ref, kl_acc, dx_acc, g_ref, z_even, z_odd = refs
     tokens = x_ref.shape[0]
     n_blocks = tokens // GRAD_ROWS
 
     if first:
         @pl.when(pl.program_id(0) == 0)
         def _():
-            dx_acc[...] = jnp.zeros_like(dx_acc)
-            kl_acc[...] = jnp.zeros_like(kl_acc)
+            def block(b, c):
+                rows = pl.ds(pl.multiple_of(b * GRAD_ROWS, GRAD_ROWS), GRAD_ROWS)
+                dx_acc[rows, :] = lax.dot_general(head_g[rows, :], head_tab[...], NT_DIMS, preferred_element_type=F32)
+                return c
+
+            lax.fori_loop(0, n_blocks, block, 0)
 
     def window(b, size=GRAD_ROWS, skip=0):
         return pl.ds(pl.multiple_of(b * GRAD_ROWS + skip, size), size)
@@ -272,11 +332,11 @@
     add_dx(n_blocks - 1)
 
 
-def chunk_grad(start, size, x, x_t, stu_col, tea_col, tab_t, tea, carry):
+def chunk_grad(start, size, x, x_t, stu_col, tea_col, tab_t, tea, kl, dx, head_g):
     tokens, dim = x.shape
     off = start // GRAD_TILE
     whole = pl.BlockSpec(memory_space=VMEM)
-    first = carry is None
+    first = dx is None
     work = tokens * size
     return pl.pallas_call(
         functools.partial(chunk_kernel, first),
@@ -285,21 +345,22 @@
             whole, whole, whole, whole,
             pl.BlockSpec((dim, GRAD_TILE), lambda j: (0, j + off)),
             pl.BlockSpec((tokens, GRAD_TILE), lambda j: (0, j + off)),
-        ] + ([] if first else [whole, whole]),
+            whole,
+        ] + ([whole, pl.BlockSpec((dim, GRAD_TILE), lambda j: (0, 0))] if first else [whole]),
         out_specs=[pl.BlockSpec((dim, GRAD_TILE), lambda j: (0, j)), whole, whole],
         out_shape=[
             jax.ShapeDtypeStruct((dim, size), F32),
+            jax.ShapeDtypeStruct((tokens, 128), F32),
             jax.ShapeDtypeStruct((tokens, dim), F32),
-            jax.ShapeDtypeStruct((tokens, 128), F32),
         ],
         scratch_shapes=[
             VMEM((tokens, GRAD_TILE), BF16), VMEM((GRAD_ROWS, GRAD_TILE), F32), VMEM((GRAD_ROWS, GRAD_TILE), F32),
         ],
-        input_output_aliases={} if first else {6: 1, 7: 2},
+        input_output_aliases={6: 1} if first else {6: 1, 7: 2},
         compiler_params=pltpu.CompilerParams(dimension_semantics=("arbitrary",), vmem_limit_bytes=32 * 2**20),
         cost_estimate=pl.CostEstimate(flops=work * 3 * 2 * dim, bytes_accessed=work * 2, transcendentals=0),
         name="chunk_grad",
-    )(x, x_t, stu_col, tea_col, tab_t, tea, *(() if first else carry))
+    )(x, x_t, stu_col, tea_col, tab_t, tea, kl, *((head_g, tab_t) if first else (dx,)))
 
 
 def dx_kernel(n_tp, dx_ref, kl_ref, base_ref, hid_ref, gain_ref, gh_ref, part_ref,
@@ -421,7 +482,7 @@
     )(*lead, own, other)
 
 
-CHUNKS = (256, 512, 1536, 3584, 3584, 2048, 512, 256)
+CHUNKS = (GRAD_TILE, 512, 1536, 3584, 3584, 2048, 512, 256)
 
 
 def solution(mesh):
@@ -436,17 +497,17 @@
         mask = mask_rows.reshape(tokens // 128, 128)
         gain = w_final.reshape(1, dim)
         x, x_t, stat = stats(hid_t, gain, mask, tab_t, tea_rows)
-        stu_col, tea_col, base = gather_stats(stat, mask, n_tp)
-        carry = None
+        stu_col, tea_col, base, part, kl, head_g = head(stat, mask, x, x_t, tab_t, tea_rows, n_tp)
+        dx = None
         own, other = [], []
         start = 0
-        for size in CHUNKS:
-            part, dx, kl = chunk_grad(start, size, x, x_t, stu_col, tea_col, tab_t, tea_rows, carry)
-            carry = (dx, kl)
+        for c, size in enumerate(CHUNKS):
+            if c:
+                part, kl, dx = chunk_grad(start, size, x, x_t, stu_col, tea_col, tab_t, tea_rows, kl, dx, head_g)
             other.append(lax.ppermute(part, "dp", swap))
             own.append(part)
             start += size
-        gh_t, share = reduce_dx(*carry, base, hid_t, gain, n_tp)
+        gh_t, share = reduce_dx(dx, kl, base, hid_t, gain, n_tp)
         share_other = lax.ppermute(share, "dp", swap)
         share = share + share_other
         out = None

time: 738 us -> 736 us (level)
    pallas_call x8 -> x7, Pallas kernels: 190 us -> 193 us  [chunk_grad(): pl.pallas_call(functools.partial(chunk_kernel, first), grid=(size // GRAD...]
where the time goes in v4:
time: 736 us; the launch traced here: 735 us
  Pallas kernels  418 us (57%)
  waiting for transfers between devices  300 us (41%)
  starting transfers between devices  9.54 us (1%)
    ppermute x1, waiting for transfers between devices, step(): share_other = lax.ppermute(share, 'dp', swap)  261 us
    pallas_call x7, Pallas kernels, chunk_grad(): pl.pallas_call(functools.partial(chunk_kernel, first), grid=(size // GRAD...  193 us
    pallas_call x1, Pallas kernels, reduce_dx(): pl.pallas_call(functools.partial(dx_kernel, n_tp), in_specs=[whole, whole...  111 us
    pallas_call x1, Pallas kernels, stats(): pl.pallas_call(stats_kernel, grid=(vocab // STAT_TILE,), in_specs=[whole,...  61.3 us
    pallas_call x8, Pallas kernels, add_chunk(): pl.pallas_call(add_kernel, grid=(size // tile,), in_specs=[hbm, block, bl...  45.2 us
    ppermute x8, waiting for transfers between devices, step(): other.append(lax.ppermute(part, 'dp', swap))  39.3 us
  transfers between devices with their start and end apart: 9, of which 3 were waited for; matrix products, arithmetic and copies ran while one was open for 0% of the time, Pallas kernels for 42%

profile of v4, /device:TPU:0, one launch (start us, length us, event | category | flops | bytes accessed | tf_op | source)
XLA Modules:
  0.0 734.8 jit_solution(15754256829751327294)
XLA Ops:
  2.0 1.7 copy-done.3
  3.7 61.3 %stats.1 = (bf16[2048,576]{1,0:T(8,128)(2,1)S(1)}, bf16[576,2048]{1,0:T(8,128)(2,1)S(1)}, f32[32,128]{1,0:T(8,128)S(1)}) custom-call(bf16[576,2048]{1,0:T(8,128)(2,1)S(1)} %bitcast.9, f32[1,576]{1,0:T(1,128)S(1)} %reshape.14.gain_ref, f32[16,128]{1,0:T(8,128)S(1)} %bitcast.7, bf16[576,12288]{1,0:T(8,128)(2,1)} %bitcast.12, bf16[576,12288]{1,0:T(8,128)(2,1)} %bitcast.13, ...), custom_call_target="tpu_custom_call" | custom-call | flops 49999998976 | bytes 70000000 | tf_op jit(solution)/shard_map/stats/pallas_call | solution.py:121
  65.0 8.2 %head.1 = (f32[2048,128]{1,0:T(8,128)S(1)}, f32[2048,128]{1,0:T(8,128)S(1)}, f32[8,128]{1,0:T(8,128)S(1)}, f32[576,256]{1,0:T(8,128)S(1)}, f32[2048,128]{1,0:T(8,128)S(1)}, /*index=5*/bf16[2048,256]{1,0:T(8,128)(2,1)S(1)}) custom-call(f32[32,128]{1,0:T(8,128)S(1)} %get-tuple-element.38.stat_ref, f32[16,128]{1,0:T(8,128)S(1)} %bitcast.8, ...), custom_call_target="tpu_custom_call" | custom-call | flops 5000000000 | bytes 2000000 | tf_op jit(solution)/shard_map/head/pallas_call | solution.py:246
  73.2 11.4 %chunk_grad.7 = (f32[576,512]{1,0:T(8,128)S(1)}, f32[2048,128]{1,0:T(8,128)S(1)}, f32[2048,576]{1,0:T(8,128)S(1)}) custom-call(bf16[2048,576]{1,0:T(8,128)(2,1)S(1)} %get-tuple-element.36.x_ref, bf16[576,2048]{1,0:T(8,128)(2,1)S(1)} %get-tuple-element.37.xt_ref, f32[2048,128]{1,0:T(8,128)S(1)} %get-tuple-element.39.stu_col, ...), custom_call_target="tpu_custom_call", output_to_operand_aliasing={{1}: (6, {})} | custom-call | flops 3623878656 | bytes 2097152 | tf_op jit(solution)/shard_map/chunk_grad/pallas_call | solution.py:341
  84.6 24.9 %chunk_grad.8 = (f32[576,1536]{1,0:T(8,128)}, f32[2048,128]{1,0:T(8,128)S(1)}, f32[2048,576]{1,0:T(8,128)S(1)}) custom-call(bf16[2048,576]{1,0:T(8,128)(2,1)S(1)} %get-tuple-element.36.x_ref, bf16[576,2048]{1,0:T(8,128)(2,1)S(1)} %get-tuple-element.37.xt_ref, ...), custom_call_target="tpu_custom_call", output_to_operand_aliasing={{1}: (6, {}), {2}: (7, {})} | custom-call | flops 10871635968 | bytes 6291456 | tf_op jit(solution)/shard_map/chunk_grad/pallas_call | solution.py:341
  110.3 55.2 %chunk_grad.9 = (f32[576,3584]{1,0:T(8,128)}, f32[2048,128]{1,0:T(8,128)S(1)}, f32[2048,576]{1,0:T(8,128)S(1)}) custom-call(bf16[2048,576]{1,0:T(8,128)(2,1)S(1)} %get-tuple-element.36.x_ref, bf16[576,2048]{1,0:T(8,128)(2,1)S(1)} %get-tuple-element.37.xt_ref, ...), custom_call_target="tpu_custom_call", output_to_operand_aliasing={{1}: (6, {}), {2}: (7, {})} | custom-call | flops 25367150592 | bytes 14680064 | tf_op jit(solution)/shard_map/chunk_grad/pallas_call | solution.py:341
  165.5 1.3 collective-permute-start.4
  166.8 55.1 %chunk_grad.10 = (f32[576,3584]{1,0:T(8,128)}, f32[2048,128]{1,0:T(8,128)S(1)}, f32[2048,576]{1,0:T(8,128)S(1)}) custom-call(bf16[2048,576]{1,0:T(8,128)(2,1)S(1)} %get-tuple-element.36.x_ref, bf16[576,2048]{1,0:T(8,128)(2,1)S(1)} %get-tuple-element.37.xt_ref, ...), custom_call_target="tpu_custom_call", output_to_operand_aliasing={{1}: (6, {}), {2}: (7, {})} | custom-call | flops 25367150592 | bytes 14680064 | tf_op jit(solution)/shard_map/chunk_grad/pallas_call | solution.py:341
  222.7 32.5 %chunk_grad.11 = (f32[576,2048]{1,0:T(8,128)}, f32[2048,128]{1,0:T(8,128)S(1)}, f32[2048,576]{1,0:T(8,128)S(1)}) custom-call(bf16[2048,576]{1,0:T(8,128)(2,1)S(1)} %get-tuple-element.36.x_ref, bf16[576,2048]{1,0:T(8,128)(2,1)S(1)} %get-tuple-element.37.xt_ref, ...), custom_call_target="tpu_custom_call", output_to_operand_aliasing={{1}: (6, {}), {2}: (7, {})} | custom-call | flops 14495514624 | bytes 8388608 | tf_op jit(solution)/shard_map/chunk_grad/pallas_call | solution.py:341
  255.2 1.3 collective-permute-start.6
  256.4 9.0 %chunk_grad.12 = (f32[576,512]{1,0:T(8,128)S(1)}, f32[2048,128]{1,0:T(8,128)S(1)}, f32[2048,576]{1,0:T(8,128)S(1)}) custom-call(bf16[2048,576]{1,0:T(8,128)(2,1)S(1)} %get-tuple-element.36.x_ref, bf16[576,2048]{1,0:T(8,128)(2,1)S(1)} %get-tuple-element.37.xt_ref, ...), custom_call_target="tpu_custom_call", output_to_operand_aliasing={{1}: (6, {}), {2}: (7, {})} | custom-call | flops 3623878656 | bytes 2097152 | tf_op jit(solution)/shard_map/chunk_grad/pallas_call | solution.py:341
  265.4 5.2 chunk_grad.13
  270.7 110.5 %reduce_dx.1 = (f32[576,2048]{1,0:T(8,128)S(1)}, f32[8,640]{1,0:T(8,128)S(1)}) custom-call(f32[2048,576]{1,0:T(8,128)S(1)} %get-tuple-element.55.dx_ref, f32[2048,128]{1,0:T(8,128)S(1)} %get-tuple-element.56.kl_ref, f32[8,128]{1,0:T(8,128)S(1)} %get-tuple-element.57.base_ref, bf16[576,2048]{1,0:T(8,128)(2,1)S(1)} %bitcast.10, f32[1,576]{1,0:T(1,128)S(1)} %copy-done.2), custom_call_target="tpu_custom_call" | custom-call | flops 49999998976 | bytes 20000000 | tf_op jit(solution)/shard_map/reduce_dx/pallas_call | solution.py:441
  381.2 1.7 collective-permute-start
  382.9 260.8 %collective-permute-done = f32[8,640]{1,0:T(8,128)S(1)} collective-permute-done((f32[8,640]{1,0:T(8,128)S(1)}, f32[8,640]{1,0:T(8,128)S(1)}, u32[]{:S(2)}, u32[]{:S(2)}) %collective-permute-start) | collective-permute-done | bytes 20512 | tf_op jit(solution)/shard_map/ppermute | solution.py:511
  644.6 13.8 %collective-permute-done.1.refs_2_ = f32[576,256]{1,0:T(8,128)S(1)} collective-permute-done((f32[576,256]{1,0:T(8,128)S(1)}, f32[576,256]{1,0:T(8,128)S(1)}, u32[]{:S(2)}, u32[]{:S(2)}) %collective-permute-start.1) | collective-permute-done | bytes 589856 | tf_op jit(solution)/shard_map/ppermute | solution.py:507
  659.2 25.5 %collective-permute-done.2.refs_2_ = f32[576,512]{1,0:T(8,128)S(1)} collective-permute-done((f32[576,512]{1,0:T(8,128)S(1)}, f32[576,512]{1,0:T(8,128)S(1)}, u32[]{:S(2)}, u32[]{:S(2)}) %collective-permute-start.2) | collective-permute-done | bytes 1179680 | tf_op jit(solution)/shard_map/ppermute | solution.py:507
  686.7 1.8 convert_bitcast_fusion
  690.5 1.2 add_chunk.9.refs_0_
  691.8 6.1 add_chunk.10.refs_0_
  697.9 13.4 %add_chunk.11.refs_0_ = f32[576,12288]{1,0:T(8,128)} custom-call(f32[576,12288]{1,0:T(8,128)} %add_chunk.10.refs_0_, f32[576,3584]{1,0:T(8,128)} %get-tuple-element.63.refs_1_, f32[576,3584]{1,0:T(8,128)} %collective-permute-done.4.refs_2_), custom_call_target="tpu_custom_call", output_to_operand_aliasing={{}: (0, {})} | custom-call | flops 2064384 | bytes 24772608 | tf_op jit(solution)/shard_map/add_chunk/pallas_call | solution.py:472
  711.3 13.4 %add_chunk.12.refs_0_ = f32[576,12288]{1,0:T(8,128)} custom-call(f32[576,12288]{1,0:T(8,128)} %add_chunk.11.refs_0_, f32[576,3584]{1,0:T(8,128)} %get-tuple-element.64.refs_1_, f32[576,3584]{1,0:T(8,128)} %collective-permute-done.5.refs_2_), custom_call_target="tpu_custom_call", output_to_operand_aliasing={{}: (0, {})} | custom-call | flops 2064384 | bytes 24772608 | tf_op jit(solution)/shard_map/add_chunk/pallas_call | solution.py:472
  724.7 8.0 %add_chunk.13.refs_0_ = f32[576,12288]{1,0:T(8,128)} custom-call(f32[576,12288]{1,0:T(8,128)} %add_chunk.12.refs_0_, f32[576,2048]{1,0:T(8,128)} %get-tuple-element.65.refs_1_, f32[576,2048]{1,0:T(8,128)} %collective-permute-done.6.refs_2_), custom_call_target="tpu_custom_call", output_to_operand_aliasing={{}: (0, {})} | custom-call | flops 1179648 | bytes 14155776 | tf_op jit(solution)/shard_map/add_chunk/pallas_call | solution.py:472
  732.7 1.2 add_chunk.14.refs_0_
  (27 shorter events, 9.6 us)
Async XLA Ops:
  1.3 63.7 %copy-start.1 = (f32[1,576]{1,0:T(1,128)}, f32[1,576]{1,0:T(1,128)S(1)}, u32[]{:S(2)}) copy-start(f32[1,576]{1,0:T(1,128)S(1)} %reshape.14.gain_ref) | copy-start | bytes 6916
  1.3 0.7 copy-start
  2.0 1.7 copy-start.3
  109.5 576.1 %collective-permute-start.3 = (f32[576,1536]{1,0:T(8,128)}, f32[576,1536]{1,0:T(8,128)}, u32[]{:S(2)}, u32[]{:S(2)}) collective-permute-start(f32[576,1536]{1,0:T(8,128)} %get-tuple-element.62.refs_1_), channel_id=1, source_target_pairs={{0,4},{4,0},{1,5},{5,1},{2,6},{6,2},{3,7},{7,3}} | collective-permute-start | bytes 10616840 | tf_op jit(solution)/shard_map/ppermute | solution.py:507
  165.5 532.4 %collective-permute-start.4 = (f32[576,3584]{1,0:T(8,128)}, f32[576,3584]{1,0:T(8,128)}, u32[]{:S(2)}, u32[]{:S(2)}) collective-permute-start(f32[576,3584]{1,0:T(8,128)} %get-tuple-element.63.refs_1_), channel_id=1, source_target_pairs={{0,4},{4,0},{1,5},{5,1},{2,6},{6,2},{3,7},{7,3}} | collective-permute-start | bytes 24772616 | tf_op jit(solution)/shard_map/ppermute | solution.py:507
  221.9 489.4 %collective-permute-start.5 = (f32[576,3584]{1,0:T(8,128)}, f32[576,3584]{1,0:T(8,128)}, u32[]{:S(2)}, u32[]{:S(2)}) collective-permute-start(f32[576,3584]{1,0:T(8,128)} %get-tuple-element.64.refs_1_), channel_id=1, source_target_pairs={{0,4},{4,0},{1,5},{5,1},{2,6},{6,2},{3,7},{7,3}} | collective-permute-start | bytes 24772616 | tf_op jit(solution)/shard_map/ppermute | solution.py:507
  255.2 469.6 %collective-permute-start.6 = (f32[576,2048]{1,0:T(8,128)}, f32[576,2048]{1,0:T(8,128)}, u32[]{:S(2)}, u32[]{:S(2)}) collective-permute-start(f32[576,2048]{1,0:T(8,128)} %get-tuple-element.65.refs_1_), channel_id=1, source_target_pairs={{0,4},{4,0},{1,5},{5,1},{2,6},{6,2},{3,7},{7,3}} | collective-permute-start | bytes 14155784 | tf_op jit(solution)/shard_map/ppermute | solution.py:507
  265.4 5.2 copy-start.2
  265.4 5.2 copy-start.4
  381.2 262.5 %collective-permute-start = (f32[8,640]{1,0:T(8,128)S(1)}, f32[8,640]{1,0:T(8,128)S(1)}, u32[]{:S(2)}, u32[]{:S(2)}) collective-permute-start(f32[8,640]{1,0:T(8,128)S(1)} %get-tuple-element.58), channel_id=1, source_target_pairs={{0,4},{4,0},{1,5},{5,1},{2,6},{6,2},{3,7},{7,3}} | collective-permute-start | bytes 61448 | tf_op jit(solution)/shard_map/ppermute | solution.py:511
  643.7 14.6 %collective-permute-start.1 = (f32[576,256]{1,0:T(8,128)S(1)}, f32[576,256]{1,0:T(8,128)S(1)}, u32[]{:S(2)}, u32[]{:S(2)}) collective-permute-start(f32[576,256]{1,0:T(8,128)S(1)} %get-tuple-element.60.refs_1_), channel_id=1, source_target_pairs={{0,4},{4,0},{1,5},{5,1},{2,6},{6,2},{3,7},{7,3}} | collective-permute-start | bytes 1769480 | tf_op jit(solution)/shard_map/ppermute | solution.py:507
  658.3 26.4 %collective-permute-start.2 = (f32[576,512]{1,0:T(8,128)S(1)}, f32[576,512]{1,0:T(8,128)S(1)}, u32[]{:S(2)}, u32[]{:S(2)}) collective-permute-start(f32[576,512]{1,0:T(8,128)S(1)} %get-tuple-element.61.refs_1_), channel_id=1, source_target_pairs={{0,4},{4,0},{1,5},{5,1},{2,6},{6,2},{3,7},{7,3}} | collective-permute-start | bytes 3538952 | tf_op jit(solution)/shard_map/ppermute | solution.py:507
  684.7 48.0 %collective-permute-start.7 = (f32[576,512]{1,0:T(8,128)S(1)}, f32[576,512]{1,0:T(8,128)S(1)}, u32[]{:S(2)}, u32[]{:S(2)}) collective-permute-start(f32[576,512]{1,0:T(8,128)S(1)} %get-tuple-element.66.refs_1_), channel_id=1, source_target_pairs={{0,4},{4,0},{1,5},{5,1},{2,6},{6,2},{3,7},{7,3}} | collective-permute-start | bytes 3538952 | tf_op jit(solution)/shard_map/ppermute | solution.py:507
  685.6 48.4 %collective-permute-start.8 = (f32[576,256]{1,0:T(8,128)S(1)}, f32[576,256]{1,0:T(8,128)S(1)}, u32[]{:S(2)}, u32[]{:S(2)}) collective-permute-start(f32[576,256]{1,0:T(8,128)S(1)} %get-tuple-element.67.refs_1_), channel_id=1, source_target_pairs={{0,4},{4,0},{1,5},{5,1},{2,6},{6,2},{3,7},{7,3}} | collective-permute-start | bytes 1769480 | tf_op jit(solution)/shard_map/ppermute | solution.py:507

commit v5 on v4

--- a/solution.py
+++ b/solution.py
@@ -20,6 +20,120 @@
 NT_DIMS = (((1,), (1,)), ((), ()))
 
 
+SHARED = 256
+
+
+def lift_kernel(hid_hbm, tea_hbm, hid_ref, hid_out, tea_out, tea_ref, sem):
+    tp = lax.axis_index("tp")
+    width = hid_out.shape[1]
+    start = tea_hbm.shape[1] - SHARED
+    loads = [
+        pltpu.make_async_copy(hid_hbm, hid_ref, sem.at[0]),
+        pltpu.make_async_copy(tea_hbm.at[:, start:start + SHARED], tea_ref, sem.at[1]),
+    ]
+    for load in loads:
+        load.start()
+    loads[0].wait()
+    hid_out[...] = hid_ref[:, pl.ds(pl.multiple_of(tp * width, width), width)].astype(F32)
+    loads[1].wait()
+    tea_out[...] = tea_ref[...].astype(F32)
+
+
+def lift(hid_t, tea, n_tp):
+    dim, tokens = hid_t.shape
+    hbm = pl.BlockSpec(memory_space=pl.ANY)
+    whole = pl.BlockSpec(memory_space=VMEM)
+    return pl.pallas_call(
+        lift_kernel,
+        in_specs=[hbm, hbm],
+        out_specs=[whole, whole, whole],
+        out_shape=[
+            jax.ShapeDtypeStruct((dim, tokens), BF16),
+            jax.ShapeDtypeStruct((dim, tokens // n_tp), F32),
+            jax.ShapeDtypeStruct((tokens, SHARED), F32),
+        ],
+        scratch_shapes=[VMEM((tokens, SHARED), BF16), pltpu.SemaphoreType.DMA((2,))],
+        compiler_params=pltpu.CompilerParams(vmem_limit_bytes=48 * 2**20),
+        cost_estimate=pl.CostEstimate(flops=3_000_000, bytes_accessed=5_000_000, transcendentals=0),
+        name="lift",
+    )(hid_t, tea)
+
+
+def join_kernel(n_tp, *refs):
+    out_ref = refs[-1]
+    tp = lax.axis_index("tp")
+    width = refs[0].shape[1]
+    for k, ref in enumerate(refs[:-1]):
+        owner = lax.rem(tp - k + n_tp, n_tp)
+        out_ref[:, pl.ds(pl.multiple_of(owner * width, width), width)] = ref[...].astype(BF16)
+
+
+def join(parts, n_tp):
+    dim, width = parts[0].shape
+    whole = pl.BlockSpec(memory_space=VMEM)
+    return pl.pallas_call(
+        functools.partial(join_kernel, n_tp),
+        in_specs=[whole] * n_tp,
+        out_specs=whole,
+        out_shape=jax.ShapeDtypeStruct((dim, width * n_tp), BF16),
+        compiler_params=pltpu.CompilerParams(vmem_limit_bytes=16 * 2**20),
+        cost_estimate=pl.CostEstimate(flops=3_000_000, bytes_accessed=5_000_000, transcendentals=0),
+        name="join",
+    )(*parts)
+
+
+def make_x(hid_ref, gain_ref, x_ref, xt_ref):
+    dim, tokens = hid_ref.shape
+    gain = jnp.broadcast_to(1.0 + gain_ref[...], (128, gain_ref.shape[1])).T[:dim, :]
+    for blk in range(tokens // 128):
+        hid = hid_ref[:, blk * 128:(blk + 1) * 128].astype(F32)
+        inv_rms = lax.rsqrt(jnp.sum(hid * hid, axis=0, keepdims=True) * (1.0 / dim) + NORM_EPS)
+        x_t = (hid * inv_rms * gain).astype(BF16)
+        xt_ref[:, blk * 128:(blk + 1) * 128] = x_t
+        x_ref[blk * 128:(blk + 1) * 128, :] = x_t.T
+
+
+def shared_kernel(hid_ref, gain_ref, row_ref, tab_ref, tea_ref, de_ref, x_ref, xt_ref, g_ref):
+    tokens = x_ref.shape[0]
+    make_x(hid_ref, gain_ref, x_ref, xt_ref)
+    for blk in range(tokens // 128):
+        rows = slice(blk * 128, (blk + 1) * 128)
+        stu_scale = jnp.broadcast_to(row_ref[blk:blk + 1, :], (128, 128)).T
+        tea_scale = jnp.broadcast_to(row_ref[16 + blk:17 + blk, :], (128, 128)).T
+        z = jnp.dot(x_ref[rows, :], tab_ref[...], preferred_element_type=F32)
+        for lane in range(0, SHARED, 128):
+            lanes = slice(lane, lane + 128)
+            stu = jnp.tanh(z[:, lanes] * INV_CAP)
+            tea = jnp.tanh(tea_ref[rows, lanes] * INV_CAP)
+            stu_p = jnp.exp2(stu * CAP_LOG2E) * stu_scale
+            tea_p = jnp.exp2(tea * CAP_LOG2E) * tea_scale
+            g_ref[rows, lanes] = ((stu_p - tea_p) * (1.0 - stu * stu)).astype(BF16)
+    de_ref[...] = jnp.dot(xt_ref[...], g_ref[...], preferred_element_type=F32)
+
+
+def shared_grad(hid_t, gain, scale_rows, tab_t, tea):
+    dim, tokens = hid_t.shape
+    last = tab_t.shape[1] // SHARED - 1
+
+    def spec(shape):
+        return pl.BlockSpec(shape, lambda j: (0, 0))
+
+    return pl.pallas_call(
+        shared_kernel,
+        grid=(1,),
+        in_specs=[
+            spec(hid_t.shape), spec(gain.shape), spec(scale_rows.shape),
+            pl.BlockSpec((dim, SHARED), lambda j: (0, last)), spec(tea.shape),
+        ],
+        out_specs=spec((dim, SHARED)),
+        out_shape=jax.ShapeDtypeStruct((dim, SHARED), F32),
+        scratch_shapes=[VMEM((tokens, dim), BF16), VMEM((dim, tokens), BF16), VMEM((tokens, SHARED), BF16)],
+        compiler_params=pltpu.CompilerParams(dimension_semantics=("arbitrary",), vmem_limit_bytes=40 * 2**20),
+        cost_estimate=pl.CostEstimate(flops=tokens * SHARED * 4 * dim, bytes_accessed=tokens * SHARED * 4, transcendentals=0),
+        name="shared_grad",
+    )(hid_t, gain, scale_rows, tab_t, tea)
+
+
 STAT_TILE = 1024
 STAT_ROWS = 128
 PER_BLOCK = STAT_ROWS // GROUP
@@ -28,7 +142,7 @@
 def stats_kernel(hid_ref, gain_ref, mask_ref, tab_ref, next_ref, tea_ref, x_ref, xt_ref, stat_ref,
                  stu_acc, tea_acc, z_even, z_odd, count_vmem, count_smem, groups, live, sem):
     step = pl.program_id(0)
-    dim, tokens = hid_ref.shape
+    _, tokens = hid_ref.shape
     n_groups = tokens // GROUP
 
     def source(i):
@@ -65,14 +179,7 @@
         count_vmem[...] = counts.astype(jnp.int32)
         copy = pltpu.make_async_copy(count_vmem, count_smem, sem)
         copy.start()
-        gain = jnp.broadcast_to(1.0 + gain_ref[...], (128, gain_ref.shape[1])).T[:dim, :]
-        for blk in range(tokens // 128):
-            hid = hid_ref[:, blk * 128:(blk + 1) * 128].astype(F32)
-            inv_rms = lax.rsqrt(jnp.sum(hid * hid, axis=0, keepdims=True) * (1.0 / dim) + NORM_EPS)
-            x_t = hid * inv_rms * gain
-            x_t = x_t.astype(BF16)
-            xt_ref[:, blk * 128:(blk + 1) * 128] = x_t
-            x_ref[blk * 128:(blk + 1) * 128, :] = x_t.T
+        make_x(hid_ref, gain_ref, x_ref, xt_ref)
         copy.wait()
 
         def add_group(g, n):
@@ -90,7 +197,8 @@
         live[0] = n_live
         logits(0, tab_ref, z_even)
 
-    more = jnp.maximum((live[0] + 2 * PER_BLOCK - 1) // (2 * PER_BLOCK) - 1, 0)
+    n_blocks = jnp.maximum((live[0] + PER_BLOCK - 1) // PER_BLOCK, 1)
+    more = (n_blocks - 1) // 2
 
     def pair(p, c):
         logits(2 * p + 1, tab_ref, z_odd)
@@ -100,10 +208,19 @@
         return c
 
     lax.fori_loop(0, more, pair, 0)
-    logits(2 * more + 1, tab_ref, z_odd)
-    accumulate(2 * more, z_even)
-    logits(0, next_ref, z_even)
-    accumulate(2 * more + 1, z_odd)
+
+    @pl.when(n_blocks % 2 == 0)
+    def _():
+        logits(2 * more + 1, tab_ref, z_odd)
+        accumulate(2 * more, z_even)
+        logits(0, next_ref, z_even)
+        accumulate(2 * more + 1, z_odd)
+
+    @pl.when(n_blocks % 2 == 1)
+    def _():
+        logits(0, next_ref, z_odd)
+        accumulate(2 * more, z_even)
+        z_even[...] = z_odd[...]
 
     @pl.when(step == pl.num_programs(0) - 1)
     def _():
@@ -151,7 +268,7 @@
 SLICE = 16
 
 
-def head_kernel(n_tp, stat_ref, mask_ref, x_ref, xt_ref, tab_hbm, tea_hbm, stu_col, tea_col, base_ref, de_ref, kl_acc, g_ref,
+def head_kernel(n_tp, stat_ref, mask_ref, x_ref, xt_ref, tab_hbm, tea_hbm, stu_col, tea_col, base_ref, row_ref, de_ref, kl_acc, g_ref,
                 slots, mask_slot, tab_ref, tea_ref, stu_q, tea_q, z_even, z_odd, load_sem, send_sem, recv_sem):
     tp = lax.axis_index("tp")
     dp = lax.axis_index("dp")
@@ -226,6 +343,8 @@
     base = jnp.sum(weight * (jnp.log(stu_sum) - jnp.log(tea_sum)))
     base_ref[...] = jnp.full((8, 128), base, F32)
     stu_row, tea_row = weight / stu_sum, weight / tea_sum
+    row_ref[:16, :] = stu_row
+    row_ref[16:, :] = tea_row
     for blk in range(tokens // 128):
         rows = slice(blk * 128, (blk + 1) * 128)
         stu_scale = jnp.broadcast_to(stu_row[blk:blk + 1, :], (128, 128)).T
@@ -246,11 +365,12 @@
     return pl.pallas_call(
         functools.partial(head_kernel, n_tp),
         in_specs=[whole, whole, whole, whole, hbm, hbm],
-        out_specs=[whole] * 6,
+        out_specs=[whole] * 7,
         out_shape=[
             jax.ShapeDtypeStruct((tokens, 128), F32),
             jax.ShapeDtypeStruct((tokens, 128), F32),
             jax.ShapeDtypeStruct((8, 128), F32),
+            jax.ShapeDtypeStruct((32, 128), F32),
             jax.ShapeDtypeStruct((dim, GRAD_TILE), F32),
             jax.ShapeDtypeStruct((tokens, 128), F32),
             jax.ShapeDtypeStruct((tokens, GRAD_TILE), BF16),
@@ -482,7 +602,7 @@
     )(*lead, own, other)
 
 
-CHUNKS = (GRAD_TILE, 512, 1536, 3584, 3584, 2048, 512, 256)
+CHUNKS = (GRAD_TILE, 512, 1536, 3584, 3584, 2048, 256, 256)
 
 
 def solution(mesh):
@@ -496,8 +616,11 @@
         tab_t = tab_rows.T
         mask = mask_rows.reshape(tokens // 128, 128)
         gain = w_final.reshape(1, dim)
-        x, x_t, stat = stats(hid_t, gain, mask, tab_t, tea_rows)
-        stu_col, tea_col, base, part, kl, head_g = head(stat, mask, x, x_t, tab_t, tea_rows, n_tp)
+        hid_v, hid_own, tea_own = lift(hid_t, tea_rows, n_tp)
+        hid_part = lax.ppermute(hid_own, "dp", swap)
+        tea_other = lax.ppermute(tea_own, "dp", swap)
+        x, x_t, stat = stats(hid_v, gain, mask, tab_t, tea_rows)
+        stu_col, tea_col, base, scale_rows, part, kl, head_g = head(stat, mask, x, x_t, tab_t, tea_rows, n_tp)
         dx = None
         own, other = [], []
         start = 0
@@ -507,10 +630,18 @@
             other.append(lax.ppermute(part, "dp", swap))
             own.append(part)
             start += size
+        _, kl, dx = chunk_grad(start, SHARED, x, x_t, stu_col, tea_col, tab_t, tea_rows, kl, dx, head_g)
+        rows_other = lax.ppermute(scale_rows, "dp", swap)
+        parts = [hid_part]
+        for k in range(1, n_tp):
+            parts.append(lax.ppermute(hid_part, "tp", [(i, (i + k) % n_tp) for i in range(n_tp)]))
         gh_t, share = reduce_dx(dx, kl, base, hid_t, gain, n_tp)
         share_other = lax.ppermute(share, "dp", swap)
         share = share + share_other
-        out = None
+        hid_other = join(parts, n_tp)
+        term_own = shared_grad(hid_t, gain, scale_rows, tab_t, tea_own)
+        term_other = shared_grad(hid_other, gain, rows_other, tab_t, tea_other)
+        out = add_chunk(start, SHARED, vocab, term_own, term_other, None, gh_t)
         start = 0
         for size, a, b in zip(CHUNKS, own, other):
             out = add_chunk(start, size, vocab, a, b, out, gh_t)

time: 736 us -> 821 us (1.12)
  waiting for transfers between devices: 300 us -> 363 us
  local copies, waits for them, and re-layouts: 4.19 us -> 14.2 us
    ppermute x1, waiting for transfers between devices: 261 us -> 142 us  [step(): share_other = lax.ppermute(share, 'dp', swap)]
    ppermute x8, waiting for transfers between devices: 39.3 us -> 140 us  [step(): other.append(lax.ppermute(part, 'dp', swap))]
    ppermute x0 -> x6, waiting for transfers between devices: none -> 80.8 us  [the longest x3 54 us: step(): lax.ppermute(hid_part, 'tp', [(i, (i + k) % n_tp) for i in range(n_tp)])]
    pallas_call x0 -> x4, Pallas kernels: none -> 14.1 us  [the longest x2 10.5 us: shared_grad(): pl.pallas_call(shared_kernel, grid=(1,), in_specs=[spec(hid_t.shape), spe...]
    unnamed x10 -> x42, local copies, waits for them, and re-layouts: 2.38 us -> 12.4 us
    pallas_call x7 -> x8, Pallas kernels: 193 us -> 189 us  [chunk_grad(): pl.pallas_call(functools.partial(chunk_kernel, first), grid=(size // GRAD...]
    pallas_call x8 -> x9, Pallas kernels: 45.2 us -> 42.6 us  [add_chunk(): pl.pallas_call(add_kernel, grid=(size // tile,), in_specs=[hbm, block, bl...]
  transfers between devices with their start and end apart: 9 -> 15, of which waited for: 3 -> 7; matrix products, arithmetic and copies ran while one was open for 0% -> 0% of each run, Pallas kernels for 42% -> 43%
where the time goes in v5:
time: 821 us; the launch traced here: 820 us
  Pallas kernels  426 us (52%)
  waiting for transfers between devices  363 us (44%)
  local copies, waits for them, and re-layouts  14.2 us (2%)
  starting transfers between devices  13.6 us (2%)
    pallas_call x8, Pallas kernels, chunk_grad(): pl.pallas_call(functools.partial(chunk_kernel, first), grid=(size // GRAD...  189 us
    ppermute x1, waiting for transfers between devices, step(): share_other = lax.ppermute(share, 'dp', swap)  142 us
    ppermute x8, waiting for transfers between devices, step(): other.append(lax.ppermute(part, 'dp', swap))  140 us
    pallas_call x1, Pallas kernels, reduce_dx(): pl.pallas_call(functools.partial(dx_kernel, n_tp), in_specs=[whole, whole...  110 us
    pallas_call x1, Pallas kernels, stats(): pl.pallas_call(stats_kernel, grid=(vocab // STAT_TILE,), in_specs=[whole,...  62 us
    ppermute x3, waiting for transfers between devices, step(): lax.ppermute(hid_part, 'tp', [(i, (i + k) % n_tp) for i in range(n_tp)])  54 us
    pallas_call x9, Pallas kernels, add_chunk(): pl.pallas_call(add_kernel, grid=(size // tile,), in_specs=[hbm, block, bl...  42.6 us
    ppermute x1, waiting for transfers between devices, step(): hid_part = lax.ppermute(hid_own, 'dp', swap)  26.8 us
  transfers between devices with their start and end apart: 15, of which 7 were waited for; matrix products, arithmetic and copies ran while one was open for 0% of the time, Pallas kernels for 43%

profile of v5, /device:TPU:0, one launch (start us, length us, event | category | flops | bytes accessed | tf_op | source)
XLA Modules:
  0.0 819.7 jit_solution(4265208130577037575)
XLA Ops:
  1.3 3.4 lift.1
  4.8 62.0 %stats.1 = (bf16[2048,576]{1,0:T(8,128)(2,1)S(1)}, bf16[576,2048]{1,0:T(8,128)(2,1)S(1)}, f32[32,128]{1,0:T(8,128)S(1)}) custom-call(bf16[576,2048]{1,0:T(8,128)(2,1)S(1)} %get-tuple-element.42.hid_ref, f32[1,576]{1,0:T(1,128)S(1)} %reshape.14.gain_ref, f32[16,128]{1,0:T(8,128)S(1)} %bitcast.10, bf16[576,12288]{1,0:T(8,128)(2,1)} %bitcast.13, ...), custom_call_target="tpu_custom_call" | custom-call | flops 49999998976 | bytes 70000000 | tf_op jit(solution)/shard_map/stats/pallas_call | solution.py:238
  66.8 8.1 head.1
  78.2 11.1 %chunk_grad.8 = (f32[576,512]{1,0:T(8,128)S(1)}, f32[2048,128]{1,0:T(8,128)S(1)}, f32[2048,576]{1,0:T(8,128)S(1)}) custom-call(bf16[2048,576]{1,0:T(8,128)(2,1)S(1)} %get-tuple-element.43.x_ref, bf16[576,2048]{1,0:T(8,128)(2,1)S(1)} %get-tuple-element.44.xt_ref, f32[2048,128]{1,0:T(8,128)S(1)} %get-tuple-element.46.stu_col, ...), custom_call_target="tpu_custom_call", output_to_operand_aliasing={{1}: (6, {})} | custom-call | flops 3623878656 | bytes 2097152 | tf_op jit(solution)/shard_map/chunk_grad/pallas_call | solution.py:461
  89.3 23.6 %chunk_grad.9 = (f32[576,1536]{1,0:T(8,128)S(1)}, f32[2048,128]{1,0:T(8,128)S(1)}, f32[2048,576]{1,0:T(8,128)S(1)}) custom-call(bf16[2048,576]{1,0:T(8,128)(2,1)S(1)} %get-tuple-element.43.x_ref, bf16[576,2048]{1,0:T(8,128)(2,1)S(1)} %get-tuple-element.44.xt_ref, ...), custom_call_target="tpu_custom_call", output_to_operand_aliasing={{1}: (6, {}), {2}: (7, {})} | custom-call | flops 10871635968 | bytes 6291456 | tf_op jit(solution)/shard_map/chunk_grad/pallas_call | solution.py:461
  113.0 53.9 %chunk_grad.10 = (f32[576,3584]{1,0:T(8,128)}, f32[2048,128]{1,0:T(8,128)S(1)}, f32[2048,576]{1,0:T(8,128)S(1)}) custom-call(bf16[2048,576]{1,0:T(8,128)(2,1)S(1)} %get-tuple-element.43.x_ref, bf16[576,2048]{1,0:T(8,128)(2,1)S(1)} %get-tuple-element.44.xt_ref, ...), custom_call_target="tpu_custom_call", output_to_operand_aliasing={{1}: (6, {}), {2}: (7, {})} | custom-call | flops 25367150592 | bytes 14680064 | tf_op jit(solution)/shard_map/chunk_grad/pallas_call | solution.py:461
  167.7 52.9 %chunk_grad.11 = (f32[576,3584]{1,0:T(8,128)}, f32[2048,128]{1,0:T(8,128)S(1)}, f32[2048,576]{1,0:T(8,128)S(1)}) custom-call(bf16[2048,576]{1,0:T(8,128)(2,1)S(1)} %get-tuple-element.43.x_ref, bf16[576,2048]{1,0:T(8,128)(2,1)S(1)} %get-tuple-element.44.xt_ref, ...), custom_call_target="tpu_custom_call", output_to_operand_aliasing={{1}: (6, {}), {2}: (7, {})} | custom-call | flops 25367150592 | bytes 14680064 | tf_op jit(solution)/shard_map/chunk_grad/pallas_call | solution.py:461
  221.7 30.5 %chunk_grad.12 = (f32[576,2048]{1,0:T(8,128)S(1)}, f32[2048,128]{1,0:T(8,128)S(1)}, f32[2048,576]{1,0:T(8,128)S(1)}) custom-call(bf16[2048,576]{1,0:T(8,128)(2,1)S(1)} %get-tuple-element.43.x_ref, bf16[576,2048]{1,0:T(8,128)(2,1)S(1)} %get-tuple-element.44.xt_ref, ...), custom_call_target="tpu_custom_call", output_to_operand_aliasing={{1}: (6, {}), {2}: (7, {})} | custom-call | flops 14495514624 | bytes 8388608 | tf_op jit(solution)/shard_map/chunk_grad/pallas_call | solution.py:461
  252.2 4.9 chunk_grad.13
  257.2 5.7 chunk_grad.14
  262.9 6.1 chunk_grad.15
  269.0 110.4 %reduce_dx.1 = (f32[576,2048]{1,0:T(8,128)S(1)}, f32[8,640]{1,0:T(8,128)S(1)}) custom-call(f32[2048,576]{1,0:T(8,128)S(1)} %get-tuple-element.64.dx_ref, f32[2048,128]{1,0:T(8,128)S(1)} %get-tuple-element.65.kl_ref, f32[8,128]{1,0:T(8,128)S(1)} %get-tuple-element.66.base_ref, bf16[576,2048]{1,0:T(8,128)(2,1)S(1)} %bitcast.8, f32[1,576]{1,0:T(1,128)S(1)} %copy-done.16), custom_call_target="tpu_custom_call" | custom-call | flops 49999998976 | bytes 20000000 | tf_op jit(solution)/shard_map/reduce_dx/pallas_call | solution.py:561
  381.2 142.1 %collective-permute-done = f32[8,640]{1,0:T(8,128)S(1)} collective-permute-done((f32[8,640]{1,0:T(8,128)S(1)}, f32[8,640]{1,0:T(8,128)S(1)}, u32[]{:S(2)}, u32[]{:S(2)}) %collective-permute-start) | collective-permute-done | bytes 20512 | tf_op jit(solution)/shard_map/ppermute | solution.py:639
  525.3 26.8 %collective-permute-done.1.refs_0_ = f32[576,512]{1,0:T(8,128)S(1)} collective-permute-done((f32[576,512]{1,0:T(8,128)S(1)}, f32[576,512]{1,0:T(8,128)S(1)}, u32[]{:S(2)}, u32[]{:S(2)}) %collective-permute-start.1) | collective-permute-done | bytes 1179680 | tf_op jit(solution)/shard_map/ppermute | solution.py:620
  552.9 24.5 %collective-permute-done.8.refs_2_ = f32[576,512]{1,0:T(8,128)S(1)} collective-permute-done((f32[576,512]{1,0:T(8,128)S(1)}, f32[576,512]{1,0:T(8,128)S(1)}, u32[]{:S(2)}, u32[]{:S(2)}) %collective-permute-start.8) | collective-permute-done | bytes 1179680 | tf_op jit(solution)/shard_map/ppermute | solution.py:630
  579.3 14.8 %collective-permute-done.2.refs_1_ = f32[576,512]{1,0:T(8,128)S(1)} collective-permute-done((f32[576,512]{1,0:T(8,128)S(1)}, f32[576,512]{1,0:T(8,128)S(1)}, u32[]{:S(2)}, u32[]{:S(2)}) %collective-permute-start.2) | collective-permute-done | bytes 1179680 | tf_op jit(solution)/shard_map/ppermute | solution.py:637
  595.4 25.5 %collective-permute-done.3.refs_2_ = f32[576,512]{1,0:T(8,128)S(1)} collective-permute-done((f32[576,512]{1,0:T(8,128)S(1)}, f32[576,512]{1,0:T(8,128)S(1)}, u32[]{:S(2)}, u32[]{:S(2)}) %collective-permute-start.3) | collective-permute-done | bytes 1179680 | tf_op jit(solution)/shard_map/ppermute | solution.py:637
  621.9 13.7 %collective-permute-done.4.refs_3_ = f32[576,512]{1,0:T(8,128)S(1)} collective-permute-done((f32[576,512]{1,0:T(8,128)S(1)}, f32[576,512]{1,0:T(8,128)S(1)}, u32[]{:S(2)}, u32[]{:S(2)}) %collective-permute-start.4) | collective-permute-done | bytes 1179680 | tf_op jit(solution)/shard_map/ppermute | solution.py:637
  638.3 116.0 %collective-permute-done.9.refs_2_ = f32[576,1536]{1,0:T(8,128)S(1)} collective-permute-done((f32[576,1536]{1,0:T(8,128)S(1)}, f32[576,1536]{1,0:T(8,128)S(1)}, u32[]{:S(2)}, u32[]{:S(2)}) %collective-permute-start.9) | collective-permute-done | bytes 3538976 | tf_op jit(solution)/shard_map/ppermute | solution.py:630
  758.7 5.2 shared_grad.2.refs_1_
  768.4 5.3 shared_grad.3.refs_2_
  784.7 13.4 %add_chunk.13.refs_0_ = f32[576,12288]{1,0:T(8,128)} custom-call(f32[576,12288]{1,0:T(8,128)} %add_chunk.12.refs_0_, f32[576,3584]{1,0:T(8,128)} %get-tuple-element.75.refs_1_, f32[576,3584]{1,0:T(8,128)} %collective-permute-done.10.refs_2_), custom_call_target="tpu_custom_call", output_to_operand_aliasing={{}: (0, {})} | custom-call | flops 2064384 | bytes 24772608 | tf_op jit(solution)/shard_map/add_chunk/pallas_call | solution.py:592
  798.1 13.4 %add_chunk.14.refs_0_ = f32[576,12288]{1,0:T(8,128)} custom-call(f32[576,12288]{1,0:T(8,128)} %add_chunk.13.refs_0_, f32[576,3584]{1,0:T(8,128)} %get-tuple-element.76.refs_1_, f32[576,3584]{1,0:T(8,128)} %collective-permute-done.11.refs_2_), custom_call_target="tpu_custom_call", output_to_operand_aliasing={{}: (0, {})} | custom-call | flops 2064384 | bytes 24772608 | tf_op jit(solution)/shard_map/add_chunk/pallas_call | solution.py:592
  811.5 4.2 add_chunk.15.refs_0_
  (77 shorter events, 41.4 us)
Async XLA Ops:
  1.3 3.4 copy-start.15
  1.3 3.5 copy-start.18
  4.8 62.0 %copy-start.19 = (f32[576,512]{1,0:T(8,128)}, f32[576,512]{1,0:T(8,128)S(1)}, u32[]{:S(2)}) copy-start(f32[576,512]{1,0:T(8,128)S(1)} %get-tuple-element.71) | copy-start | bytes 3538948
  74.9 304.5 %collective-permute-start.5 = (f32[32,128]{1,0:T(8,128)}, f32[32,128]{1,0:T(8,128)}, u32[]{:S(2)}, u32[]{:S(2)}) collective-permute-start(f32[32,128]{1,0:T(8,128)} %get-tuple-element.69.row_ref), channel_id=1, source_target_pairs={{0,4},{4,0},{1,5},{5,1},{2,6},{6,2},{3,7},{7,3}} | collective-permute-start | bytes 49160 | tf_op jit(solution)/shard_map/ppermute | solution.py:634
  76.2 502.3 %collective-permute-start.6 = (f32[2048,256]{1,0:T(8,128)}, f32[2048,256]{1,0:T(8,128)}, u32[]{:S(2)}, u32[]{:S(2)}) collective-permute-start(f32[2048,256]{1,0:T(8,128)} %get-tuple-element.70.tea_ref), channel_id=1, source_target_pairs={{0,4},{4,0},{1,5},{5,1},{2,6},{6,2},{3,7},{7,3}} | collective-permute-start | bytes 6291464 | tf_op jit(solution)/shard_map/ppermute | solution.py:621
  77.0 447.1 %collective-permute-start.7 = (f32[576,256]{1,0:T(8,128)}, f32[576,256]{1,0:T(8,128)}, u32[]{:S(2)}, u32[]{:S(2)}) collective-permute-start(f32[576,256]{1,0:T(8,128)} %get-tuple-element.72.refs_1_), channel_id=1, source_target_pairs={{0,4},{4,0},{1,5},{5,1},{2,6},{6,2},{3,7},{7,3}} | collective-permute-start | bytes 1769480 | tf_op jit(solution)/shard_map/ppermute | solution.py:630
  89.3 434.8 %copy-start.11 = (f32[576,512]{1,0:T(8,128)}, f32[576,512]{1,0:T(8,128)S(1)}, u32[]{:S(2)}) copy-start(f32[576,512]{1,0:T(8,128)S(1)} %get-tuple-element.73.refs_1_) | copy-start | bytes 3538948
  112.9 465.5 %copy-start.1 = (f32[576,1536]{1,0:T(8,128)}, f32[576,1536]{1,0:T(8,128)S(1)}, u32[]{:S(2)}) copy-start(f32[576,1536]{1,0:T(8,128)S(1)} %get-tuple-element.74.refs_1_) | copy-start | bytes 10616836
  166.9 617.8 %collective-permute-start.10 = (f32[576,3584]{1,0:T(8,128)}, f32[576,3584]{1,0:T(8,128)}, u32[]{:S(2)}, u32[]{:S(2)}) collective-permute-start(f32[576,3584]{1,0:T(8,128)} %get-tuple-element.75.refs_1_), channel_id=1, source_target_pairs={{0,4},{4,0},{1,5},{5,1},{2,6},{6,2},{3,7},{7,3}} | collective-permute-start | bytes 24772616 | tf_op jit(solution)/shard_map/ppermute | solution.py:630
  220.5 577.6 %collective-permute-start.11 = (f32[576,3584]{1,0:T(8,128)}, f32[576,3584]{1,0:T(8,128)}, u32[]{:S(2)}, u32[]{:S(2)}) collective-permute-start(f32[576,3584]{1,0:T(8,128)} %get-tuple-element.76.refs_1_), channel_id=1, source_target_pairs={{0,4},{4,0},{1,5},{5,1},{2,6},{6,2},{3,7},{7,3}} | collective-permute-start | bytes 24772616 | tf_op jit(solution)/shard_map/ppermute | solution.py:630
  262.9 6.1 copy-start
  262.9 6.1 copy-start.16
  269.0 254.2 %copy-start.20 = (f32[576,512]{1,0:T(8,128)S(1)}, f32[576,512]{1,0:T(8,128)}, u32[]{:S(2)}) copy-start(f32[576,512]{1,0:T(8,128)} %copy-done.19) | copy-start | bytes 3538948
  379.4 143.8 %collective-permute-start = (f32[8,640]{1,0:T(8,128)S(1)}, f32[8,640]{1,0:T(8,128)S(1)}, u32[]{:S(2)}, u32[]{:S(2)}) collective-permute-start(f32[8,640]{1,0:T(8,128)S(1)} %get-tuple-element.67), channel_id=1, source_target_pairs={{0,4},{4,0},{1,5},{5,1},{2,6},{6,2},{3,7},{7,3}} | collective-permute-start | bytes 61448 | tf_op jit(solution)/shard_map/ppermute | solution.py:639
  523.3 28.8 %collective-permute-start.1 = (f32[576,512]{1,0:T(8,128)S(1)}, f32[576,512]{1,0:T(8,128)S(1)}, u32[]{:S(2)}, u32[]{:S(2)}) collective-permute-start(f32[576,512]{1,0:T(8,128)S(1)} %copy-done.20), channel_id=1, source_target_pairs={{0,4},{4,0},{1,5},{5,1},{2,6},{6,2},{3,7},{7,3}} | collective-permute-start | bytes 3538952 | tf_op jit(solution)/shard_map/ppermute | solution.py:620
  524.1 53.3 %collective-permute-start.8 = (f32[576,512]{1,0:T(8,128)S(1)}, f32[576,512]{1,0:T(8,128)S(1)}, u32[]{:S(2)}, u32[]{:S(2)}) collective-permute-start(f32[576,512]{1,0:T(8,128)S(1)} %get-tuple-element.73.refs_1_), channel_id=1, source_target_pairs={{0,4},{4,0},{1,5},{5,1},{2,6},{6,2},{3,7},{7,3}} | collective-permute-start | bytes 3538952 | tf_op jit(solution)/shard_map/ppermute | solution.py:630
  552.1 259.4 %collective-permute-start.12 = (f32[576,2048]{1,0:T(8,128)S(1)}, f32[576,2048]{1,0:T(8,128)S(1)}, u32[]{:S(2)}, u32[]{:S(2)}) collective-permute-start(f32[576,2048]{1,0:T(8,128)S(1)} %get-tuple-element.77.refs_1_), channel_id=1, source_target_pairs={{0,4},{4,0},{1,5},{5,1},{2,6},{6,2},{3,7},{7,3}} | collective-permute-start | bytes 14155784 | tf_op jit(solution)/shard_map/ppermute | solution.py:630
  578.4 15.6 %collective-permute-start.2 = (f32[576,512]{1,0:T(8,128)S(1)}, f32[576,512]{1,0:T(8,128)S(1)}, u32[]{:S(2)}, u32[]{:S(2)}) collective-permute-start(f32[576,512]{1,0:T(8,128)S(1)} %collective-permute-done.1.refs_0_), channel_id=1, source_target_pairs={{0,1},{1,2},{2,3},{3,0},{4,5},{5,6},{6,7},{7,4}} | collective-permute-start | bytes 3538952 | tf_op jit(solution)/shard_map/ppermute | solution.py:637
  578.4 175.9 %collective-permute-start.9 = (f32[576,1536]{1,0:T(8,128)S(1)}, f32[576,1536]{1,0:T(8,128)S(1)}, u32[]{:S(2)}, u32[]{:S(2)}) collective-permute-start(f32[576,1536]{1,0:T(8,128)S(1)} %get-tuple-element.74.refs_1_), channel_id=1, source_target_pairs={{0,4},{4,0},{1,5},{5,1},{2,6},{6,2},{3,7},{7,3}} | collective-permute-start | bytes 10616840 | tf_op jit(solution)/shard_map/ppermute | solution.py:630
  595.1 25.8 %collective-permute-start.3 = (f32[576,512]{1,0:T(8,128)S(1)}, f32[576,512]{1,0:T(8,128)S(1)}, u32[]{:S(2)}, u32[]{:S(2)}) collective-permute-start(f32[576,512]{1,0:T(8,128)S(1)} %collective-permute-done.1.refs_0_), channel_id=1, source_target_pairs={{0,2},{1,3},{2,0},{3,1},{4,6},{5,7},{6,4},{7,5}} | collective-permute-start | bytes 3538952 | tf_op jit(solution)/shard_map/ppermute | solution.py:637
  621.9 13.7 %collective-permute-start.4 = (f32[576,512]{1,0:T(8,128)S(1)}, f32[576,512]{1,0:T(8,128)S(1)}, u32[]{:S(2)}, u32[]{:S(2)}) collective-permute-start(f32[576,512]{1,0:T(8,128)S(1)} %collective-permute-done.1.refs_0_), channel_id=1, source_target_pairs={{0,3},{1,0},{2,1},{3,2},{4,7},{5,4},{6,5},{7,6}} | collective-permute-start | bytes 3538952 | tf_op jit(solution)/shard_map/ppermute | solution.py:637
  636.6 179.0 %collective-permute-start.13 = (f32[576,256]{1,0:T(8,128)S(1)}, f32[576,256]{1,0:T(8,128)}, u32[]{:S(2)}, u32[]{:S(2)}) collective-permute-start(f32[576,256]{1,0:T(8,128)S(1)} %get-tuple-element.78.refs_1_), channel_id=1, source_target_pairs={{0,4},{4,0},{1,5},{5,1},{2,6},{6,2},{3,7},{7,3}} | collective-permute-start | bytes 1769480 | tf_op jit(solution)/shard_map/ppermute | solution.py:630
  756.1 61.5 %collective-permute-start.14 = (f32[576,256]{1,0:T(8,128)}, f32[576,256]{1,0:T(8,128)}, u32[]{:S(2)}, u32[]{:S(2)}) collective-permute-start(f32[576,256]{1,0:T(8,128)} %get-tuple-element.79.refs_1_), channel_id=1, source_target_pairs={{0,4},{4,0},{1,5},{5,1},{2,6},{6,2},{3,7},{7,3}} | collective-permute-start | bytes 1769480 | tf_op jit(solution)/shard_map/ppermute | solution.py:630
  778.0 3.5 copy-start.4
  (12 other events, 18.3 us)

commit v6 on v5

--- a/solution.py
+++ b/solution.py
@@ -23,40 +23,50 @@
 SHARED = 256
 
 
-def lift_kernel(hid_hbm, tea_hbm, hid_ref, hid_out, tea_out, tea_ref, sem):
+def lift_hidden_kernel(hid_hbm, hid_ref, out_ref, run_ref, sem):
     tp = lax.axis_index("tp")
-    width = hid_out.shape[1]
-    start = tea_hbm.shape[1] - SHARED
-    loads = [
-        pltpu.make_async_copy(hid_hbm, hid_ref, sem.at[0]),
-        pltpu.make_async_copy(tea_hbm.at[:, start:start + SHARED], tea_ref, sem.at[1]),
-    ]
-    for load in loads:
-        load.start()
-    loads[0].wait()
-    hid_out[...] = hid_ref[:, pl.ds(pl.multiple_of(tp * width, width), width)].astype(F32)
-    loads[1].wait()
-    tea_out[...] = tea_ref[...].astype(F32)
-
-
-def lift(hid_t, tea, n_tp):
+    width = out_ref.shape[1]
+    run = pltpu.make_async_copy(hid_hbm.at[:, pl.ds(pl.multiple_of(tp * width, width), width)], run_ref, sem.at[0])
+    run.start()
+    load = pltpu.make_async_copy(hid_hbm, hid_ref, sem.at[1])
+    load.start()
+    run.wait()
+    out_ref[...] = run_ref[...].astype(F32)
+    load.wait()
+
+
+def lift_hidden(hid_t, n_tp):
     dim, tokens = hid_t.shape
-    hbm = pl.BlockSpec(memory_space=pl.ANY)
     whole = pl.BlockSpec(memory_space=VMEM)
     return pl.pallas_call(
-        lift_kernel,
-        in_specs=[hbm, hbm],
-        out_specs=[whole, whole, whole],
-        out_shape=[
-            jax.ShapeDtypeStruct((dim, tokens), BF16),
-            jax.ShapeDtypeStruct((dim, tokens // n_tp), F32),
-            jax.ShapeDtypeStruct((tokens, SHARED), F32),
-        ],
-        scratch_shapes=[VMEM((tokens, SHARED), BF16), pltpu.SemaphoreType.DMA((2,))],
-        compiler_params=pltpu.CompilerParams(vmem_limit_bytes=48 * 2**20),
+        lift_hidden_kernel,
+        in_specs=[pl.BlockSpec(memory_space=pl.ANY)],
+        out_specs=[whole, whole],
+        out_shape=[jax.ShapeDtypeStruct((dim, tokens), BF16), jax.ShapeDtypeStruct((dim, tokens // n_tp), F32)],
+        scratch_shapes=[VMEM((dim, tokens // n_tp), BF16), pltpu.SemaphoreType.DMA((2,))],
+        compiler_params=pltpu.CompilerParams(vmem_limit_bytes=99 * 2**19),
         cost_estimate=pl.CostEstimate(flops=3_000_000, bytes_accessed=5_000_000, transcendentals=0),
-        name="lift",
-    )(hid_t, tea)
+        name="lift_hidden",
+    )(hid_t)
+
+
+def lift_teacher_kernel(tea_ref, out_ref):
+    out_ref[...] = tea_ref[...].astype(F32)
+
+
+def lift_teacher(tea):
+    tokens, vocab = tea.shape
+    rows, last = tokens // 4, vocab // SHARED - 1
+    return pl.pallas_call(
+        lift_teacher_kernel,
+        grid=(4,),
+        in_specs=[pl.BlockSpec((rows, SHARED), lambda j: (j, last))],
+        out_specs=pl.BlockSpec((rows, SHARED), lambda j: (j, 0)),
+        out_shape=jax.ShapeDtypeStruct((tokens, SHARED), F32),
+        compiler_params=pltpu.CompilerParams(dimension_semantics=("arbitrary",), vmem_limit_bytes=48 * 2**20),
+        cost_estimate=pl.CostEstimate(flops=3_000_000, bytes_accessed=5_000_000, transcendentals=0),
+        name="lift_teacher",
+    )(tea)
 
 
 def join_kernel(n_tp, *refs):
@@ -268,8 +278,8 @@
 SLICE = 16
 
 
-def head_kernel(n_tp, stat_ref, mask_ref, x_ref, xt_ref, tab_hbm, tea_hbm, stu_col, tea_col, base_ref, row_ref, de_ref, kl_acc, g_ref,
-                slots, mask_slot, tab_ref, tea_ref, stu_q, tea_q, z_even, z_odd, load_sem, send_sem, recv_sem):
+def head_kernel(n_tp, stat_ref, mask_ref, mask_other, x_ref, xt_ref, tab_hbm, tea_hbm, stu_col, tea_col, base_ref, row_ref, de_ref, kl_acc, g_ref,
+                slots, tab_ref, tea_ref, stu_q, tea_q, z_even, z_odd, load_sem, send_sem, recv_sem):
     tp = lax.axis_index("tp")
     dp = lax.axis_index("dp")
     tokens = x_ref.shape[0]
@@ -279,16 +289,14 @@
     load_tab.start()
     load_tea.start()
     barrier = pltpu.get_barrier_semaphore()
-    peers = [(dp, lax.rem(tp + k, n_tp)) for k in range(1, n_tp)] + [(1 - dp, tp)]
+    peers = [(dp, lax.rem(tp + k, n_tp)) for k in range(1, n_tp)]
     for peer in peers:
         pl.semaphore_signal(barrier, inc=1, device_id=peer, device_id_type=MESH)
     pl.semaphore_wait(barrier, len(peers))
     copies = []
     for k, peer in enumerate(peers):
-        last = k == n_tp - 1
         copies.append(pltpu.make_async_remote_copy(
-            src_ref=mask_ref if last else stat_ref,
-            dst_ref=mask_slot if last else slots.at[k],
+            src_ref=stat_ref, dst_ref=slots.at[k],
             send_sem=send_sem.at[k], recv_sem=recv_sem.at[k], device_id=peer, device_id_type=MESH))
         copies[-1].start()
     load_tab.wait()
@@ -337,7 +345,7 @@
         total = total + part
     total = jnp.where(total > 0.0, total, 1.0)
     mask = mask_ref[...]
-    mask_sum = jnp.sum(mask) + jnp.sum(mask_slot[...])
+    mask_sum = jnp.sum(mask) + jnp.sum(mask_other[...])
     weight = mask / mask_sum
     stu_sum, tea_sum = total[:16, :], total[16:, :]
     base = jnp.sum(weight * (jnp.log(stu_sum) - jnp.log(tea_sum)))
@@ -358,13 +366,13 @@
     de_ref[...] = jnp.dot(xt_ref[...], g_ref[...], preferred_element_type=F32)
 
 
-def head(stat, mask, x, x_t, tab_t, tea, n_tp):
+def head(stat, mask, mask_other, x, x_t, tab_t, tea, n_tp):
     tokens, dim = x.shape
     whole = pl.BlockSpec(memory_space=VMEM)
     hbm = pl.BlockSpec(memory_space=pl.ANY)
     return pl.pallas_call(
         functools.partial(head_kernel, n_tp),
-        in_specs=[whole, whole, whole, whole, hbm, hbm],
+        in_specs=[whole, whole, whole, whole, whole, hbm, hbm],
         out_specs=[whole] * 7,
         out_shape=[
             jax.ShapeDtypeStruct((tokens, 128), F32),
@@ -376,16 +384,16 @@
             jax.ShapeDtypeStruct((tokens, GRAD_TILE), BF16),
         ],
         scratch_shapes=[
-            VMEM((n_tp - 1,) + stat.shape, F32), VMEM(mask.shape, F32),
+            VMEM((n_tp - 1,) + stat.shape, F32),
             VMEM((dim, GRAD_TILE), BF16), VMEM((tokens, GRAD_TILE), BF16),
             VMEM((tokens, GRAD_TILE), F32), VMEM((tokens, GRAD_TILE), F32),
             VMEM((GRAD_ROWS, GRAD_TILE), F32), VMEM((GRAD_ROWS, GRAD_TILE), F32),
-            pltpu.SemaphoreType.DMA((2,)), pltpu.SemaphoreType.DMA((n_tp,)), pltpu.SemaphoreType.DMA((n_tp,)),
+            pltpu.SemaphoreType.DMA((2,)), pltpu.SemaphoreType.DMA((n_tp - 1,)), pltpu.SemaphoreType.DMA((n_tp - 1,)),
         ],
         compiler_params=pltpu.CompilerParams(collective_id=0, has_side_effects=True, vmem_limit_bytes=40 * 2**20),
         cost_estimate=pl.CostEstimate(flops=5_000_000_000, bytes_accessed=2_000_000, transcendentals=0),
         name="head",
-    )(stat, mask, x, x_t, tab_t, tea)
+    )(stat, mask, mask_other, x, x_t, tab_t, tea)
 
 
 def chunk_kernel(first, x_ref, xt_ref, stu_col, tea_col, tab_ref, tea_ref, _, *refs):
@@ -602,7 +610,7 @@
     )(*lead, own, other)
 
 
-CHUNKS = (GRAD_TILE, 512, 1536, 3584, 3584, 2048, 256, 256)
+CHUNKS = (GRAD_TILE, 512, 1536, 3584, 3840, 2048, 256)
 
 
 def solution(mesh):
@@ -616,11 +624,13 @@
         tab_t = tab_rows.T
         mask = mask_rows.reshape(tokens // 128, 128)
         gain = w_final.reshape(1, dim)
-        hid_v, hid_own, tea_own = lift(hid_t, tea_rows, n_tp)
+        hid_v, hid_own = lift_hidden(hid_t, n_tp)
         hid_part = lax.ppermute(hid_own, "dp", swap)
+        mask_other = lax.ppermute(mask, "dp", swap)
+        tea_own = lift_teacher(tea_rows)
         tea_other = lax.ppermute(tea_own, "dp", swap)
         x, x_t, stat = stats(hid_v, gain, mask, tab_t, tea_rows)
-        stu_col, tea_col, base, scale_rows, part, kl, head_g = head(stat, mask, x, x_t, tab_t, tea_rows, n_tp)
+        stu_col, tea_col, base, scale_rows, part, kl, head_g = head(stat, mask, mask_other, x, x_t, tab_t, tea_rows, n_tp)
         dx = None
         own, other = [], []
         start = 0

time: 821 us -> 829 us (level)
    ppermute x1, waiting for transfers between devices: 0.01 us -> 44.8 us  [step(): tea_other = lax.ppermute(tea_own, 'dp', swap)]
    ppermute x1, waiting for transfers between devices: 26.8 us -> 0.01 us  [step(): hid_part = lax.ppermute(hid_own, 'dp', swap)]
    ppermute x3, waiting for transfers between devices: 54 us -> 37 us  [step(): lax.ppermute(hid_part, 'tp', [(i, (i + k) % n_tp) for i in range(n_tp)])]
    ppermute x1, waiting for transfers between devices: 142 us -> 155 us  [step(): share_other = lax.ppermute(share, 'dp', swap)]
    ppermute x8 -> x7, waiting for transfers between devices: 140 us -> 134 us  [step(): other.append(lax.ppermute(part, 'dp', swap))]
    pallas_call x8 -> x7, Pallas kernels: 189 us -> 186 us  [chunk_grad(): pl.pallas_call(functools.partial(chunk_kernel, first), grid=(size // GRAD...]
    pallas_call x9 -> x8, Pallas kernels: 42.6 us -> 44.2 us  [add_chunk(): pl.pallas_call(add_kernel, grid=(size // tile,), in_specs=[hbm, block, bl...]
  transfers between devices with their start and end apart: 15 -> 15, of which waited for: 7 -> 6; matrix products, arithmetic and copies ran while one was open for 0% -> 0% of each run, Pallas kernels for 43% -> 51%
where the time goes in v6:
time: 829 us; the launch traced here: 827 us
  Pallas kernels  426 us (51%)
  waiting for transfers between devices  371 us (45%)
  local copies, waits for them, and re-layouts  14.9 us (2%)
  starting transfers between devices  12.6 us (2%)
    pallas_call x7, Pallas kernels, chunk_grad(): pl.pallas_call(functools.partial(chunk_kernel, first), grid=(size // GRAD...  186 us
    ppermute x1, waiting for transfers between devices, step(): share_other = lax.ppermute(share, 'dp', swap)  155 us
    ppermute x7, waiting for transfers between devices, step(): other.append(lax.ppermute(part, 'dp', swap))  134 us
    pallas_call x1, Pallas kernels, reduce_dx(): pl.pallas_call(functools.partial(dx_kernel, n_tp), in_specs=[whole, whole...  111 us
    pallas_call x1, Pallas kernels, stats(): pl.pallas_call(stats_kernel, grid=(vocab // STAT_TILE,), in_specs=[whole,...  61.6 us
    ppermute x1, waiting for transfers between devices, step(): tea_other = lax.ppermute(tea_own, 'dp', swap)  44.8 us
    pallas_call x8, Pallas kernels, add_chunk(): pl.pallas_call(add_kernel, grid=(size // tile,), in_specs=[hbm, block, bl...  44.2 us
    ppermute x3, waiting for transfers between devices, step(): lax.ppermute(hid_part, 'tp', [(i, (i + k) % n_tp) for i in range(n_tp)])  37 us
  transfers between devices with their start and end apart: 15, of which 6 were waited for; matrix products, arithmetic and copies ran while one was open for 0% of the time, Pallas kernels for 51%

profile of v6, /device:TPU:0, one launch (start us, length us, event | category | flops | bytes accessed | tf_op | source)
XLA Modules:
  0.0 827.4 jit_solution(15136657423899743190)
XLA Ops:
  0.6 3.4 collective-permute-start
  8.3 61.6 %stats.1 = (bf16[2048,576]{1,0:T(8,128)(2,1)S(1)}, bf16[576,2048]{1,0:T(8,128)(2,1)S(1)}, f32[32,128]{1,0:T(8,128)S(1)}) custom-call(bf16[576,2048]{1,0:T(8,128)(2,1)S(1)} %get-tuple-element.38.hid_ref, f32[1,576]{1,0:T(1,128)S(1)} %reshape.14.gain_ref, f32[16,128]{1,0:T(8,128)S(1)} %bitcast.13, bf16[576,12288]{1,0:T(8,128)(2,1)} %bitcast.16, ...), custom_call_target="tpu_custom_call" | custom-call | flops 49999998976 | bytes 70000000 | tf_op jit(solution)/shard_map/stats/pallas_call | solution.py:248
  70.0 6.7 head.1
  78.7 11.1 %chunk_grad.7 = (f32[576,512]{1,0:T(8,128)S(1)}, f32[2048,128]{1,0:T(8,128)S(1)}, f32[2048,576]{1,0:T(8,128)S(1)}) custom-call(bf16[2048,576]{1,0:T(8,128)(2,1)S(1)} %get-tuple-element.39.x_ref, bf16[576,2048]{1,0:T(8,128)(2,1)S(1)} %get-tuple-element.40.xt_ref, f32[2048,128]{1,0:T(8,128)S(1)} %get-tuple-element.42.stu_col, ...), custom_call_target="tpu_custom_call", output_to_operand_aliasing={{1}: (6, {})} | custom-call | flops 3623878656 | bytes 2097152 | tf_op jit(solution)/shard_map/chunk_grad/pallas_call | solution.py:469
  89.8 23.6 %chunk_grad.8 = (f32[576,1536]{1,0:T(8,128)S(1)}, f32[2048,128]{1,0:T(8,128)S(1)}, f32[2048,576]{1,0:T(8,128)S(1)}) custom-call(bf16[2048,576]{1,0:T(8,128)(2,1)S(1)} %get-tuple-element.39.x_ref, bf16[576,2048]{1,0:T(8,128)(2,1)S(1)} %get-tuple-element.40.xt_ref, ...), custom_call_target="tpu_custom_call", output_to_operand_aliasing={{1}: (6, {}), {2}: (7, {})} | custom-call | flops 10871635968 | bytes 6291456 | tf_op jit(solution)/shard_map/chunk_grad/pallas_call | solution.py:469
  115.3 52.9 %chunk_grad.9 = (f32[576,3584]{1,0:T(8,128)}, f32[2048,128]{1,0:T(8,128)S(1)}, f32[2048,576]{1,0:T(8,128)S(1)}) custom-call(bf16[2048,576]{1,0:T(8,128)(2,1)S(1)} %get-tuple-element.39.x_ref, bf16[576,2048]{1,0:T(8,128)(2,1)S(1)} %get-tuple-element.40.xt_ref, ...), custom_call_target="tpu_custom_call", output_to_operand_aliasing={{1}: (6, {}), {2}: (7, {})} | custom-call | flops 25367150592 | bytes 14680064 | tf_op jit(solution)/shard_map/chunk_grad/pallas_call | solution.py:469
  168.2 56.7 %chunk_grad.10 = (f32[576,3840]{1,0:T(8,128)}, f32[2048,128]{1,0:T(8,128)S(1)}, f32[2048,576]{1,0:T(8,128)S(1)}) custom-call(bf16[2048,576]{1,0:T(8,128)(2,1)S(1)} %get-tuple-element.39.x_ref, bf16[576,2048]{1,0:T(8,128)(2,1)S(1)} %get-tuple-element.40.xt_ref, ...), custom_call_target="tpu_custom_call", output_to_operand_aliasing={{1}: (6, {}), {2}: (7, {})} | custom-call | flops 27179089920 | bytes 15728640 | tf_op jit(solution)/shard_map/chunk_grad/pallas_call | solution.py:469
  226.7 30.5 %chunk_grad.11 = (f32[576,2048]{1,0:T(8,128)S(1)}, f32[2048,128]{1,0:T(8,128)S(1)}, f32[2048,576]{1,0:T(8,128)S(1)}) custom-call(bf16[2048,576]{1,0:T(8,128)(2,1)S(1)} %get-tuple-element.39.x_ref, bf16[576,2048]{1,0:T(8,128)(2,1)S(1)} %get-tuple-element.40.xt_ref, ...), custom_call_target="tpu_custom_call", output_to_operand_aliasing={{1}: (6, {}), {2}: (7, {})} | custom-call | flops 14495514624 | bytes 8388608 | tf_op jit(solution)/shard_map/chunk_grad/pallas_call | solution.py:469
  259.4 4.9 chunk_grad.12
  265.2 5.9 chunk_grad.13
  271.1 111.3 %reduce_dx.1 = (f32[576,2048]{1,0:T(8,128)S(1)}, f32[8,640]{1,0:T(8,128)S(1)}) custom-call(f32[2048,576]{1,0:T(8,128)S(1)} %get-tuple-element.58.dx_ref, f32[2048,128]{1,0:T(8,128)S(1)} %get-tuple-element.59.kl_ref, f32[8,128]{1,0:T(8,128)S(1)} %get-tuple-element.60.base_ref, bf16[576,2048]{1,0:T(8,128)(2,1)S(1)} %bitcast.8, f32[1,576]{1,0:T(1,128)S(1)} %copy-done.18), custom_call_target="tpu_custom_call" | custom-call | flops 49999998976 | bytes 20000000 | tf_op jit(solution)/shard_map/reduce_dx/pallas_call | solution.py:569
  382.6 154.9 %collective-permute-done.1 = f32[8,640]{1,0:T(8,128)S(1)} collective-permute-done((f32[8,640]{1,0:T(8,128)S(1)}, f32[8,640]{1,0:T(8,128)S(1)}, u32[]{:S(2)}, u32[]{:S(2)}) %collective-permute-start.1) | collective-permute-done | bytes 20512 | tf_op jit(solution)/shard_map/ppermute | solution.py:649
  537.9 3.3 lift_teacher.1.tea_ref
  543.3 23.2 %collective-permute-done.9.refs_2_ = f32[576,512]{1,0:T(8,128)} collective-permute-done((f32[576,512]{1,0:T(8,128)S(1)}, f32[576,512]{1,0:T(8,128)}, u32[]{:S(2)}, u32[]{:S(2)}) %collective-permute-start.9) | collective-permute-done | bytes 1179680 | tf_op jit(solution)/shard_map/ppermute | solution.py:640
  566.5 44.8 %collective-permute-done.7.tea_ref = f32[2048,256]{1,0:T(8,128)S(1)} collective-permute-done((f32[2048,256]{1,0:T(8,128)S(1)}, f32[2048,256]{1,0:T(8,128)S(1)}, u32[]{:S(2)}, u32[]{:S(2)}) %collective-permute-start.7) | collective-permute-done | bytes 2097184 | tf_op jit(solution)/shard_map/ppermute | solution.py:631
  614.2 22.9 %collective-permute-done.4.refs_2_ = f32[576,512]{1,0:T(8,128)S(1)} collective-permute-done((f32[576,512]{1,0:T(8,128)}, f32[576,512]{1,0:T(8,128)S(1)}, u32[]{:S(2)}, u32[]{:S(2)}) %collective-permute-start.4) | collective-permute-done | bytes 1179680 | tf_op jit(solution)/shard_map/ppermute | solution.py:647
  638.2 14.0 %collective-permute-done.5.refs_3_ = f32[576,512]{1,0:T(8,128)S(1)} collective-permute-done((f32[576,512]{1,0:T(8,128)}, f32[576,512]{1,0:T(8,128)S(1)}, u32[]{:S(2)}, u32[]{:S(2)}) %collective-permute-start.5) | collective-permute-done | bytes 1179680 | tf_op jit(solution)/shard_map/ppermute | solution.py:647
  656.2 4.5 shared_grad.2.refs_1_
  666.4 4.5 shared_grad.3.refs_2_
  677.3 111.1 %collective-permute-done.10.refs_2_ = f32[576,1536]{1,0:T(8,128)} collective-permute-done((f32[576,1536]{1,0:T(8,128)S(1)}, f32[576,1536]{1,0:T(8,128)}, u32[]{:S(2)}, u32[]{:S(2)}) %collective-permute-start.10) | collective-permute-done | bytes 3538976 | tf_op jit(solution)/shard_map/ppermute | solution.py:640
  788.4 5.6 add_chunk.11.refs_0_
  794.0 13.4 %add_chunk.12.refs_0_ = f32[576,12288]{1,0:T(8,128)} custom-call(f32[576,12288]{1,0:T(8,128)} %add_chunk.11.refs_0_, f32[576,3584]{1,0:T(8,128)} %get-tuple-element.68.refs_1_, f32[576,3584]{1,0:T(8,128)} %collective-permute-done.11.refs_2_), custom_call_target="tpu_custom_call", output_to_operand_aliasing={{}: (0, {})} | custom-call | flops 2064384 | bytes 24772608 | tf_op jit(solution)/shard_map/add_chunk/pallas_call | solution.py:600
  807.4 14.9 %add_chunk.13.refs_0_ = f32[576,12288]{1,0:T(8,128)} custom-call(f32[576,12288]{1,0:T(8,128)} %add_chunk.12.refs_0_, f32[576,3840]{1,0:T(8,128)} %get-tuple-element.69.refs_1_, f32[576,3840]{1,0:T(8,128)} %collective-permute-done.12.refs_2_), custom_call_target="tpu_custom_call", output_to_operand_aliasing={{}: (0, {})} | custom-call | flops 2211840 | bytes 26542080 | tf_op jit(solution)/shard_map/add_chunk/pallas_call | solution.py:600
  822.3 3.2 add_chunk.14.refs_0_
  (81 shorter events, 37.7 us)
Async XLA Ops:
  0.6 69.3 %collective-permute-start = (f32[16,128]{1,0:T(8,128)}, f32[16,128]{1,0:T(8,128)S(1)}, u32[]{:S(2)}, u32[]{:S(2)}) collective-permute-start(f32[16,128]{1,0:T(8,128)} %bitcast.12), channel_id=1, source_target_pairs={{0,4},{4,0},{1,5},{5,1},{2,6},{6,2},{3,7},{7,3}} | collective-permute-start | bytes 24584 | tf_op jit(solution)/shard_map/ppermute | solution.py:629
  6.9 535.7 %collective-permute-start.2 = (f32[576,512]{1,0:T(8,128)}, f32[576,512]{1,0:T(8,128)}, u32[]{:S(2)}, u32[]{:S(2)}) collective-permute-start(f32[576,512]{1,0:T(8,128)} %get-tuple-element.64), channel_id=1, source_target_pairs={{0,4},{4,0},{1,5},{5,1},{2,6},{6,2},{3,7},{7,3}} | collective-permute-start | bytes 3538952 | tf_op jit(solution)/shard_map/ppermute | solution.py:628
  7.6 62.3 %copy-start.17 = (f32[1,576]{1,0:T(1,128)}, f32[1,576]{1,0:T(1,128)S(1)}, u32[]{:S(2)}) copy-start(f32[1,576]{1,0:T(1,128)S(1)} %reshape.14.gain_ref) | copy-start | bytes 6916
  8.3 61.6 %copy-start.20 = (f32[2048]{0:T(1024)S(1)}, f32[2048]{0:T(1024)}, u32[]{:S(2)}) copy-start(f32[2048]{0:T(1024)} %param.9) | copy-start | bytes 24580
  76.7 305.7 %collective-permute-start.6 = (f32[32,128]{1,0:T(8,128)}, f32[32,128]{1,0:T(8,128)}, u32[]{:S(2)}, u32[]{:S(2)}) collective-permute-start(f32[32,128]{1,0:T(8,128)} %get-tuple-element.63.row_ref), channel_id=1, source_target_pairs={{0,4},{4,0},{1,5},{5,1},{2,6},{6,2},{3,7},{7,3}} | collective-permute-start | bytes 49160 | tf_op jit(solution)/shard_map/ppermute | solution.py:644
  76.7 464.5 %collective-permute-start.8 = (f32[576,256]{1,0:T(8,128)}, f32[576,256]{1,0:T(8,128)}, u32[]{:S(2)}, u32[]{:S(2)}) collective-permute-start(f32[576,256]{1,0:T(8,128)} %get-tuple-element.65.refs_1_), channel_id=1, source_target_pairs={{0,4},{4,0},{1,5},{5,1},{2,6},{6,2},{3,7},{7,3}} | collective-permute-start | bytes 1769480 | tf_op jit(solution)/shard_map/ppermute | solution.py:640
  89.8 447.7 %copy-start.13 = (f32[576,512]{1,0:T(8,128)}, f32[576,512]{1,0:T(8,128)S(1)}, u32[]{:S(2)}) copy-start(f32[576,512]{1,0:T(8,128)S(1)} %get-tuple-element.66.refs_1_) | copy-start | bytes 3538948
  168.2 625.8 %collective-permute-start.11 = (f32[576,3584]{1,0:T(8,128)}, f32[576,3584]{1,0:T(8,128)}, u32[]{:S(2)}, u32[]{:S(2)}) collective-permute-start(f32[576,3584]{1,0:T(8,128)} %get-tuple-element.68.refs_1_), channel_id=1, source_target_pairs={{0,4},{4,0},{1,5},{5,1},{2,6},{6,2},{3,7},{7,3}} | collective-permute-start | bytes 24772616 | tf_op jit(solution)/shard_map/ppermute | solution.py:640
  224.9 582.5 %collective-permute-start.12 = (f32[576,3840]{1,0:T(8,128)}, f32[576,3840]{1,0:T(8,128)}, u32[]{:S(2)}, u32[]{:S(2)}) collective-permute-start(f32[576,3840]{1,0:T(8,128)} %get-tuple-element.69.refs_1_), channel_id=1, source_target_pairs={{0,4},{4,0},{1,5},{5,1},{2,6},{6,2},{3,7},{7,3}} | collective-permute-start | bytes 26542088 | tf_op jit(solution)/shard_map/ppermute | solution.py:640
  265.2 5.9 copy-start
  265.2 5.9 copy-start.18
  382.4 155.1 %collective-permute-start.1 = (f32[8,640]{1,0:T(8,128)S(1)}, f32[8,640]{1,0:T(8,128)S(1)}, u32[]{:S(2)}, u32[]{:S(2)}) collective-permute-start(f32[8,640]{1,0:T(8,128)S(1)} %get-tuple-element.61), channel_id=1, source_target_pairs={{0,4},{4,0},{1,5},{5,1},{2,6},{6,2},{3,7},{7,3}} | collective-permute-start | bytes 61448 | tf_op jit(solution)/shard_map/ppermute | solution.py:649
  537.5 5.1 slice-start
  537.5 75.1 %copy-start.4 = (f32[576,1536]{1,0:T(8,128)S(1)}, f32[576,1536]{1,0:T(8,128)}, u32[]{:S(2)}) copy-start(f32[576,1536]{1,0:T(8,128)} %copy-done.3) | copy-start | bytes 10616836
  537.5 29.0 %collective-permute-start.9 = (f32[576,512]{1,0:T(8,128)S(1)}, f32[576,512]{1,0:T(8,128)}, u32[]{:S(2)}, u32[]{:S(2)}) collective-permute-start(f32[576,512]{1,0:T(8,128)S(1)} %get-tuple-element.66.refs_1_), channel_id=1, source_target_pairs={{0,4},{4,0},{1,5},{5,1},{2,6},{6,2},{3,7},{7,3}} | collective-permute-start | bytes 3538952 | tf_op jit(solution)/shard_map/ppermute | solution.py:640
  541.2 115.0 %copy-start.1 = (bf16[2048,576]{0,1:T(8,128)(2,1)S(1)}, bf16[2048,576]{0,1:T(8,128)(2,1)}, u32[]{:S(2)}) copy-start(bf16[2048,576]{0,1:T(8,128)(2,1)} %param.5) | copy-start | bytes 7077892
  541.2 70.1 %collective-permute-start.7 = (f32[2048,256]{1,0:T(8,128)S(1)}, f32[2048,256]{1,0:T(8,128)S(1)}, u32[]{:S(2)}, u32[]{:S(2)}) collective-permute-start(f32[2048,256]{1,0:T(8,128)S(1)} %lift_teacher.1.tea_ref), channel_id=1, source_target_pairs={{0,4},{4,0},{1,5},{5,1},{2,6},{6,2},{3,7},{7,3}} | collective-permute-start | bytes 6291464 | tf_op jit(solution)/shard_map/ppermute | solution.py:631
  542.6 279.6 %collective-permute-start.13 = (f32[576,2048]{1,0:T(8,128)S(1)}, f32[576,2048]{1,0:T(8,128)S(1)}, u32[]{:S(2)}, u32[]{:S(2)}) collective-permute-start(f32[576,2048]{1,0:T(8,128)S(1)} %bitcast.11), channel_id=1, source_target_pairs={{0,4},{4,0},{1,5},{5,1},{2,6},{6,2},{3,7},{7,3}} | collective-permute-start | bytes 14155784 | tf_op jit(solution)/shard_map/ppermute | solution.py:640
  566.5 46.5 %collective-permute-start.3 = (f32[576,512]{1,0:T(8,128)}, f32[576,512]{1,0:T(8,128)S(1)}, u32[]{:S(2)}, u32[]{:S(2)}) collective-permute-start(f32[576,512]{1,0:T(8,128)} %collective-permute-done.2.refs_0_), channel_id=1, source_target_pairs={{0,1},{1,2},{2,3},{3,0},{4,5},{5,6},{6,7},{7,4}} | collective-permute-start | bytes 3538952 | tf_op jit(solution)/shard_map/ppermute | solution.py:647
  612.7 175.7 %collective-permute-start.10 = (f32[576,1536]{1,0:T(8,128)S(1)}, f32[576,1536]{1,0:T(8,128)}, u32[]{:S(2)}, u32[]{:S(2)}) collective-permute-start(f32[576,1536]{1,0:T(8,128)S(1)} %copy-done.4), channel_id=1, source_target_pairs={{0,4},{4,0},{1,5},{5,1},{2,6},{6,2},{3,7},{7,3}} | collective-permute-start | bytes 10616840 | tf_op jit(solution)/shard_map/ppermute | solution.py:640
  613.0 43.2 %copy-start.7 = (f32[576,512]{1,0:T(8,128)}, f32[576,512]{1,0:T(8,128)S(1)}, u32[]{:S(2)}) copy-start(f32[576,512]{1,0:T(8,128)S(1)} %collective-permute-done.3.refs_1_) | copy-start | bytes 3538948
  613.0 24.2 %collective-permute-start.4 = (f32[576,512]{1,0:T(8,128)}, f32[576,512]{1,0:T(8,128)S(1)}, u32[]{:S(2)}, u32[]{:S(2)}) collective-permute-start(f32[576,512]{1,0:T(8,128)} %collective-permute-done.2.refs_0_), channel_id=1, source_target_pairs={{0,2},{1,3},{2,0},{3,1},{4,6},{5,7},{6,4},{7,5}} | collective-permute-start | bytes 3538952 | tf_op jit(solution)/shard_map/ppermute | solution.py:647
  638.2 14.0 %collective-permute-start.5 = (f32[576,512]{1,0:T(8,128)}, f32[576,512]{1,0:T(8,128)S(1)}, u32[]{:S(2)}, u32[]{:S(2)}) collective-permute-start(f32[576,512]{1,0:T(8,128)} %collective-permute-done.2.refs_0_), channel_id=1, source_target_pairs={{0,3},{1,0},{2,1},{3,2},{4,7},{5,4},{6,5},{7,6}} | collective-permute-start | bytes 3538952 | tf_op jit(solution)/shard_map/ppermute | solution.py:647
  653.2 172.2 %collective-permute-start.14 = (f32[576,256]{1,0:T(8,128)}, f32[576,256]{1,0:T(8,128)}, u32[]{:S(2)}, u32[]{:S(2)}) collective-permute-start(f32[576,256]{1,0:T(8,128)} %copy-done.15), channel_id=1, source_target_pairs={{0,4},{4,0},{1,5},{5,1},{2,6},{6,2},{3,7},{7,3}} | collective-permute-start | bytes 1769480 | tf_op jit(solution)/shard_map/ppermute | solution.py:640
  (14 other events, 25.7 us)

commit v7 on v5

--- a/solution.py
+++ b/solution.py
@@ -268,8 +268,8 @@
 SLICE = 16
 
 
-def head_kernel(n_tp, stat_ref, mask_ref, x_ref, xt_ref, tab_hbm, tea_hbm, stu_col, tea_col, base_ref, row_ref, de_ref, kl_acc, g_ref,
-                slots, mask_slot, tab_ref, tea_ref, stu_q, tea_q, z_even, z_odd, load_sem, send_sem, recv_sem):
+def head_kernel(n_tp, stat_ref, mask_ref, mask_other, x_ref, xt_ref, tab_hbm, tea_hbm, stu_col, tea_col, base_ref, row_ref, de_ref, kl_acc, g_ref,
+                slots, tab_ref, tea_ref, stu_q, tea_q, z_even, z_odd, load_sem, send_sem, recv_sem):
     tp = lax.axis_index("tp")
     dp = lax.axis_index("dp")
     tokens = x_ref.shape[0]
@@ -279,16 +279,14 @@
     load_tab.start()
     load_tea.start()
     barrier = pltpu.get_barrier_semaphore()
-    peers = [(dp, lax.rem(tp + k, n_tp)) for k in range(1, n_tp)] + [(1 - dp, tp)]
+    peers = [(dp, lax.rem(tp + k, n_tp)) for k in range(1, n_tp)]
     for peer in peers:
         pl.semaphore_signal(barrier, inc=1, device_id=peer, device_id_type=MESH)
     pl.semaphore_wait(barrier, len(peers))
     copies = []
     for k, peer in enumerate(peers):
-        last = k == n_tp - 1
         copies.append(pltpu.make_async_remote_copy(
-            src_ref=mask_ref if last else stat_ref,
-            dst_ref=mask_slot if last else slots.at[k],
+            src_ref=stat_ref, dst_ref=slots.at[k],
             send_sem=send_sem.at[k], recv_sem=recv_sem.at[k], device_id=peer, device_id_type=MESH))
         copies[-1].start()
     load_tab.wait()
@@ -337,7 +335,7 @@
         total = total + part
     total = jnp.where(total > 0.0, total, 1.0)
     mask = mask_ref[...]
-    mask_sum = jnp.sum(mask) + jnp.sum(mask_slot[...])
+    mask_sum = jnp.sum(mask) + jnp.sum(mask_other[...])
     weight = mask / mask_sum
     stu_sum, tea_sum = total[:16, :], total[16:, :]
     base = jnp.sum(weight * (jnp.log(stu_sum) - jnp.log(tea_sum)))
@@ -358,13 +356,13 @@
     de_ref[...] = jnp.dot(xt_ref[...], g_ref[...], preferred_element_type=F32)
 
 
-def head(stat, mask, x, x_t, tab_t, tea, n_tp):
+def head(stat, mask, mask_other, x, x_t, tab_t, tea, n_tp):
     tokens, dim = x.shape
     whole = pl.BlockSpec(memory_space=VMEM)
     hbm = pl.BlockSpec(memory_space=pl.ANY)
     return pl.pallas_call(
         functools.partial(head_kernel, n_tp),
-        in_specs=[whole, whole, whole, whole, hbm, hbm],
+        in_specs=[whole, whole, whole, whole, whole, hbm, hbm],
         out_specs=[whole] * 7,
         out_shape=[
             jax.ShapeDtypeStruct((tokens, 128), F32),
@@ -376,16 +374,16 @@
             jax.ShapeDtypeStruct((tokens, GRAD_TILE), BF16),
         ],
         scratch_shapes=[
-            VMEM((n_tp - 1,) + stat.shape, F32), VMEM(mask.shape, F32),
+            VMEM((n_tp - 1,) + stat.shape, F32),
             VMEM((dim, GRAD_TILE), BF16), VMEM((tokens, GRAD_TILE), BF16),
             VMEM((tokens, GRAD_TILE), F32), VMEM((tokens, GRAD_TILE), F32),
             VMEM((GRAD_ROWS, GRAD_TILE), F32), VMEM((GRAD_ROWS, GRAD_TILE), F32),
-            pltpu.SemaphoreType.DMA((2,)), pltpu.SemaphoreType.DMA((n_tp,)), pltpu.SemaphoreType.DMA((n_tp,)),
+            pltpu.SemaphoreType.DMA((2,)), pltpu.SemaphoreType.DMA((n_tp - 1,)), pltpu.SemaphoreType.DMA((n_tp - 1,)),
         ],
         compiler_params=pltpu.CompilerParams(collective_id=0, has_side_effects=True, vmem_limit_bytes=40 * 2**20),
         cost_estimate=pl.CostEstimate(flops=5_000_000_000, bytes_accessed=2_000_000, transcendentals=0),
         name="head",
-    )(stat, mask, x, x_t, tab_t, tea)
+    )(stat, mask, mask_other, x, x_t, tab_t, tea)
 
 
 def chunk_kernel(first, x_ref, xt_ref, stu_col, tea_col, tab_ref, tea_ref, _, *refs):
@@ -618,9 +616,10 @@
         gain = w_final.reshape(1, dim)
         hid_v, hid_own, tea_own = lift(hid_t, tea_rows, n_tp)
         hid_part = lax.ppermute(hid_own, "dp", swap)
+        mask_other = lax.ppermute(mask, "dp", swap)
         tea_other = lax.ppermute(tea_own, "dp", swap)
         x, x_t, stat = stats(hid_v, gain, mask, tab_t, tea_rows)
-        stu_col, tea_col, base, scale_rows, part, kl, head_g = head(stat, mask, x, x_t, tab_t, tea_rows, n_tp)
+        stu_col, tea_col, base, scale_rows, part, kl, head_g = head(stat, mask, mask_other, x, x_t, tab_t, tea_rows, n_tp)
         dx = None
         own, other = [], []
         start = 0

time: 821 us -> 821 us (level)
  transfers between devices with their start and end apart: 15 -> 16, of which waited for: 7 -> 7; matrix products, arithmetic and copies ran while one was open for 0% -> 0% of each run, Pallas kernels for 43% -> 52%
where the time goes in v7:
time: 821 us; the launch traced here: 820 us
  Pallas kernels  425 us (52%)
  waiting for transfers between devices  366 us (45%)
  local copies, waits for them, and re-layouts  14.5 us (2%)
  starting transfers between devices  12 us (1%)
    pallas_call x8, Pallas kernels, chunk_grad(): pl.pallas_call(functools.partial(chunk_kernel, first), grid=(size // GRAD...  189 us
    ppermute x1, waiting for transfers between devices, step(): share_other = lax.ppermute(share, 'dp', swap)  143 us
    ppermute x8, waiting for transfers between devices, step(): other.append(lax.ppermute(part, 'dp', swap))  141 us
    pallas_call x1, Pallas kernels, reduce_dx(): pl.pallas_call(functools.partial(dx_kernel, n_tp), in_specs=[whole, whole...  111 us
    pallas_call x1, Pallas kernels, stats(): pl.pallas_call(stats_kernel, grid=(vocab // STAT_TILE,), in_specs=[whole,...  61.6 us
    ppermute x3, waiting for transfers between devices, step(): lax.ppermute(hid_part, 'tp', [(i, (i + k) % n_tp) for i in range(n_tp)])  54.5 us
    pallas_call x9, Pallas kernels, add_chunk(): pl.pallas_call(add_kernel, grid=(size // tile,), in_specs=[hbm, block, bl...  42.6 us
    ppermute x1, waiting for transfers between devices, step(): hid_part = lax.ppermute(hid_own, 'dp', swap)  26.8 us
  transfers between devices with their start and end apart: 16, of which 7 were waited for; matrix products, arithmetic and copies ran while one was open for 0% of the time, Pallas kernels for 52%

profile of v7, /device:TPU:0, one launch (start us, length us, event | category | flops | bytes accessed | tf_op | source)
XLA Modules:
  0.0 820.2 jit_solution(15078216539674780840)
XLA Ops:
  4.0 3.4 lift.1
  8.5 61.6 %stats.1 = (bf16[2048,576]{1,0:T(8,128)(2,1)S(1)}, bf16[576,2048]{1,0:T(8,128)(2,1)S(1)}, f32[32,128]{1,0:T(8,128)S(1)}) custom-call(bf16[576,2048]{1,0:T(8,128)(2,1)S(1)} %get-tuple-element.42.hid_ref, f32[1,576]{1,0:T(1,128)S(1)} %reshape.14.gain_ref, f32[16,128]{1,0:T(8,128)S(1)} %bitcast.11, bf16[576,12288]{1,0:T(8,128)(2,1)} %bitcast.14, ...), custom_call_target="tpu_custom_call" | custom-call | flops 49999998976 | bytes 70000000 | tf_op jit(solution)/shard_map/stats/pallas_call | solution.py:238
  70.1 6.7 head.1
  78.9 11.1 %chunk_grad.8 = (f32[576,512]{1,0:T(8,128)S(1)}, f32[2048,128]{1,0:T(8,128)S(1)}, f32[2048,576]{1,0:T(8,128)S(1)}) custom-call(bf16[2048,576]{1,0:T(8,128)(2,1)S(1)} %get-tuple-element.43.x_ref, bf16[576,2048]{1,0:T(8,128)(2,1)S(1)} %get-tuple-element.44.xt_ref, f32[2048,128]{1,0:T(8,128)S(1)} %get-tuple-element.46.stu_col, ...), custom_call_target="tpu_custom_call", output_to_operand_aliasing={{1}: (6, {})} | custom-call | flops 3623878656 | bytes 2097152 | tf_op jit(solution)/shard_map/chunk_grad/pallas_call | solution.py:459
  90.0 23.6 %chunk_grad.9 = (f32[576,1536]{1,0:T(8,128)S(1)}, f32[2048,128]{1,0:T(8,128)S(1)}, f32[2048,576]{1,0:T(8,128)S(1)}) custom-call(bf16[2048,576]{1,0:T(8,128)(2,1)S(1)} %get-tuple-element.43.x_ref, bf16[576,2048]{1,0:T(8,128)(2,1)S(1)} %get-tuple-element.44.xt_ref, ...), custom_call_target="tpu_custom_call", output_to_operand_aliasing={{1}: (6, {}), {2}: (7, {})} | custom-call | flops 10871635968 | bytes 6291456 | tf_op jit(solution)/shard_map/chunk_grad/pallas_call | solution.py:459
  113.7 53.9 %chunk_grad.10 = (f32[576,3584]{1,0:T(8,128)}, f32[2048,128]{1,0:T(8,128)S(1)}, f32[2048,576]{1,0:T(8,128)S(1)}) custom-call(bf16[2048,576]{1,0:T(8,128)(2,1)S(1)} %get-tuple-element.43.x_ref, bf16[576,2048]{1,0:T(8,128)(2,1)S(1)} %get-tuple-element.44.xt_ref, ...), custom_call_target="tpu_custom_call", output_to_operand_aliasing={{1}: (6, {}), {2}: (7, {})} | custom-call | flops 25367150592 | bytes 14680064 | tf_op jit(solution)/shard_map/chunk_grad/pallas_call | solution.py:459
  167.6 53.0 %chunk_grad.11 = (f32[576,3584]{1,0:T(8,128)}, f32[2048,128]{1,0:T(8,128)S(1)}, f32[2048,576]{1,0:T(8,128)S(1)}) custom-call(bf16[2048,576]{1,0:T(8,128)(2,1)S(1)} %get-tuple-element.43.x_ref, bf16[576,2048]{1,0:T(8,128)(2,1)S(1)} %get-tuple-element.44.xt_ref, ...), custom_call_target="tpu_custom_call", output_to_operand_aliasing={{1}: (6, {}), {2}: (7, {})} | custom-call | flops 25367150592 | bytes 14680064 | tf_op jit(solution)/shard_map/chunk_grad/pallas_call | solution.py:459
  222.5 30.5 %chunk_grad.12 = (f32[576,2048]{1,0:T(8,128)S(1)}, f32[2048,128]{1,0:T(8,128)S(1)}, f32[2048,576]{1,0:T(8,128)S(1)}) custom-call(bf16[2048,576]{1,0:T(8,128)(2,1)S(1)} %get-tuple-element.43.x_ref, bf16[576,2048]{1,0:T(8,128)(2,1)S(1)} %get-tuple-element.44.xt_ref, ...), custom_call_target="tpu_custom_call", output_to_operand_aliasing={{1}: (6, {}), {2}: (7, {})} | custom-call | flops 14495514624 | bytes 8388608 | tf_op jit(solution)/shard_map/chunk_grad/pallas_call | solution.py:459
  253.0 4.9 chunk_grad.13
  257.9 5.7 chunk_grad.14
  263.7 6.1 chunk_grad.15
  269.8 111.3 %reduce_dx.1 = (f32[576,2048]{1,0:T(8,128)S(1)}, f32[8,640]{1,0:T(8,128)S(1)}) custom-call(f32[2048,576]{1,0:T(8,128)S(1)} %get-tuple-element.64.dx_ref, f32[2048,128]{1,0:T(8,128)S(1)} %get-tuple-element.65.kl_ref, f32[8,128]{1,0:T(8,128)S(1)} %get-tuple-element.66.base_ref, bf16[576,2048]{1,0:T(8,128)(2,1)S(1)} %bitcast.8, f32[1,576]{1,0:T(1,128)S(1)} %copy-done.16), custom_call_target="tpu_custom_call" | custom-call | flops 49999998976 | bytes 20000000 | tf_op jit(solution)/shard_map/reduce_dx/pallas_call | solution.py:559
  381.3 143.0 %collective-permute-done.1 = f32[8,640]{1,0:T(8,128)S(1)} collective-permute-done((f32[8,640]{1,0:T(8,128)S(1)}, f32[8,640]{1,0:T(8,128)S(1)}, u32[]{:S(2)}, u32[]{:S(2)}) %collective-permute-start.1) | collective-permute-done | bytes 20512 | tf_op jit(solution)/shard_map/ppermute | solution.py:638
  526.4 26.8 %collective-permute-done.2.refs_0_ = f32[576,512]{1,0:T(8,128)S(1)} collective-permute-done((f32[576,512]{1,0:T(8,128)S(1)}, f32[576,512]{1,0:T(8,128)S(1)}, u32[]{:S(2)}, u32[]{:S(2)}) %collective-permute-start.2) | collective-permute-done | bytes 1179680 | tf_op jit(solution)/shard_map/ppermute | solution.py:618
  553.5 25.0 %collective-permute-done.9.refs_2_ = f32[576,512]{1,0:T(8,128)S(1)} collective-permute-done((f32[576,512]{1,0:T(8,128)S(1)}, f32[576,512]{1,0:T(8,128)S(1)}, u32[]{:S(2)}, u32[]{:S(2)}) %collective-permute-start.9) | collective-permute-done | bytes 1179680 | tf_op jit(solution)/shard_map/ppermute | solution.py:629
  579.8 15.3 %collective-permute-done.3.refs_1_ = f32[576,512]{1,0:T(8,128)S(1)} collective-permute-done((f32[576,512]{1,0:T(8,128)S(1)}, f32[576,512]{1,0:T(8,128)S(1)}, u32[]{:S(2)}, u32[]{:S(2)}) %collective-permute-start.3) | collective-permute-done | bytes 1179680 | tf_op jit(solution)/shard_map/ppermute | solution.py:636
  597.3 25.5 %collective-permute-done.4.refs_2_ = f32[576,512]{1,0:T(8,128)S(1)} collective-permute-done((f32[576,512]{1,0:T(8,128)S(1)}, f32[576,512]{1,0:T(8,128)S(1)}, u32[]{:S(2)}, u32[]{:S(2)}) %collective-permute-start.4) | collective-permute-done | bytes 1179680 | tf_op jit(solution)/shard_map/ppermute | solution.py:636
  623.8 13.7 %collective-permute-done.5.refs_3_ = f32[576,512]{1,0:T(8,128)S(1)} collective-permute-done((f32[576,512]{1,0:T(8,128)S(1)}, f32[576,512]{1,0:T(8,128)S(1)}, u32[]{:S(2)}, u32[]{:S(2)}) %collective-permute-start.5) | collective-permute-done | bytes 1179680 | tf_op jit(solution)/shard_map/ppermute | solution.py:636
  638.9 116.5 %collective-permute-done.10.refs_2_ = f32[576,1536]{1,0:T(8,128)S(1)} collective-permute-done((f32[576,1536]{1,0:T(8,128)S(1)}, f32[576,1536]{1,0:T(8,128)S(1)}, u32[]{:S(2)}, u32[]{:S(2)}) %collective-permute-start.10) | collective-permute-done | bytes 3538976 | tf_op jit(solution)/shard_map/ppermute | solution.py:629
  759.2 5.2 shared_grad.2.refs_1_
  768.9 5.3 shared_grad.3.refs_2_
  785.2 13.4 %add_chunk.13.refs_0_ = f32[576,12288]{1,0:T(8,128)} custom-call(f32[576,12288]{1,0:T(8,128)} %add_chunk.12.refs_0_, f32[576,3584]{1,0:T(8,128)} %get-tuple-element.75.refs_1_, f32[576,3584]{1,0:T(8,128)} %collective-permute-done.11.refs_2_), custom_call_target="tpu_custom_call", output_to_operand_aliasing={{}: (0, {})} | custom-call | flops 2064384 | bytes 24772608 | tf_op jit(solution)/shard_map/add_chunk/pallas_call | solution.py:590
  798.6 13.4 %add_chunk.14.refs_0_ = f32[576,12288]{1,0:T(8,128)} custom-call(f32[576,12288]{1,0:T(8,128)} %add_chunk.13.refs_0_, f32[576,3584]{1,0:T(8,128)} %get-tuple-element.76.refs_1_, f32[576,3584]{1,0:T(8,128)} %collective-permute-done.12.refs_2_), custom_call_target="tpu_custom_call", output_to_operand_aliasing={{}: (0, {})} | custom-call | flops 2064384 | bytes 24772608 | tf_op jit(solution)/shard_map/add_chunk/pallas_call | solution.py:590
  812.0 4.2 add_chunk.15.refs_0_
  (81 shorter events, 40.1 us)
Async XLA Ops:
  0.6 69.5 %collective-permute-start = (f32[16,128]{1,0:T(8,128)}, f32[16,128]{1,0:T(8,128)S(1)}, u32[]{:S(2)}, u32[]{:S(2)}) collective-permute-start(f32[16,128]{1,0:T(8,128)} %bitcast.10), channel_id=1, source_target_pairs={{0,4},{4,0},{1,5},{5,1},{2,6},{6,2},{3,7},{7,3}} | collective-permute-start | bytes 24584 | tf_op jit(solution)/shard_map/ppermute | solution.py:619
  4.0 4.5 copy-start.21
  4.0 4.5 copy-start.18
  8.4 571.0 %collective-permute-start.7 = (f32[2048,256]{1,0:T(8,128)}, f32[2048,256]{1,0:T(8,128)}, u32[]{:S(2)}, u32[]{:S(2)}) collective-permute-start(f32[2048,256]{1,0:T(8,128)} %get-tuple-element.70.tea_ref), channel_id=1, source_target_pairs={{0,4},{4,0},{1,5},{5,1},{2,6},{6,2},{3,7},{7,3}} | collective-permute-start | bytes 6291464 | tf_op jit(solution)/shard_map/ppermute | solution.py:620
  8.5 61.6 %copy-start.15 = (f32[1,576]{1,0:T(1,128)}, f32[1,576]{1,0:T(1,128)S(1)}, u32[]{:S(2)}) copy-start(f32[1,576]{1,0:T(1,128)S(1)} %reshape.14.gain_ref) | copy-start | bytes 6916
  76.9 304.3 %collective-permute-start.6 = (f32[32,128]{1,0:T(8,128)}, f32[32,128]{1,0:T(8,128)}, u32[]{:S(2)}, u32[]{:S(2)}) collective-permute-start(f32[32,128]{1,0:T(8,128)} %get-tuple-element.69.row_ref), channel_id=1, source_target_pairs={{0,4},{4,0},{1,5},{5,1},{2,6},{6,2},{3,7},{7,3}} | collective-permute-start | bytes 49160 | tf_op jit(solution)/shard_map/ppermute | solution.py:633
  76.9 447.7 %collective-permute-start.8 = (f32[576,256]{1,0:T(8,128)}, f32[576,256]{1,0:T(8,128)}, u32[]{:S(2)}, u32[]{:S(2)}) collective-permute-start(f32[576,256]{1,0:T(8,128)} %get-tuple-element.72.refs_1_), channel_id=1, source_target_pairs={{0,4},{4,0},{1,5},{5,1},{2,6},{6,2},{3,7},{7,3}} | collective-permute-start | bytes 1769480 | tf_op jit(solution)/shard_map/ppermute | solution.py:629
  90.0 434.7 %copy-start.11 = (f32[576,512]{1,0:T(8,128)}, f32[576,512]{1,0:T(8,128)S(1)}, u32[]{:S(2)}) copy-start(f32[576,512]{1,0:T(8,128)S(1)} %get-tuple-element.73.refs_1_) | copy-start | bytes 3538948
  113.6 465.8 %copy-start.1 = (f32[576,1536]{1,0:T(8,128)}, f32[576,1536]{1,0:T(8,128)S(1)}, u32[]{:S(2)}) copy-start(f32[576,1536]{1,0:T(8,128)S(1)} %get-tuple-element.74.refs_1_) | copy-start | bytes 10616836
  167.6 617.6 %collective-permute-start.11 = (f32[576,3584]{1,0:T(8,128)}, f32[576,3584]{1,0:T(8,128)}, u32[]{:S(2)}, u32[]{:S(2)}) collective-permute-start(f32[576,3584]{1,0:T(8,128)} %get-tuple-element.75.refs_1_), channel_id=1, source_target_pairs={{0,4},{4,0},{1,5},{5,1},{2,6},{6,2},{3,7},{7,3}} | collective-permute-start | bytes 24772616 | tf_op jit(solution)/shard_map/ppermute | solution.py:629
  220.6 577.9 %collective-permute-start.12 = (f32[576,3584]{1,0:T(8,128)}, f32[576,3584]{1,0:T(8,128)}, u32[]{:S(2)}, u32[]{:S(2)}) collective-permute-start(f32[576,3584]{1,0:T(8,128)} %get-tuple-element.76.refs_1_), channel_id=1, source_target_pairs={{0,4},{4,0},{1,5},{5,1},{2,6},{6,2},{3,7},{7,3}} | collective-permute-start | bytes 24772616 | tf_op jit(solution)/shard_map/ppermute | solution.py:629
  263.7 6.1 copy-start
  263.7 6.1 copy-start.16
  269.8 254.5 %copy-start.20 = (f32[576,512]{1,0:T(8,128)S(1)}, f32[576,512]{1,0:T(8,128)}, u32[]{:S(2)}) copy-start(f32[576,512]{1,0:T(8,128)} %copy-done.19) | copy-start | bytes 3538948
  381.1 143.2 %collective-permute-start.1 = (f32[8,640]{1,0:T(8,128)S(1)}, f32[8,640]{1,0:T(8,128)S(1)}, u32[]{:S(2)}, u32[]{:S(2)}) collective-permute-start(f32[8,640]{1,0:T(8,128)S(1)} %get-tuple-element.67), channel_id=1, source_target_pairs={{0,4},{4,0},{1,5},{5,1},{2,6},{6,2},{3,7},{7,3}} | collective-permute-start | bytes 61448 | tf_op jit(solution)/shard_map/ppermute | solution.py:638
  524.3 28.8 %collective-permute-start.2 = (f32[576,512]{1,0:T(8,128)S(1)}, f32[576,512]{1,0:T(8,128)S(1)}, u32[]{:S(2)}, u32[]{:S(2)}) collective-permute-start(f32[576,512]{1,0:T(8,128)S(1)} %copy-done.20), channel_id=1, source_target_pairs={{0,4},{4,0},{1,5},{5,1},{2,6},{6,2},{3,7},{7,3}} | collective-permute-start | bytes 3538952 | tf_op jit(solution)/shard_map/ppermute | solution.py:618
  524.6 53.8 %collective-permute-start.9 = (f32[576,512]{1,0:T(8,128)S(1)}, f32[576,512]{1,0:T(8,128)S(1)}, u32[]{:S(2)}, u32[]{:S(2)}) collective-permute-start(f32[576,512]{1,0:T(8,128)S(1)} %get-tuple-element.73.refs_1_), channel_id=1, source_target_pairs={{0,4},{4,0},{1,5},{5,1},{2,6},{6,2},{3,7},{7,3}} | collective-permute-start | bytes 3538952 | tf_op jit(solution)/shard_map/ppermute | solution.py:629
  553.2 258.9 %collective-permute-start.13 = (f32[576,2048]{1,0:T(8,128)S(1)}, f32[576,2048]{1,0:T(8,128)S(1)}, u32[]{:S(2)}, u32[]{:S(2)}) collective-permute-start(f32[576,2048]{1,0:T(8,128)S(1)} %get-tuple-element.77.refs_1_), channel_id=1, source_target_pairs={{0,4},{4,0},{1,5},{5,1},{2,6},{6,2},{3,7},{7,3}} | collective-permute-start | bytes 14155784 | tf_op jit(solution)/shard_map/ppermute | solution.py:629
  579.4 15.6 %collective-permute-start.3 = (f32[576,512]{1,0:T(8,128)S(1)}, f32[576,512]{1,0:T(8,128)S(1)}, u32[]{:S(2)}, u32[]{:S(2)}) collective-permute-start(f32[576,512]{1,0:T(8,128)S(1)} %collective-permute-done.2.refs_0_), channel_id=1, source_target_pairs={{0,1},{1,2},{2,3},{3,0},{4,5},{5,6},{6,7},{7,4}} | collective-permute-start | bytes 3538952 | tf_op jit(solution)/shard_map/ppermute | solution.py:636
  579.4 175.9 %collective-permute-start.10 = (f32[576,1536]{1,0:T(8,128)S(1)}, f32[576,1536]{1,0:T(8,128)S(1)}, u32[]{:S(2)}, u32[]{:S(2)}) collective-permute-start(f32[576,1536]{1,0:T(8,128)S(1)} %get-tuple-element.74.refs_1_), channel_id=1, source_target_pairs={{0,4},{4,0},{1,5},{5,1},{2,6},{6,2},{3,7},{7,3}} | collective-permute-start | bytes 10616840 | tf_op jit(solution)/shard_map/ppermute | solution.py:629
  596.1 26.7 %collective-permute-start.4 = (f32[576,512]{1,0:T(8,128)S(1)}, f32[576,512]{1,0:T(8,128)S(1)}, u32[]{:S(2)}, u32[]{:S(2)}) collective-permute-start(f32[576,512]{1,0:T(8,128)S(1)} %collective-permute-done.2.refs_0_), channel_id=1, source_target_pairs={{0,2},{1,3},{2,0},{3,1},{4,6},{5,7},{6,4},{7,5}} | collective-permute-start | bytes 3538952 | tf_op jit(solution)/shard_map/ppermute | solution.py:636
  623.8 13.7 %collective-permute-start.5 = (f32[576,512]{1,0:T(8,128)S(1)}, f32[576,512]{1,0:T(8,128)S(1)}, u32[]{:S(2)}, u32[]{:S(2)}) collective-permute-start(f32[576,512]{1,0:T(8,128)S(1)} %collective-permute-done.2.refs_0_), channel_id=1, source_target_pairs={{0,3},{1,0},{2,1},{3,2},{4,7},{5,4},{6,5},{7,6}} | collective-permute-start | bytes 3538952 | tf_op jit(solution)/shard_map/ppermute | solution.py:636
  638.6 177.6 %collective-permute-start.14 = (f32[576,256]{1,0:T(8,128)S(1)}, f32[576,256]{1,0:T(8,128)}, u32[]{:S(2)}, u32[]{:S(2)}) collective-permute-start(f32[576,256]{1,0:T(8,128)S(1)} %get-tuple-element.78.refs_1_), channel_id=1, source_target_pairs={{0,4},{4,0},{1,5},{5,1},{2,6},{6,2},{3,7},{7,3}} | collective-permute-start | bytes 1769480 | tf_op jit(solution)/shard_map/ppermute | solution.py:629
  757.2 61.0 %collective-permute-start.15 = (f32[576,256]{1,0:T(8,128)}, f32[576,256]{1,0:T(8,128)}, u32[]{:S(2)}, u32[]{:S(2)}) collective-permute-start(f32[576,256]{1,0:T(8,128)} %get-tuple-element.79.refs_1_), channel_id=1, source_target_pairs={{0,4},{4,0},{1,5},{5,1},{2,6},{6,2},{3,7},{7,3}} | collective-permute-start | bytes 1769480 | tf_op jit(solution)/shard_map/ppermute | solution.py:629
  (14 other events, 22.8 us)
